TPU v7x, 512 devices: a 4x2x32 block of a 4x8x32 slice. The times are simulated.
512 devices in a mesh: groups: 2 (over y), block: 32 (over z), seg: 4 (over x), sub: 2 (over core).
Axes of the slice: x: 4, y: 2, z: 32, core: 2. Of those that a mesh axis runs over, the one named last changes fastest.
The devices are a block of a 4x8x32 slice.
Arguments:
- old_fields: float32 [32768, 4, 512], P(('groups', 'block', 'seg', 'sub')), parts along dimension 0, may hold values from -6 to 6
- corner_shift: float32 [24, 32768], P(None, ('groups', 'block', 'seg', 'sub')), parts along dimension 1, may hold values from -0.2 to 0.2
- targets: float32 [3, 2097152], P(None, ('groups', 'block', 'seg', 'sub')), parts along dimension 1, may hold values from -0.7 to 0.7
- owners: int32 [16384], P(('groups', 'block', 'seg', 'sub')), parts along dimension 0, may hold values from 0 to 16383, as said below
Outputs:
- new_fields: float32 [4, 2097152], P(None, ('groups', 'block', 'seg', 'sub')), parts along dimension 1
There are 2 independent parts, one for each index of `groups`. A program takes and returns all parts, laid end to end along the dimension named above; each array names one. Nothing has to cross between parts.
Inputs may be any that keep to these rules, and one draw needn't show every extreme that they name: `owners`: owner e lies on device e // 64. At most 2 of the blocks on the rows of one device are owned by elements of any one device, and in every draw some device owns exactly 2 blocks of every device.
All inputs are finite; a program needn't handle non-finite values.
Results may differ from a plain program's by a relative error of at most 0.00029.
Values sent between devices are 32-bit elements; how exact they have to be, the bound alone decides.
No kernel may reach another device: no remote copies, remote signals or barrier semaphores. Data moves between devices by JAX's collectives and lax.ppermute only.
A program may use at most 64 MiB of HBM per device.

v0:
```python
import jax
import jax.numpy as jnp
import numpy as np
from jax import lax
from jax.sharding import PartitionSpec as P

NEWTON = 3
CAP = 2


GLL_POINTS = (
    -1.0,
    -0.8717401485096066,
    -0.5917001814331423,
    -0.2092992179024789,
    0.2092992179024789,
    0.5917001814331423,
    0.8717401485096066,
    1.0,
)
EXACT = lax.Precision.HIGHEST


def in_blocks(array, dim, count):
    before, after = (array.shape[:dim], array.shape[dim + 1 :])
    return jnp.moveaxis(array.reshape(*before, count, -1, *after), dim, 0)


def joined_along(blocks, dim):
    blocks = jnp.moveaxis(blocks, 0, dim)
    lengths = blocks.shape
    return blocks.reshape(*lengths[:dim], lengths[dim] * lengths[dim + 1], *lengths[dim + 2 :])


def joined_exchange(array, axis, axes, splits, concats):
    sizes = [lax.axis_size(a) for a in axes]
    blocks = in_blocks(array, splits[0], sizes[0])
    blocks = jnp.moveaxis(in_blocks(blocks, splits[1] + 1, sizes[1]), 0, 1)
    inside = blocks.shape[2:]
    blocks = blocks.reshape(-1, *inside)
    blocks = lax.all_to_all(blocks, axis, split_axis=0, concat_axis=0, tiled=True)
    blocks = joined_along(blocks.reshape(*sizes, *inside), concats[0] + 1)
    return joined_along(blocks, concats[1])


def lagrange_rows(coords):
    gll_nodes = jnp.array(GLL_POINTS, jnp.float32)
    offsets = coords[None, :] - gll_nodes[:, None]
    spacing = gll_nodes[:, None] - gll_nodes[None, :] + jnp.eye(8, dtype=jnp.float32)
    diag_mask = jnp.eye(8, dtype=bool)
    factors = jnp.where(diag_mask[:, :, None], 1.0, offsets[None, :, :] / spacing[:, :, None])
    return jnp.prod(factors, axis=1)


def corner_signs():
    bit_table = np.array(
        [[corner >> 2 - coord_dim & 1 for corner in range(8)] for coord_dim in range(3)], np.float32
    )
    return jnp.asarray(2.0 * bit_table - 1.0)


def outer_prod(first, second, third):
    return (first[:, None, None, :] * second[None, :, None, :] * third[None, None, :, :]).reshape(
        8, -1
    )


def trilinear(ref_pos):
    shape_list = []
    slope_list = []
    for coord_dim in range(3):
        coordinate = ref_pos[coord_dim]
        shape_list.append(jnp.stack([0.5 - 0.5 * coordinate, 0.5 + 0.5 * coordinate]))
        slope_list.append(
            jnp.stack([jnp.full_like(coordinate, -0.5), jnp.full_like(coordinate, 0.5)])
        )
    values = outer_prod(shape_list[0], shape_list[1], shape_list[2])
    slopes = [
        outer_prod(slope_list[0], shape_list[1], shape_list[2]),
        outer_prod(shape_list[0], slope_list[1], shape_list[2]),
        outer_prod(shape_list[0], shape_list[1], slope_list[2]),
    ]
    return (values, slopes)


def solve_three(matrix, rhs_rows):
    cofactors = []
    for row_id in range(3):
        keep_rows = [remain for remain in range(3) if remain != row_id]
        cof_row = []
        for col_id in range(3):
            keep_cols = [remain for remain in range(3) if remain != col_id]
            sign_factor = 1.0 if (row_id + col_id) % 2 == 0 else -1.0
            cof_row.append(
                sign_factor
                * (
                    matrix[keep_rows[0]][keep_cols[0]] * matrix[keep_rows[1]][keep_cols[1]]
                    - matrix[keep_rows[0]][keep_cols[1]] * matrix[keep_rows[1]][keep_cols[0]]
                )
            )
        cofactors.append(cof_row)
    determinant = (
        matrix[0][0] * cofactors[0][0]
        + matrix[0][1] * cofactors[0][1]
        + matrix[0][2] * cofactors[0][2]
    )
    return [
        (
            cofactors[0][col_id] * rhs_rows[0]
            + cofactors[1][col_id] * rhs_rows[1]
            + cofactors[2][col_id] * rhs_rows[2]
        )
        / determinant
        for col_id in range(3)
    ]


def invert_map(corners, target):
    ref_pos = jnp.zeros_like(target)
    for iteration in range(NEWTON):
        values, slopes = trilinear(ref_pos)
        mapped = jnp.dot(corners, values, precision=EXACT)
        columns = [jnp.dot(corners, slope_row, precision=EXACT) for slope_row in slopes]
        matrix = [[columns[col_id][row_id] for col_id in range(3)] for row_id in range(3)]
        misfit = mapped - target
        update = solve_three(matrix, [misfit[row_id] for row_id in range(3)])
        ref_pos = jnp.clip(ref_pos - jnp.stack(update), -1.2, 1.2)
    return ref_pos


def interpolate(element_field, corners, target):
    ref_pos = invert_map(corners, target)
    along_x = lagrange_rows(ref_pos[0])
    along_y = lagrange_rows(ref_pos[1])
    along_z = lagrange_rows(ref_pos[2])
    weights = (along_y[:, None, :] * along_z[None, :, :]).reshape(64, -1)
    var_count = element_field.shape[0]
    partial_sum = jnp.dot(element_field.reshape(var_count * 8, 64), weights, precision=EXACT)
    return jnp.sum(partial_sum.reshape(var_count, 8, -1) * along_x[None, :, :], axis=1)


def interpolate_blocks(fields, shifts, points):
    cube_signs = corner_signs()

    def per_block(inputs):
        element_field, shift_row, target = inputs
        return interpolate(element_field, cube_signs + shift_row.reshape(3, 8), target)

    return lax.map(per_block, (fields, shifts, points), batch_size=64)


def slot_table(owners, elems_local, capacity):
    owner_dev = owners // elems_local
    local_elem = owners - owner_dev * elems_local
    block_count = owners.shape[0]
    earlier = jnp.tril(jnp.ones((block_count, block_count), jnp.int32), -1)
    matches = (owner_dev[:, None] == owner_dev[None, :]).astype(jnp.int32)
    arrival = jnp.sum(matches * earlier, axis=1)
    return (owner_dev * capacity + arrival, local_elem)


def shards(old_fields, corner_shift, targets, owners):
    outer_count = lax.axis_size("block")
    inner_count = lax.axis_size("seg") * lax.axis_size("sub")
    slot_count = outer_count * inner_count * CAP
    elems_local = old_fields.shape[0]
    var_count = old_fields.shape[1]
    block_count = owners.shape[0]
    slot_index, local_elem = slot_table(owners, elems_local, CAP)
    block_points = targets.reshape(3, block_count, -1).transpose(1, 0, 2)
    point_count = block_points.shape[2]
    outgoing = jnp.zeros((slot_count, 3, point_count), jnp.float32).at[slot_index].set(block_points)
    wanted = jnp.full((slot_count,), -1, jnp.int32).at[slot_index].set(local_elem)
    arrived, asked = (
        lax.all_to_all(
            lax.all_to_all(
                outgoing.reshape(outer_count, inner_count, CAP, 3, point_count),
                "block",
                split_axis=0,
                concat_axis=0,
                tiled=True,
            ),
            ("seg", "sub"),
            split_axis=1,
            concat_axis=1,
            tiled=True,
        ),
        lax.all_to_all(
            lax.all_to_all(
                wanted.reshape(outer_count, inner_count, CAP),
                "block",
                split_axis=0,
                concat_axis=0,
                tiled=True,
            ),
            ("seg", "sub"),
            split_axis=1,
            concat_axis=1,
            tiled=True,
        ),
    )
    asked = asked.reshape(slot_count)
    live_slot = asked >= 0
    element = jnp.where(live_slot, asked, 0)
    fields = old_fields[element]
    shifts = jnp.transpose(corner_shift[:, element])
    computed = interpolate_blocks(fields, shifts, arrived.reshape(slot_count, 3, point_count))
    computed = jnp.where(live_slot[:, None, None], computed, 0.0)
    returned = joined_exchange(
        computed.reshape(outer_count, inner_count, CAP, var_count, point_count),
        ("block", "seg", "sub"),
        ("block", ("seg", "sub")),
        (0, 1),
        (0, 1),
    )
    mine = returned.reshape(slot_count, var_count, point_count)[slot_index]
    return mine.transpose(1, 0, 2).reshape(var_count, -1)


def solution(mesh):
    in_specs = (
        P(("groups", "block", "seg", "sub"), None, None),
        P(None, ("groups", "block", "seg", "sub")),
        P(None, ("groups", "block", "seg", "sub")),
        P(("groups", "block", "seg", "sub")),
    )
    out_specs = P(None, ("groups", "block", "seg", "sub"))
    return jax.shard_map(shards, mesh=mesh, in_specs=in_specs, out_specs=out_specs, check_vma=False)
```

profile of v0, /device:TPU:40, one launch (start us, length us, event | category | flops | bytes accessed | tf_op | source)
XLA Modules:
  0.0 457.5 jit_solution(9812434180337854026)
XLA Ops:
  2.6 45.8 %all-to-all-start = ((s32[32,8,2]{1,2,0:T(2,128)}), s32[32,8,2]{1,2,0:T(2,128)S(1)}, u32[]{:S(2)}, u32[]{:S(2)}) async-start(s32[32,8,2]{1,2,0:T(2,128)} %copy.250), calls=%async_computation | async-start | bytes 65536 | tf_op jit(solution)/shard_map/all_to_all | solution.py:189
  48.5 2.5 scatter_fusion
  51.1 1.3 copy.258
  52.4 18.5 %all-to-all-done = s32[32,8,2]{1,2,0:T(2,128)S(1)} async-done(((s32[32,8,2]{1,2,0:T(2,128)}), s32[32,8,2]{1,2,0:T(2,128)S(1)}, u32[]{:S(2)}, u32[]{:S(2)}) %all-to-all-start) | async-done | bytes 2080 | tf_op jit(solution)/shard_map/all_to_all | solution.py:189
  70.9 4.8 %all-to-all-start.2 = ((f32[32,8,2,3,128]{4,2,1,3,0:T(2,128)}), f32[32,8,2,3,128]{4,2,1,3,0:T(2,128)S(1)}, u32[]{:S(2)}, u32[]{:S(2)}) async-start(f32[32,8,2,3,128]{4,2,1,3,0:T(2,128)} %copy.258), calls=%async_computation.2 | async-start | bytes 1572864 | tf_op jit(solution)/shard_map/all_to_all | solution.py:176
  76.4 85.2 %all-to-all-done.2 = f32[32,8,2,3,128]{4,2,1,3,0:T(2,128)S(1)} async-done(((f32[32,8,2,3,128]{4,2,1,3,0:T(2,128)}), f32[32,8,2,3,128]{4,2,1,3,0:T(2,128)S(1)}, u32[]{:S(2)}, u32[]{:S(2)}) %all-to-all-start.2) | async-done | bytes 786464 | tf_op jit(solution)/shard_map/all_to_all | solution.py:176
  161.6 4.6 %all-to-all-start.1 = ((s32[32,8,2]{0,2,1:T(2,128)}), s32[32,8,2]{0,2,1:T(2,128)S(1)}, u32[]{:S(2)}, u32[]{:S(2)}) async-start(s32[32,8,2]{0,2,1:T(2,128)} %copy.251), calls=%async_computation.1 | async-start | bytes 16384 | tf_op jit(solution)/shard_map/all_to_all | solution.py:188
  166.2 1.3 copy.259
  167.5 4.0 all-to-all-done.1
  171.5 3.8 all-to-all-start.3
  175.7 4.6 %gather_fusion = f32[512,4,512]{2,1,0:T(4,128)} fusion(f32[64,4,512]{2,1,0:T(4,128)S(1)} %copy-done, s32[1024]{0:T(1024)S(1)} %pad_clamp_fusion.1), kind=kCustom, calls=%fused_computation | custom fusion | bytes 8390656 | tf_op jit(solution)/shard_map/gather | solution.py:205
  181.7 6.5 %all-to-all-done.3 = f32[32,8,2,3,128]{4,2,0,3,1:T(2,128)S(1)} async-done(((f32[32,8,2,3,128]{4,2,0,3,1:T(2,128)}), f32[32,8,2,3,128]{4,2,0,3,1:T(2,128)S(1)}, u32[]{:S(2)}, u32[]{:S(2)}) %all-to-all-start.3) | async-done | bytes 786464 | tf_op jit(solution)/shard_map/all_to_all | solution.py:175
  188.2 1.2 copy.260
  189.4 144.6 %while.12 = (s32[]{:T(128)}, f32[8,64,4,128]{3,2,1,0:T(4,128)}, f32[8,64,4,512]{3,2,1,0:T(4,128)}, f32[8,64,24]{1,2,0:T(8,128)S(1)}, f32[8,64,3,128]{3,1,0,2:T(8...) while((s32[]{:T(128)}, f32[8,64,4,128]{3,2,1,0:T(4,128)}, ...), condition=%wide.region_8.9_spmd.clone.clone, body=%wide.region_3.8_spmd.sunk.clone.clone.sunk | while | flops 238395200 | bytes 22388688 | solution.py:149
  190.9 1.3 convolution_subtract_fusion.2
  201.3 2.1 fusion.229
  203.3 1.1 constant_dynamic-slice_fusion.2
  204.8 2.2 fusion.230
  208.9 1.3 convolution_subtract_fusion.2
  219.3 2.1 fusion.229
  221.4 1.1 constant_dynamic-slice_fusion.2
  222.9 2.2 fusion.230
  227.0 1.3 convolution_subtract_fusion.2
  237.4 2.1 fusion.229
  239.5 1.1 constant_dynamic-slice_fusion.2
  240.9 2.2 fusion.230
  245.0 1.3 convolution_subtract_fusion.2
  255.4 2.1 fusion.229
  257.5 1.1 constant_dynamic-slice_fusion.2
  259.0 2.2 fusion.230
  263.1 1.3 convolution_subtract_fusion.2
  273.5 2.1 fusion.229
  275.6 1.1 constant_dynamic-slice_fusion.2
  277.0 2.2 fusion.230
  281.2 1.3 convolution_subtract_fusion.2
  291.5 2.1 fusion.229
  295.1 2.2 fusion.230
  299.2 1.3 convolution_subtract_fusion.2
  309.6 2.1 fusion.229
  311.7 1.1 constant_dynamic-slice_fusion.2
  313.2 2.2 fusion.230
  317.3 1.3 convolution_subtract_fusion.2
  327.6 2.1 fusion.229
  331.2 2.2 fusion.230
  334.0 3.7 broadcast_select_fusion
  337.7 16.7 %all-to-all-start.4 = ((f32[256,1,1,2,4,128]{5,4,3,2,1,0:T(4,128)}), f32[256,1,1,2,4,128]{5,4,3,2,1,0:T(4,128)S(1)}, u32[]{:S(2)}, u32[]{:S(2)}) async-start(f32[256,1,1,2,4,128]{5,4,3,2,1,0:T(4,128)} %broadcast_select_fusion), calls=%async_computation.4 | async-start | bytes 2097152 | tf_op jit(solution)/shard_map/all_to_all | solution.py:41
  354.4 101.8 %all-to-all-done.4 = f32[256,1,1,2,4,128]{5,4,3,2,1,0:T(4,128)S(1)} async-done(((f32[256,1,1,2,4,128]{5,4,3,2,1,0:T(4,128)}), f32[256,1,1,2,4,128]{5,4,3,2,1,0:T(4,128)S(1)}, u32[]{:S(2)}, u32[]{:S(2)}) %all-to-all-start.4) | async-done | bytes 1048608 | tf_op jit(solution)/shard_map/all_to_all | solution.py:41
  456.3 1.2 gather_fusion.2
  (525 shorter events, 95.3 us)
Async XLA Ops:
  0.0 175.7 %copy-start = (f32[64,4,512]{2,1,0:T(4,128)S(1)}, f32[64,4,512]{2,1,0:T(4,128)}, u32[]{:S(2)}) copy-start(f32[64,4,512]{2,1,0:T(4,128)} %param.10) | copy-start | bytes 1572868
  2.6 68.3 %all-to-all-start = ((s32[32,8,2]{1,2,0:T(2,128)}), s32[32,8,2]{1,2,0:T(2,128)S(1)}, u32[]{:S(2)}, u32[]{:S(2)}) async-start(s32[32,8,2]{1,2,0:T(2,128)} %copy.250), calls=%async_computation | async-start | bytes 65536 | tf_op jit(solution)/shard_map/all_to_all | solution.py:189
  52.4 122.9 %copy-start.7 = (f32[24,64]{1,0:T(8,128)S(1)}, f32[24,64]{1,0:T(8,128)}, u32[]{:S(2)}) copy-start(f32[24,64]{1,0:T(8,128)} %param.11) | copy-start | bytes 18436
  70.9 90.7 %all-to-all-start.2 = ((f32[32,8,2,3,128]{4,2,1,3,0:T(2,128)}), f32[32,8,2,3,128]{4,2,1,3,0:T(2,128)S(1)}, u32[]{:S(2)}, u32[]{:S(2)}) async-start(f32[32,8,2,3,128]{4,2,1,3,0:T(2,128)} %copy.258), calls=%async_computation.2 | async-start | bytes 1572864 | tf_op jit(solution)/shard_map/all_to_all | solution.py:176
  161.6 9.9 %all-to-all-start.1 = ((s32[32,8,2]{0,2,1:T(2,128)}), s32[32,8,2]{0,2,1:T(2,128)S(1)}, u32[]{:S(2)}, u32[]{:S(2)}) async-start(s32[32,8,2]{0,2,1:T(2,128)} %copy.251), calls=%async_computation.1 | async-start | bytes 16384 | tf_op jit(solution)/shard_map/all_to_all | solution.py:188
  171.5 16.7 %all-to-all-start.3 = ((f32[32,8,2,3,128]{4,2,0,3,1:T(2,128)}), f32[32,8,2,3,128]{4,2,0,3,1:T(2,128)S(1)}, u32[]{:S(2)}, u32[]{:S(2)}) async-start(f32[32,8,2,3,128]{4,2,0,3,1:T(2,128)} %copy.259), calls=%async_computation.3 | async-start | bytes 1572864 | tf_op jit(solution)/shard_map/all_to_all | solution.py:175
  180.3 9.0 %copy-start.1 = (f32[2,128]{1,0:T(2,128)S(1)}, f32[2,128]{1,0:T(2,128)}, u32[]{:S(2)}) copy-start(f32[2,128]{1,0:T(2,128)} %constant.47.clone.4) | copy-start | bytes 3076
  180.3 9.0 %copy-start.2 = (f32[2,128]{1,0:T(2,128)S(1)}, f32[2,128]{1,0:T(2,128)}, u32[]{:S(2)}) copy-start(f32[2,128]{1,0:T(2,128)} %constant.39.clone.4) | copy-start | bytes 3076
  180.3 9.0 %copy-start.3 = (f32[3,8]{1,0:T(4,128)S(1)}, f32[3,8]{1,0:T(4,128)}, u32[]{:S(2)}) copy-start(f32[3,8]{1,0:T(4,128)} %constant.93.clone..sunk.3) | copy-start | bytes 292
  180.3 9.0 %copy-start.4 = (f32[24]{0:T(128)S(1)}, f32[24]{0:T(128)}, u32[]{:S(2)}) copy-start(f32[24]{0:T(128)} %constant.359) | copy-start | bytes 292
  180.4 9.0 %copy-start.5 = (f32[8]{0:T(128)S(1)}, f32[8]{0:T(128)}, u32[]{:S(2)}) copy-start(f32[8]{0:T(128)} %constant.358) | copy-start | bytes 100
  180.4 9.0 %copy-start.6 = (f32[8]{0:T(128)S(1)}, f32[8]{0:T(128)}, u32[]{:S(2)}) copy-start(f32[8]{0:T(128)} %constant.94.clone..sunk.7) | copy-start | bytes 100
  337.7 118.6 %all-to-all-start.4 = ((f32[256,1,1,2,4,128]{5,4,3,2,1,0:T(4,128)}), f32[256,1,1,2,4,128]{5,4,3,2,1,0:T(4,128)S(1)}, u32[]{:S(2)}, u32[]{:S(2)}) async-start(f32[256,1,1,2,4,128]{5,4,3,2,1,0:T(4,128)} %broadcast_select_fusion), calls=%async_computation.4 | async-start | bytes 2097152 | tf_op jit(solution)/shard_map/all_to_all | solution.py:41
where the time goes:
time: 459 us; the launch traced here: 457 us
  waiting for transfers between devices  216 us (47%)
  starting transfers between devices  75.6 us (16%)
  matrix products  73.2 us (16%)
  local copies, waits for them, and re-layouts  45.8 us (10%)
  other arithmetic  43 us (9%)
    all_to_all x1, waiting for transfers between devices, joined_exchange(): lax.all_to_all(blocks, axis, split_axis=0, concat_axis=0, tiled=True)  102 us
    all_to_all x1, waiting for transfers between devices, shards(): lax.all_to_all(outgoing.reshape(outer_count, inner_count, CAP, 3, point_c...  85.2 us
    all_to_all x1, starting transfers between devices, shards(): lax.all_to_all(wanted.reshape(outer_count, inner_count, CAP), 'block', sp...  45.8 us
    dot_general x72, matrix products, invert_map(): jnp.dot(corners, slope_row, precision=EXACT)  36.5 us
    dot_general x24, matrix products, invert_map(): mapped = jnp.dot(corners, values, precision=EXACT)  19.4 us
    all_to_all x1, waiting for transfers between devices, shards(): lax.all_to_all(wanted.reshape(outer_count, inner_count, CAP), 'block', sp...  18.5 us
    dot_general x8, matrix products, interpolate(): jnp.dot(element_field.reshape(var_count * 8, 64), weights, precision=EXACT)  17.2 us
    all_to_all x1, starting transfers between devices, joined_exchange(): lax.all_to_all(blocks, axis, split_axis=0, concat_axis=0, tiled=True)  16.7 us
  transfers between devices with their start and end apart: 5, of which 5 were waited for; matrix products, arithmetic and copies ran while one was open for 3% of the time, Pallas kernels for 0%

commit v1 on v0

v1 whole, which is shorter than its diff:
```python
import functools

import jax
import jax.numpy as jnp
import numpy as np
from jax import lax
from jax.experimental import pallas as pl
from jax.experimental.pallas import tpu as pltpu
from jax.sharding import PartitionSpec as P

NEWTON = 3
CAP = 2
FIRST = 7
LANES = 128
ID_LANES = 16
FULLEST, COUNT = ID_LANES - 2, ID_LANES - 1

GLL_POINTS = (
    -1.0,
    -0.8717401485096066,
    -0.5917001814331423,
    -0.2092992179024789,
    0.2092992179024789,
    0.5917001814331423,
    0.8717401485096066,
    1.0,
)
EXACT = lax.Precision.HIGHEST


def monomial_table():
    signs = np.array([[2.0 * (c >> 2 - a & 1) - 1.0 for c in range(8)] for a in range(3)])
    table = np.zeros((24, 24), np.float32)
    offset = np.zeros((24,), np.float32)
    for m in range(8):
        row = np.ones(8)
        for a in range(3):
            if m >> 2 - a & 1:
                row = row * signs[a]
        for a in range(3):
            table[8 * a + m, 8 * a : 8 * a + 8] = row / 8.0
            offset[8 * a + m] = float(np.sum(row * signs[a]) / 8.0)
    return table, offset


def lagrange_constants():
    nodes = np.array(GLL_POINTS, np.float64)
    plain = [0, 1, 2, 3, 4, 5, 6, 7]
    orders = [plain] + [[i] * 4 + [i + 2] * 4 for i in (0, 4, 1, 5)]
    blocks = []
    for order in orders:
        for k in range(7):
            blocks.append([nodes[[m for m in range(8) if m != i][k]] for i in order])
        factor = []
        for i in order:
            others = [nodes[i] - nodes[m] for m in range(8) if m != i]
            factor.append(1.0 / np.prod(others))
        blocks.append(factor)
    table = np.array(blocks, np.float32).reshape(len(orders), 8, 8)
    return np.repeat(table[..., None], LANES, axis=-1)


def pack_kernel(first, slots, row_elems, owners_ref, targets_ref, send_ref, seen, meta):
    rows, last = send_ref.shape[0], 3 * slots
    blocks = targets_ref.shape[0]
    send_ref[...] = jnp.zeros_like(send_ref)
    meta[...] = jnp.zeros_like(meta)
    lane = lax.broadcasted_iota(jnp.int32, (1, LANES), 1)

    def clear(r, carry):
        seen[r] = 0
        return carry

    lax.fori_loop(0, rows, clear, 0)

    def place(b, fullest):
        owner = owners_ref[b]
        r = owner // row_elems
        k = seen[r]
        seen[r] = k + 1

        @pl.when(jnp.logical_and(k >= first, k < first + slots))
        def _():
            slot = k - first
            points = targets_ref[b]
            for a in range(3):
                send_ref[r, pl.ds(slot * 3 + a, 1), :] = points[a : a + 1]
            meta[pl.ds(r, 1), :] += jnp.where(lane == slot, owner - r * row_elems, 0)

        return jnp.maximum(fullest, k + 1)

    fullest = lax.fori_loop(0, blocks, place, jnp.int32(0))

    def count(r, carry):
        used = jnp.clip(seen[r] - first, 0, slots)
        ids = meta[pl.ds(r, 1), :]
        ids = jnp.where(lane == COUNT, used, jnp.where(lane == FULLEST, fullest, ids))
        send_ref[r, pl.ds(last, 1), :] = ids.astype(jnp.float32)
        return carry

    lax.fori_loop(0, rows, count, 0)


def pack(owners, block_points, rows, first, slots, row_elems):
    height = -(-(3 * slots + 1) // 8) * 8
    return pl.pallas_call(
        functools.partial(pack_kernel, first, slots, row_elems),
        out_shape=jax.ShapeDtypeStruct((rows, height, LANES), jnp.float32),
        in_specs=[
            pl.BlockSpec(memory_space=pltpu.SMEM),
            pl.BlockSpec(memory_space=pltpu.VMEM),
        ],
        out_specs=pl.BlockSpec(memory_space=pltpu.VMEM),
        scratch_shapes=[pltpu.SMEM((rows,), jnp.int32), pltpu.VMEM((rows, LANES), jnp.int32)],
        name="pack",
    )(owners, block_points)


def newton(coef, target):
    def mapped(a, m):
        return coef[8 * a + m]

    def solve(jac, misfit):
        cof = [[None] * 3 for _ in range(3)]
        for r in range(3):
            r0, r1 = (r + 1) % 3, (r + 2) % 3
            for c in range(3):
                c0, c1 = (c + 1) % 3, (c + 2) % 3
                cof[r][c] = jac[r0][c0] * jac[r1][c1] - jac[r0][c1] * jac[r1][c0]
        det = jac[0][0] * cof[0][0] + jac[0][1] * cof[0][1] + jac[0][2] * cof[0][2]
        inverse = 1.0 / det
        return [
            (cof[0][c] * misfit[0] + cof[1][c] * misfit[1] + cof[2][c] * misfit[2]) * inverse
            for c in range(3)
        ]

    jac = [[mapped(a, 4), mapped(a, 2), mapped(a, 1)] for a in range(3)]
    step = solve(jac, [mapped(a, 0) - target[a] for a in range(3)])
    pos = [jnp.clip(-s, -1.2, 1.2) for s in step]
    for _ in range(NEWTON - 1):
        u, v, w = pos
        uv, uw, vw = u * v, u * w, v * w
        jac, misfit = [], []
        for a in range(3):
            du = mapped(a, 4) + mapped(a, 6) * v + mapped(a, 5) * w + mapped(a, 7) * vw
            dv = mapped(a, 2) + mapped(a, 6) * u + mapped(a, 3) * w + mapped(a, 7) * uw
            dw = mapped(a, 1) + mapped(a, 5) * u + mapped(a, 3) * v + mapped(a, 7) * uv
            at = mapped(a, 0) + mapped(a, 2) * v + mapped(a, 1) * w + mapped(a, 3) * vw + u * du
            jac.append([du, dv, dw])
            misfit.append(at - target[a])
        step = solve(jac, misfit)
        pos = [jnp.clip(p - s, -1.2, 1.2) for p, s in zip(pos, step)]
    return pos


def lagrange(point, table):
    value = (point - table[0]) * table[7]
    for k in range(1, 7):
        value = value * (point - table[k])
    return value


def halves(value):
    high = value.astype(jnp.bfloat16)
    return high, (value - high.astype(jnp.float32)).astype(jnp.bfloat16)


def evaluate_kernel(elems, meta_ref, recv_ref, const_ref, *refs):
    pieces, (out_ref, table, points, coefs, live, sems) = refs[:8], refs[8:]
    senders = recv_ref.shape[0]
    height = pieces[0].shape[0]
    copies = [
        pltpu.make_async_copy(piece, table.at[pl.ds(k * height, height)], sems.at[k])
        for k, piece in enumerate(pieces)
    ]
    for copy in copies:
        copy.start()

    def of_sender(s, total):
        used = meta_ref[s * ID_LANES + COUNT]

        def of_slot(k, carry):
            live[total + k] = s * ID_LANES + k
            return carry

        lax.fori_loop(0, used, of_slot, 0)
        return total + used

    total = lax.fori_loop(0, senders, of_sender, jnp.int32(0))
    for copy in copies:
        copy.wait()

    lane = lax.broadcasted_iota(jnp.int32, (16, LANES), 1)

    def group(g, carry):
        where = []
        for u in range(8):
            at = live[jnp.minimum(g * 8 + u, total - 1)]
            s, k, code = at // ID_LANES, at % ID_LANES, meta_ref[at]
            base = (code // elems) * height
            elem = code % elems
            where.append((s, k, base + elem * 16))
            for a in range(3):
                points[a, pl.ds(u, 1), :] = recv_ref[s, pl.ds(k * 3 + a, 1), :]
            coefs[pl.ds(u, 1), :] = table[pl.ds(base + elems * 16 + elem, 1), :]
        all_coefs = coefs[...]
        coef = [jnp.broadcast_to(all_coefs[:, m : m + 1], (8, LANES)) for m in range(24)]
        pos = newton(coef, [points[a] for a in range(3)])
        for u in range(8):
            s, k, start = where[u]
            rows = [jnp.broadcast_to(p[u : u + 1], (8, LANES)) for p in pos]
            along_y = lagrange(rows[1], const_ref[0])
            along_z = lagrange(rows[2], const_ref[0])
            weights = jnp.concatenate(
                [jnp.broadcast_to(along_y[j : j + 1], (8, LANES)) * along_z for j in range(8)], axis=0
            )
            weights = jnp.concatenate(halves(weights), axis=0)
            field = table[pl.ds(pl.multiple_of(start, 16), 16), :]
            turned = pltpu.roll(field, LANES // 2, 1)
            even = jnp.where(lane < LANES // 2, field, turned)
            odd = jnp.where(lane < LANES // 2, turned, field)
            both = jnp.concatenate(halves(jnp.concatenate([even, odd], axis=0)), axis=0)
            sums = jnp.dot(both, weights, preferred_element_type=jnp.float32)
            total_x = None
            for q in range(4):
                term = sums[8 * q : 8 * q + 8] + sums[32 + 8 * q : 40 + 8 * q]
                term = term * lagrange(rows[0], const_ref[1 + q])
                total_x = term if total_x is None else total_x + term
            out_ref[s, k] = total_x[0:4] + total_x[4:8]
        return carry

    lax.fori_loop(0, (total + 7) // 8, group, 0)


def evaluate(meta, recv, pieces, slots, elems):
    senders = recv.shape[0]
    height = pieces[0].shape[0]
    constants = lagrange_constants()
    return pl.pallas_call(
        functools.partial(evaluate_kernel, elems),
        out_shape=jax.ShapeDtypeStruct((senders, slots, 4, LANES), jnp.float32),
        in_specs=[pl.BlockSpec(memory_space=pltpu.SMEM)]
        + [pl.BlockSpec(memory_space=pltpu.VMEM)] * 2
        + [pl.BlockSpec(memory_space=pl.ANY)] * 8,
        out_specs=pl.BlockSpec(memory_space=pltpu.VMEM),
        scratch_shapes=[
            pltpu.VMEM((8 * height, LANES), jnp.float32),
            pltpu.VMEM((3, 8, LANES), jnp.float32),
            pltpu.VMEM((8, LANES), jnp.float32),
            pltpu.SMEM((senders * ID_LANES,), jnp.int32),
            pltpu.SemaphoreType.DMA((8,)),
        ],
        name="evaluate",
    )(meta, recv, jnp.asarray(constants), *pieces)


def unpack_kernel(first, slots, row_elems, owners_ref, back_ref, before_ref, out_ref, seen):
    def clear(r, carry):
        seen[r] = 0
        return carry

    lax.fori_loop(0, back_ref.shape[0], clear, 0)

    def take(b, carry):
        r = owners_ref[b] // row_elems
        k = seen[r]
        seen[r] = k + 1
        fits = jnp.logical_and(k >= first, k < first + slots)

        @pl.when(fits)
        def _():
            out_ref[b] = back_ref[r, k - first]

        @pl.when(jnp.logical_not(fits))
        def _():
            out_ref[b] = before_ref[b]

        return carry

    lax.fori_loop(0, out_ref.shape[0], take, 0)


def unpack(owners, back, before, first, slots, row_elems):
    return pl.pallas_call(
        functools.partial(unpack_kernel, first, slots, row_elems),
        out_shape=jax.ShapeDtypeStruct(before.shape, jnp.float32),
        in_specs=[pl.BlockSpec(memory_space=pltpu.SMEM)]
        + [pl.BlockSpec(memory_space=pltpu.VMEM)] * 2,
        out_specs=pl.BlockSpec(memory_space=pltpu.VMEM),
        scratch_shapes=[pltpu.SMEM((back.shape[0],), jnp.int32)],
        name="unpack",
    )(owners, back, before)


def row_pieces(old_fields, corner_shift):
    elems = old_fields.shape[0]
    table, offset = monomial_table()
    coefs = jnp.dot(jnp.asarray(table), corner_shift, precision=EXACT) + offset[:, None]
    coefs = jnp.pad(coefs.T, ((0, 0), (0, LANES - coefs.shape[0])))
    fields = old_fields.reshape(elems, 4, 4, LANES).transpose(0, 2, 1, 3).reshape(-1, LANES)
    own = jnp.concatenate([fields, coefs], axis=0)
    segs = lax.axis_size("seg")

    def along(step):
        return lax.ppermute(own, "seg", [(i, (i + step) % segs) for i in range(segs)])

    half = [own, along(1), along(segs - 1), along(2)]
    return half + [lax.ppermute(piece, "sub", [(0, 1), (1, 0)]) for piece in half]


def all_to_all(array):
    return lax.all_to_all(array, "block", split_axis=0, concat_axis=0, tiled=True)


def shards(old_fields, corner_shift, targets, owners):
    rows = lax.axis_size("block")
    segs, subs = lax.axis_size("seg"), lax.axis_size("sub")
    elems = old_fields.shape[0]
    row_elems = elems * segs * subs
    block_count = owners.shape[0]
    most = CAP * segs * subs
    block_points = targets.reshape(3, block_count, -1).transpose(1, 0, 2)
    pieces = row_pieces(old_fields, corner_shift)

    def trip(first, slots, before):
        recv = all_to_all(pack(owners, block_points, rows, first, slots, row_elems))
        meta = recv[:, 3 * slots, :ID_LANES].astype(jnp.int32)
        device, elem = meta // elems, meta % elems
        apart = (device // subs - lax.axis_index("seg")) % segs
        piece = jnp.where(apart == 0, 0, jnp.where(apart == 1, 2, jnp.where(apart == 2, 3, 1)))
        piece = piece + jnp.where(device % subs == lax.axis_index("sub"), 0, 4)
        is_id = lax.broadcasted_iota(jnp.int32, meta.shape, 1) < FULLEST
        codes = jnp.where(is_id, piece * elems + elem, meta).reshape(-1)
        answers = all_to_all(evaluate(codes, recv, pieces, slots, elems))
        fullest = jnp.max(meta[:, FULLEST])
        return unpack(owners, answers, before, first, slots, row_elems), fullest

    done, fullest = trip(0, FIRST, block_points_like(block_points))
    done = lax.cond(
        fullest > FIRST,
        lambda held: trip(FIRST, most - FIRST, held)[0],
        lambda held: held,
        done,
    )
    return done.transpose(1, 0, 2).reshape(4, -1)


def block_points_like(block_points):
    return jnp.zeros((block_points.shape[0], 4, block_points.shape[2]), jnp.float32)


def solution(mesh):
    split = ("groups", "block", "seg", "sub")
    in_specs = (P(split, None, None), P(None, split), P(None, split), P(split))
    return jax.shard_map(
        shards, mesh=mesh, in_specs=in_specs, out_specs=P(None, split), check_vma=False
    )
```

time: 459 us -> 179 us (0.39)
  waiting for transfers between devices: 216 us -> 89.5 us
  matrix products: 73.2 us -> 0.24 us
  local copies, waits for them, and re-layouts: 45.8 us -> 1.49 us
  other arithmetic: 43 us -> 3.26 us
  Pallas kernels: 0 us -> 10.4 us
    all_to_all x5 -> x2, waiting for transfers between devices: 216 us -> 73.8 us  [all_to_all(): lax.all_to_all(array, 'block', split_axis=0, concat_axis=0, tiled=True)]
    dot_general x104 -> x1, matrix products: 73.2 us -> 0.24 us  [row_pieces(): jnp.dot(jnp.asarray(table), corner_shift, precision=EXACT) + offset[:, None]]
    all_to_all x5 -> x2, starting transfers between devices: 75.6 us -> 52.9 us  [all_to_all(): lax.all_to_all(array, 'block', split_axis=0, concat_axis=0, tiled=True)]
    ppermute x0 -> x7, starting transfers between devices: none -> 19.5 us  [the longest x3 11.3 us: along(): lax.ppermute(own, 'seg', [(i, (i + step) % segs) for i in range(segs)])]
    sub x41 -> x0, other arithmetic: 16.7 us -> none  [the longest x16 14.7 us: invert_map(): misfit = mapped - target]
    reduce_prod x8 -> x0, other arithmetic: 16.6 us -> none  [lagrange_rows(): return jnp.prod(factors, axis=1)]
    ppermute x0 -> x7, waiting for transfers between devices: none -> 15.6 us  [the longest x3 15.6 us: along(): lax.ppermute(own, 'seg', [(i, (i + step) % segs) for i in range(segs)])]
    pallas_call x0 -> x3, Pallas kernels: none -> 10.4 us  [the longest x1 4.83 us: evaluate(): pl.pallas_call(functools.partial(evaluate_kernel, elems), out_shape=jax.S...]
  transfers between devices with their start and end apart: 5 -> 9, of which waited for: 5 -> 4; matrix products, arithmetic and copies ran while one was open for 3% -> 2% of each run, Pallas kernels for 0% -> 0%
where the time goes in v1:
time: 179 us; the launch traced here: 178 us
  waiting for transfers between devices  89.5 us (50%)
  starting transfers between devices  72.5 us (41%)
  Pallas kernels  10.4 us (6%)
  other arithmetic  3.26 us (2%)
    all_to_all x2, waiting for transfers between devices, all_to_all(): lax.all_to_all(array, 'block', split_axis=0, concat_axis=0, tiled=True)  73.8 us
    all_to_all x2, starting transfers between devices, all_to_all(): lax.all_to_all(array, 'block', split_axis=0, concat_axis=0, tiled=True)  52.9 us
    ppermute x3, waiting for transfers between devices, along(): lax.ppermute(own, 'seg', [(i, (i + step) % segs) for i in range(segs)])  15.6 us
    ppermute x3, starting transfers between devices, along(): lax.ppermute(own, 'seg', [(i, (i + step) % segs) for i in range(segs)])  11.3 us
    ppermute x4, starting transfers between devices, row_pieces(): lax.ppermute(piece, 'sub', [(0, 1), (1, 0)])  8.27 us
    pallas_call x1, Pallas kernels, evaluate(): pl.pallas_call(functools.partial(evaluate_kernel, elems), out_shape=jax.S...  4.83 us
  transfers between devices with their start and end apart: 9, of which 4 were waited for; matrix products, arithmetic and copies ran while one was open for 2% of the time, Pallas kernels for 0%

profile of v1, /device:TPU:40, one launch (start us, length us, event | category | flops | bytes accessed | tf_op | source)
XLA Modules:
  0.0 178.2 jit_solution(14184996553142528639)
XLA Ops:
  0.0 0.0 copy-start
  0.0 0.0 copy-start.6
  0.0 0.7 copy-done.6
  0.7 2.9 %pack.3 = f32[32,24,128]{2,1,0:T(8,128)} custom-call(s32[32]{0:T(128)S(1)} %copy-done.6, f32[32,3,128]{2,1,0:T(4,128)} %bitcast.17), custom_call_target="tpu_custom_call" | custom-call | tf_op jit(solution)/shard_map/pack/pallas_call | solution.py:106
  3.5 0.0 copy-start.5
  3.5 0.0 copy-start.7
  3.5 0.0 copy-start.3
  3.6 45.9 %all-to-all-start.2 = ((f32[32,24,128]{2,1,0:T(8,128)}), f32[32,24,128]{2,1,0:T(8,128)}, u32[]{:S(2)}, u32[]{:S(2)}) async-start(f32[32,24,128]{2,1,0:T(8,128)} %pack.3), calls=%async_computation.2 | async-start | bytes 786432 | tf_op jit(solution)/shard_map/all_to_all | solution.py:312
  49.5 0.0 copy-done
  49.5 0.0 copy-done.5
  49.5 0.0 copy-done.7
  49.5 0.2 fusion.8
  49.7 0.0 copy-done.3
  49.8 0.0 copy-start.2
  49.8 3.7 %collective-permute-start = (f32[1088,128]{1,0:T(8,128)S(1)}, f32[1088,128]{1,0:T(8,128)S(1)}, u32[]{:S(2)}, u32[]{:S(2)}) collective-permute-start(f32[1088,128]{1,0:T(8,128)S(1)} %select_maximum_fusion.refs_0_), channel_id=1, source_target_pairs={{0,2},{2,4},{4,6},{6,0},{1,3},{3,5},{5,7},{7,1},{8,10},{10,12},{12... | collective-permute-start | bytes 1671176 | tf_op jit(solution)/shard_map/ppermute | solution.py:305
  53.5 3.5 %collective-permute-start.1 = (f32[1088,128]{1,0:T(8,128)S(1)}, f32[1088,128]{1,0:T(8,128)S(1)}, u32[]{:S(2)}, u32[]{:S(2)}) collective-permute-start(f32[1088,128]{1,0:T(8,128)S(1)} %select_maximum_fusion.refs_0_), channel_id=1, source_target_pairs={{0,6},{2,0},{4,2},{6,4},{1,7},{3,1},{5,3},{7,5},{8,14},{10,8},{12,... | collective-permute-start | bytes 1671176 | tf_op jit(solution)/shard_map/ppermute | solution.py:305
  57.1 4.0 %collective-permute-start.2 = (f32[1088,128]{1,0:T(8,128)S(1)}, f32[1088,128]{1,0:T(8,128)S(1)}, u32[]{:S(2)}, u32[]{:S(2)}) collective-permute-start(f32[1088,128]{1,0:T(8,128)S(1)} %select_maximum_fusion.refs_0_), channel_id=1, source_target_pairs={{0,4},{2,6},{4,0},{6,2},{1,5},{3,7},{5,1},{7,3},{8,12},{10,14},{12... | collective-permute-start | bytes 1671176 | tf_op jit(solution)/shard_map/ppermute | solution.py:305
  61.1 2.0 %collective-permute-start.3 = (f32[1088,128]{1,0:T(8,128)S(1)}, f32[1088,128]{1,0:T(8,128)S(1)}, u32[]{:S(2)}, u32[]{:S(2)}) collective-permute-start(f32[1088,128]{1,0:T(8,128)S(1)} %select_maximum_fusion.refs_0_), channel_id=1, source_target_pairs={{0,1},{1,0},{2,3},{3,2},{4,5},{5,4},{6,7},{7,6},{8,9},{9,8},{10,11... | collective-permute-start | bytes 1671176 | tf_op jit(solution)/shard_map/ppermute | solution.py:308
  63.1 4.6 %collective-permute-done.refs_1_ = f32[1088,128]{1,0:T(8,128)S(1)} collective-permute-done((f32[1088,128]{1,0:T(8,128)S(1)}, f32[1088,128]{1,0:T(8,128)S(1)}, u32[]{:S(2)}, u32[]{:S(2)}) %collective-permute-start) | collective-permute-done | bytes 557088 | tf_op jit(solution)/shard_map/ppermute | solution.py:305
  67.6 1.9 %collective-permute-start.4 = (f32[1088,128]{1,0:T(8,128)S(1)}, f32[1088,128]{1,0:T(8,128)S(1)}, u32[]{:S(2)}, u32[]{:S(2)}) collective-permute-start(f32[1088,128]{1,0:T(8,128)S(1)} %collective-permute-done.refs_1_), channel_id=1, source_target_pairs={{0,1},{1,0},{2,3},{3,2},{4,5},{5,4},{6,7},{7,6},{8,9},{9,8},{10,11... | collective-permute-start | bytes 1671176 | tf_op jit(solution)/shard_map/ppermute | solution.py:308
  69.6 11.1 %collective-permute-done.1.refs_2_ = f32[1088,128]{1,0:T(8,128)S(1)} collective-permute-done((f32[1088,128]{1,0:T(8,128)S(1)}, f32[1088,128]{1,0:T(8,128)S(1)}, u32[]{:S(2)}, u32[]{:S(2)}) %collective-permute-start.1) | collective-permute-done | bytes 557088 | tf_op jit(solution)/shard_map/ppermute | solution.py:305
  80.6 1.9 %collective-permute-start.5 = (f32[1088,128]{1,0:T(8,128)S(1)}, f32[1088,128]{1,0:T(8,128)}, u32[]{:S(2)}, u32[]{:S(2)}) collective-permute-start(f32[1088,128]{1,0:T(8,128)S(1)} %collective-permute-done.1.refs_2_), channel_id=1, source_target_pairs={{0,1},{1,0},{2,3},{3,2},{4,5},{5,4},{6,7},{7,6},{8,9},{9,8},{10,11... | collective-permute-start | bytes 1671176 | tf_op jit(solution)/shard_map/ppermute | solution.py:308
  82.6 0.0 collective-permute-done.2.refs_3_
  82.6 2.4 %collective-permute-start.6 = (f32[1088,128]{1,0:T(8,128)S(1)}, f32[1088,128]{1,0:T(8,128)}, u32[]{:S(2)}, u32[]{:S(2)}) collective-permute-start(f32[1088,128]{1,0:T(8,128)S(1)} %collective-permute-done.2.refs_3_), channel_id=1, source_target_pairs={{0,1},{1,0},{2,3},{3,2},{4,5},{5,4},{6,7},{7,6},{8,9},{9,8},{10,11... | collective-permute-start | bytes 1671176 | tf_op jit(solution)/shard_map/ppermute | solution.py:308
  85.1 0.1 iota.18
  85.2 17.6 %all-to-all-done.2.recv_ref = f32[32,24,128]{2,1,0:T(8,128)} async-done(((f32[32,24,128]{2,1,0:T(8,128)}), f32[32,24,128]{2,1,0:T(8,128)}, u32[]{:S(2)}, u32[]{:S(2)}) %all-to-all-start.2) | async-done | bytes 393248 | tf_op jit(solution)/shard_map/all_to_all | solution.py:312
  102.7 1.0 fusion.16
  103.7 0.1 convert_element_type.25
  103.8 0.6 fusion.13.meta_ref
  104.4 0.0 collective-permute-done.3.refs_4_
  104.4 0.0 collective-permute-done.4.refs_5_
  104.4 0.0 collective-permute-done.5.refs_6_
  104.4 0.0 collective-permute-done.6.refs_7_
  104.4 0.0 copy-done.2
  104.4 4.8 %evaluate.3 = f32[32,7,4,128]{3,2,1,0:T(4,128)} custom-call(s32[512]{0:T(512)} %fusion.13.meta_ref, f32[32,24,128]{2,1,0:T(8,128)} %all-to-all-done.2.recv_ref, f32[5,8,8,128]{3,2,1,0:T(8,128)S(1)} %copy-done.2, f32[1088,128]{1,0:T(8,128)S(1)} %select_maximum_fusion.refs_0_, f32[1088,128]{1,0:T(8,128)S(1)} %collective-permute-done.refs_1_, ...), custom_call_target="tpu_custom_call" | custom-call | tf_op jit(solution)/shard_map/evaluate/pallas_call | solution.py:239
  109.3 7.0 %all-to-all-start.3 = ((f32[32,7,4,128]{3,2,1,0:T(4,128)}), f32[32,7,4,128]{3,2,1,0:T(4,128)}, u32[]{:S(2)}, u32[]{:S(2)}) async-start(f32[32,7,4,128]{3,2,1,0:T(4,128)} %evaluate.3), calls=%async_computation.3 | async-start | bytes 917504 | tf_op jit(solution)/shard_map/all_to_all | solution.py:312
  116.3 0.9 slice_convert_fusion.1
  117.2 0.7 slice_reduce_fusion
  118.6 56.3 %all-to-all-done.3.back_ref = f32[32,7,4,128]{3,2,1,0:T(4,128)} async-done(((f32[32,7,4,128]{3,2,1,0:T(4,128)}), f32[32,7,4,128]{3,2,1,0:T(4,128)}, u32[]{:S(2)}, u32[]{:S(2)}) %all-to-all-start.3) | async-done | bytes 458784 | tf_op jit(solution)/shard_map/all_to_all | solution.py:312
  174.8 0.6 broadcast_in_dim.18.before_ref
  175.5 2.7 %unpack.3 = f32[32,4,128]{2,1,0:T(4,128)} custom-call(s32[32]{0:T(128)S(1)} %copy-done.6, f32[32,7,4,128]{3,2,1,0:T(4,128)} %all-to-all-done.3.back_ref, f32[32,4,128]{2,1,0:T(4,128)} %broadcast_in_dim.18.before_ref), custom_call_target="tpu_custom_call" | custom-call | tf_op jit(solution)/shard_map/unpack/pallas_call | solution.py:284
  (4 shorter events, 0.1 us)
Async XLA Ops:
  0.0 49.5 %copy-start = (f32[24,64]{1,0:T(8,128)S(1)}, f32[24,64]{1,0:T(8,128)}, u32[]{:S(2)}) copy-start(f32[24,64]{1,0:T(8,128)} %param.11) | copy-start | bytes 18436
  0.0 0.7 copy-start.6
  3.5 45.9 %copy-start.5 = (f32[24,24]{1,0:T(8,128)S(1)}, f32[24,24]{1,0:T(8,128)}, u32[]{:S(2)}) copy-start(f32[24,24]{1,0:T(8,128)} %constant.156.clone) | copy-start | bytes 6916
  3.5 45.9 %copy-start.7 = (f32[24]{0:T(128)S(1)}, f32[24]{0:T(128)}, u32[]{:S(2)}) copy-start(f32[24]{0:T(128)} %constant.164) | copy-start | bytes 292
  3.5 46.2 %copy-start.3 = (f32[64,4,512]{2,1,0:T(4,128)S(1)}, f32[64,4,512]{2,1,0:T(4,128)}, u32[]{:S(2)}) copy-start(f32[64,4,512]{2,1,0:T(4,128)} %param.10) | copy-start | bytes 1572868
  3.6 99.2 %all-to-all-start.2 = ((f32[32,24,128]{2,1,0:T(8,128)}), f32[32,24,128]{2,1,0:T(8,128)}, u32[]{:S(2)}, u32[]{:S(2)}) async-start(f32[32,24,128]{2,1,0:T(8,128)} %pack.3), calls=%async_computation.2 | async-start | bytes 786432 | tf_op jit(solution)/shard_map/all_to_all | solution.py:312
  49.8 54.7 %copy-start.2 = (f32[5,8,8,128]{3,2,1,0:T(8,128)S(1)}, f32[5,8,8,128]{3,2,1,0:T(8,128)}, u32[]{:S(2)}) copy-start(f32[5,8,8,128]{3,2,1,0:T(8,128)} %constant.158.clone.const_ref) | copy-start | bytes 491524
  49.8 17.8 %collective-permute-start = (f32[1088,128]{1,0:T(8,128)S(1)}, f32[1088,128]{1,0:T(8,128)S(1)}, u32[]{:S(2)}, u32[]{:S(2)}) collective-permute-start(f32[1088,128]{1,0:T(8,128)S(1)} %select_maximum_fusion.refs_0_), channel_id=1, source_target_pairs={{0,2},{2,4},{4,6},{6,0},{1,3},{3,5},{5,7},{7,1},{8,10},{10,12},{12... | collective-permute-start | bytes 1671176 | tf_op jit(solution)/shard_map/ppermute | solution.py:305
  53.5 27.1 %collective-permute-start.1 = (f32[1088,128]{1,0:T(8,128)S(1)}, f32[1088,128]{1,0:T(8,128)S(1)}, u32[]{:S(2)}, u32[]{:S(2)}) collective-permute-start(f32[1088,128]{1,0:T(8,128)S(1)} %select_maximum_fusion.refs_0_), channel_id=1, source_target_pairs={{0,6},{2,0},{4,2},{6,4},{1,7},{3,1},{5,3},{7,5},{8,14},{10,8},{12,... | collective-permute-start | bytes 1671176 | tf_op jit(solution)/shard_map/ppermute | solution.py:305
  57.1 25.5 %collective-permute-start.2 = (f32[1088,128]{1,0:T(8,128)S(1)}, f32[1088,128]{1,0:T(8,128)S(1)}, u32[]{:S(2)}, u32[]{:S(2)}) collective-permute-start(f32[1088,128]{1,0:T(8,128)S(1)} %select_maximum_fusion.refs_0_), channel_id=1, source_target_pairs={{0,4},{2,6},{4,0},{6,2},{1,5},{3,7},{5,1},{7,3},{8,12},{10,14},{12... | collective-permute-start | bytes 1671176 | tf_op jit(solution)/shard_map/ppermute | solution.py:305
  61.1 43.3 %collective-permute-start.3 = (f32[1088,128]{1,0:T(8,128)S(1)}, f32[1088,128]{1,0:T(8,128)S(1)}, u32[]{:S(2)}, u32[]{:S(2)}) collective-permute-start(f32[1088,128]{1,0:T(8,128)S(1)} %select_maximum_fusion.refs_0_), channel_id=1, source_target_pairs={{0,1},{1,0},{2,3},{3,2},{4,5},{5,4},{6,7},{7,6},{8,9},{9,8},{10,11... | collective-permute-start | bytes 1671176 | tf_op jit(solution)/shard_map/ppermute | solution.py:308
  67.6 36.8 %collective-permute-start.4 = (f32[1088,128]{1,0:T(8,128)S(1)}, f32[1088,128]{1,0:T(8,128)S(1)}, u32[]{:S(2)}, u32[]{:S(2)}) collective-permute-start(f32[1088,128]{1,0:T(8,128)S(1)} %collective-permute-done.refs_1_), channel_id=1, source_target_pairs={{0,1},{1,0},{2,3},{3,2},{4,5},{5,4},{6,7},{7,6},{8,9},{9,8},{10,11... | collective-permute-start | bytes 1671176 | tf_op jit(solution)/shard_map/ppermute | solution.py:308
  80.6 23.8 %collective-permute-start.5 = (f32[1088,128]{1,0:T(8,128)S(1)}, f32[1088,128]{1,0:T(8,128)}, u32[]{:S(2)}, u32[]{:S(2)}) collective-permute-start(f32[1088,128]{1,0:T(8,128)S(1)} %collective-permute-done.1.refs_2_), channel_id=1, source_target_pairs={{0,1},{1,0},{2,3},{3,2},{4,5},{5,4},{6,7},{7,6},{8,9},{9,8},{10,11... | collective-permute-start | bytes 1671176 | tf_op jit(solution)/shard_map/ppermute | solution.py:308
  82.6 21.8 %collective-permute-start.6 = (f32[1088,128]{1,0:T(8,128)S(1)}, f32[1088,128]{1,0:T(8,128)}, u32[]{:S(2)}, u32[]{:S(2)}) collective-permute-start(f32[1088,128]{1,0:T(8,128)S(1)} %collective-permute-done.2.refs_3_), channel_id=1, source_target_pairs={{0,1},{1,0},{2,3},{3,2},{4,5},{5,4},{6,7},{7,6},{8,9},{9,8},{10,11... | collective-permute-start | bytes 1671176 | tf_op jit(solution)/shard_map/ppermute | solution.py:308
  109.3 65.6 %all-to-all-start.3 = ((f32[32,7,4,128]{3,2,1,0:T(4,128)}), f32[32,7,4,128]{3,2,1,0:T(4,128)}, u32[]{:S(2)}, u32[]{:S(2)}) async-start(f32[32,7,4,128]{3,2,1,0:T(4,128)} %evaluate.3), calls=%async_computation.3 | async-start | bytes 917504 | tf_op jit(solution)/shard_map/all_to_all | solution.py:312

commit v2 on v1

v2 whole, which is shorter than its diff:
```python
import functools

import jax
import jax.numpy as jnp
import numpy as np
from jax import lax
from jax.experimental import pallas as pl
from jax.experimental.pallas import tpu as pltpu
from jax.sharding import PartitionSpec as P

NEWTON = 3
CAP = 2
FIRST = 7
LANES = 128
ID_LANES = 16
FULLEST, COUNT = ID_LANES - 2, ID_LANES - 1

GLL_POINTS = (
    -1.0,
    -0.8717401485096066,
    -0.5917001814331423,
    -0.2092992179024789,
    0.2092992179024789,
    0.5917001814331423,
    0.8717401485096066,
    1.0,
)
EXACT = lax.Precision.HIGHEST


def monomial_table():
    signs = np.array([[2.0 * (c >> 2 - a & 1) - 1.0 for c in range(8)] for a in range(3)])
    table = np.zeros((24, 24), np.float32)
    offset = np.zeros((24,), np.float32)
    for m in range(8):
        row = np.ones(8)
        for a in range(3):
            if m >> 2 - a & 1:
                row = row * signs[a]
        for a in range(3):
            table[8 * a + m, 8 * a : 8 * a + 8] = row / 8.0
            offset[8 * a + m] = float(np.sum(row * signs[a]) / 8.0)
    return table, offset


def lagrange_constants():
    nodes = np.array(GLL_POINTS, np.float64)
    plain = [0, 1, 2, 3, 4, 5, 6, 7]
    orders = [plain] + [[i] * 4 + [i + 2] * 4 for i in (0, 4, 1, 5)]
    blocks = []
    for order in orders:
        for k in range(7):
            blocks.append([nodes[[m for m in range(8) if m != i][k]] for i in order])
        factor = []
        for i in order:
            others = [nodes[i] - nodes[m] for m in range(8) if m != i]
            factor.append(1.0 / np.prod(others))
        blocks.append(factor)
    table = np.array(blocks, np.float32).reshape(len(orders), 8, 8)
    return np.repeat(table[..., None], LANES, axis=-1)


def divided(value, by):
    if by & (by - 1) == 0:
        return value >> (by.bit_length() - 1), value & (by - 1)
    return lax.div(value, by), lax.rem(value, by)


def pack_kernel(first, slots, elems, segs, subs, owners, targets, send_ref, at_ref, *scratch):
    owners_ref, targets_ref, seen, meta, sems = scratch
    copies = [
        pltpu.make_async_copy(owners, owners_ref, sems.at[0]),
        pltpu.make_async_copy(targets, targets_ref, sems.at[1]),
    ]
    for copy in copies:
        copy.start()
    rows, last = send_ref.shape[0], 3 * slots
    my_seg, my_sub = lax.axis_index("seg"), lax.axis_index("sub")
    lane = lax.broadcasted_iota(jnp.int32, (1, LANES), 1)
    meta[...] = jnp.zeros_like(meta)
    for r in range(rows):
        seen[r] = 0
    for copy in copies:
        copy.wait()

    def place(b, fullest):
        device, elem = divided(owners_ref[b], elems)
        device, sub = divided(device, subs)
        r, seg = divided(device, segs)
        apart = divided(seg - my_seg + segs, segs)[1]
        code = (apart + jnp.where(sub == my_sub, 0, segs)) * elems + elem
        k = seen[r]
        seen[r] = k + 1
        slot = k - first
        at_ref[b] = jnp.where(jnp.logical_and(slot >= 0, slot < slots), r * slots + slot, -1)

        @pl.when(jnp.logical_and(slot >= 0, slot < slots))
        def _():
            points = targets_ref[b]
            for a in range(3):
                send_ref[r, slot * 3 + a] = points[a : a + 1]
            added = jnp.where(lane == slot, code, jnp.where(lane == COUNT, 1, 0))
            meta[pl.ds(r, 1), :] += added

        return jnp.maximum(fullest, k + 1)

    fullest = lax.fori_loop(0, targets_ref.shape[0], place, jnp.int32(0), unroll=4)
    ids = jnp.where(lane == FULLEST, fullest, meta[...]).astype(jnp.float32)
    for r in range(rows):
        send_ref[r, last] = ids[r : r + 1]


def pack(owners, block_points, rows, first, slots, elems, segs, subs):
    blocks = owners.shape[0]
    return pl.pallas_call(
        functools.partial(pack_kernel, first, slots, elems, segs, subs),
        out_shape=[
            jax.ShapeDtypeStruct((rows, 3 * slots + 1, 1, LANES), jnp.float32),
            jax.ShapeDtypeStruct((blocks,), jnp.int32),
        ],
        in_specs=[pl.BlockSpec(memory_space=pltpu.HBM)] * 2,
        out_specs=[
            pl.BlockSpec(memory_space=pltpu.VMEM),
            pl.BlockSpec(memory_space=pltpu.SMEM),
        ],
        scratch_shapes=[
            pltpu.SMEM(owners.shape, jnp.int32),
            pltpu.VMEM(block_points.shape, jnp.float32),
            pltpu.SMEM((rows,), jnp.int32),
            pltpu.VMEM((rows, LANES), jnp.int32),
            pltpu.SemaphoreType.DMA((2,)),
        ],
        compiler_params=pltpu.CompilerParams(vmem_limit_bytes=4 << 20),
        name="pack",
    )(owners, block_points)


def newton(coef, target):
    def mapped(a, m):
        return coef[8 * a + m]

    def solve(jac, misfit):
        cof = [[None] * 3 for _ in range(3)]
        for r in range(3):
            r0, r1 = (r + 1) % 3, (r + 2) % 3
            for c in range(3):
                c0, c1 = (c + 1) % 3, (c + 2) % 3
                cof[r][c] = jac[r0][c0] * jac[r1][c1] - jac[r0][c1] * jac[r1][c0]
        det = jac[0][0] * cof[0][0] + jac[0][1] * cof[0][1] + jac[0][2] * cof[0][2]
        inverse = 1.0 / det
        return [
            (cof[0][c] * misfit[0] + cof[1][c] * misfit[1] + cof[2][c] * misfit[2]) * inverse
            for c in range(3)
        ]

    jac = [[mapped(a, 4), mapped(a, 2), mapped(a, 1)] for a in range(3)]
    step = solve(jac, [mapped(a, 0) - target[a] for a in range(3)])
    pos = [jnp.clip(-s, -1.2, 1.2) for s in step]
    for _ in range(NEWTON - 1):
        u, v, w = pos
        uv, uw, vw = u * v, u * w, v * w
        jac, misfit = [], []
        for a in range(3):
            du = mapped(a, 4) + mapped(a, 6) * v + mapped(a, 5) * w + mapped(a, 7) * vw
            dv = mapped(a, 2) + mapped(a, 6) * u + mapped(a, 3) * w + mapped(a, 7) * uw
            dw = mapped(a, 1) + mapped(a, 5) * u + mapped(a, 3) * v + mapped(a, 7) * uv
            at = mapped(a, 0) + mapped(a, 2) * v + mapped(a, 1) * w + mapped(a, 3) * vw + u * du
            jac.append([du, dv, dw])
            misfit.append(at - target[a])
        step = solve(jac, misfit)
        pos = [jnp.clip(p - s, -1.2, 1.2) for p, s in zip(pos, step)]
    return pos


def lagrange(point, table):
    value = (point - table[0]) * table[7]
    for k in range(1, 7):
        value = value * (point - table[k])
    return value


def halves(value):
    high = value.astype(jnp.bfloat16)
    return high, (value - high.astype(jnp.float32)).astype(jnp.bfloat16)


def evaluate_kernel(elems, slots, recv_ref, const_ref, *refs):
    pieces, (out_ref, fields, shapes, points, coefs, meta, live, sems) = refs[:8], refs[8:]
    senders = recv_ref.shape[0]
    ids = pltpu.make_async_copy(recv_ref.at[:, 3 * slots, 0, :], meta, sems.at[0])
    ids.start()
    copies = []
    for k, piece in enumerate(pieces):
        size = elems * 16
        copies += [
            pltpu.make_async_copy(
                piece.at[pl.ds(0, size)], fields.at[pl.ds(k * size, size)], sems.at[2 * k + 1]
            ),
            pltpu.make_async_copy(
                piece.at[pl.ds(size, elems)], shapes.at[pl.ds(k * elems, elems)], sems.at[2 * k + 2]
            ),
        ]
    for copy in copies:
        copy.start()
    ids.wait()

    def of_sender(s, total):
        used = meta[s, COUNT].astype(jnp.int32)

        def of_slot(k, carry):
            live[total + k] = s * ID_LANES + k
            return carry

        lax.fori_loop(0, used, of_slot, 0)
        return total + used

    total = lax.fori_loop(0, senders, of_sender, jnp.int32(0))
    for copy in copies:
        copy.wait()

    lane = lax.broadcasted_iota(jnp.int32, (16, LANES), 1)

    def group(g, carry):
        where = []
        for u in range(8):
            s, k = divided(live[jnp.minimum(g * 8 + u, total - 1)], ID_LANES)
            code = meta[s, k].astype(jnp.int32)
            where.append((s * slots + k, code * 16))
            for a in range(3):
                points[a, pl.ds(u, 1), :] = recv_ref[s, k * 3 + a]
            coefs[pl.ds(u, 1), :] = shapes[pl.ds(code, 1), :]
        all_coefs = coefs[...]
        coef = [jnp.broadcast_to(all_coefs[:, m : m + 1], (8, LANES)) for m in range(24)]
        pos = newton(coef, [points[a] for a in range(3)])
        for u in range(8):
            slot, start = where[u]
            rows = [jnp.broadcast_to(p[u : u + 1], (8, LANES)) for p in pos]
            along_y = lagrange(rows[1], const_ref[0])
            along_z = lagrange(rows[2], const_ref[0])
            weights = jnp.concatenate(
                [jnp.broadcast_to(along_y[j : j + 1], (8, LANES)) * along_z for j in range(8)], axis=0
            )
            weights = jnp.concatenate(halves(weights), axis=0)
            field = fields[pl.ds(pl.multiple_of(start, 16), 16), :]
            turned = pltpu.roll(field, LANES // 2, 1)
            even = jnp.where(lane < LANES // 2, field, turned)
            odd = jnp.where(lane < LANES // 2, turned, field)
            both = jnp.concatenate(halves(jnp.concatenate([even, odd], axis=0)), axis=0)
            sums = jnp.dot(both, weights, preferred_element_type=jnp.float32)
            total_x = None
            for q in range(4):
                term = sums[8 * q : 8 * q + 8] + sums[32 + 8 * q : 40 + 8 * q]
                term = term * lagrange(rows[0], const_ref[1 + q])
                total_x = term if total_x is None else total_x + term
            out_ref[slot] = total_x[0:4] + total_x[4:8]
        return carry

    lax.fori_loop(0, (total + 7) // 8, group, 0)


def evaluate(recv, pieces, slots, elems):
    senders = recv.shape[0]
    return pl.pallas_call(
        functools.partial(evaluate_kernel, elems, slots),
        out_shape=jax.ShapeDtypeStruct((senders * slots, 4, LANES), jnp.float32),
        in_specs=[pl.BlockSpec(memory_space=pltpu.VMEM)] * 2
        + [pl.BlockSpec(memory_space=pl.ANY)] * 8,
        out_specs=pl.BlockSpec(memory_space=pltpu.VMEM),
        scratch_shapes=[
            pltpu.VMEM((8 * elems * 16, LANES), jnp.float32),
            pltpu.VMEM((8 * elems, LANES), jnp.float32),
            pltpu.VMEM((3, 8, LANES), jnp.float32),
            pltpu.VMEM((8, LANES), jnp.float32),
            pltpu.SMEM((senders, LANES), jnp.float32),
            pltpu.SMEM((senders * ID_LANES,), jnp.int32),
            pltpu.SemaphoreType.DMA((17,)),
        ],
        compiler_params=pltpu.CompilerParams(vmem_limit_bytes=12 << 20),
        name="evaluate",
    )(recv, jnp.asarray(lagrange_constants()), *pieces)


def unpack_kernel(has_before, at_ref, back_ref, *refs):
    out_ref = refs[-1]
    for b in range(out_ref.shape[0]):
        if has_before:
            at = at_ref[b]
            taken = back_ref[jnp.maximum(at, 0)]
            out_ref[b] = jnp.where(at >= 0, taken, refs[0][b])
        else:
            out_ref[b] = back_ref[jnp.maximum(at_ref[b], 0)]

def unpack(at, back, before):
    held = [] if before is None else [before]
    return pl.pallas_call(
        functools.partial(unpack_kernel, before is not None),
        out_shape=jax.ShapeDtypeStruct((at.shape[0], 4, LANES), jnp.float32),
        in_specs=[pl.BlockSpec(memory_space=pltpu.SMEM)]
        + [pl.BlockSpec(memory_space=pltpu.VMEM)] * (1 + len(held)),
        out_specs=pl.BlockSpec(memory_space=pltpu.VMEM),
        compiler_params=pltpu.CompilerParams(vmem_limit_bytes=4 << 20),
        name="unpack",
    )(at, back, *held)


def row_pieces(old_fields, corner_shift):
    elems = old_fields.shape[0]
    table, offset = monomial_table()
    coefs = jnp.dot(jnp.asarray(table), corner_shift, precision=EXACT) + offset[:, None]
    coefs = jnp.pad(coefs.T, ((0, 0), (0, LANES - coefs.shape[0])))
    fields = old_fields.reshape(elems, 4, 4, LANES).transpose(0, 2, 1, 3).reshape(-1, LANES)
    own = jnp.concatenate([fields, coefs], axis=0)
    segs = lax.axis_size("seg")

    def along(step):
        return lax.ppermute(own, "seg", [(i, (i + step) % segs) for i in range(segs)])

    half = [own] + [along(segs - apart) for apart in range(1, segs)]
    return half + [lax.ppermute(piece, "sub", [(0, 1), (1, 0)]) for piece in half]


def all_to_all(array):
    return lax.all_to_all(array, "block", split_axis=0, concat_axis=0, tiled=True)


def shards(old_fields, corner_shift, targets, owners):
    rows = lax.axis_size("block")
    segs, subs = lax.axis_size("seg"), lax.axis_size("sub")
    elems = old_fields.shape[0]
    most = CAP * segs * subs
    block_points = targets.reshape(3, owners.shape[0], -1).transpose(1, 0, 2)
    pieces = row_pieces(old_fields, corner_shift)

    def trip(first, slots, before):
        send, at = pack(owners, block_points, rows, first, slots, elems, segs, subs)
        recv = all_to_all(send)
        answers = evaluate(recv, pieces, slots, elems).reshape(rows, slots, 4, LANES)
        back = all_to_all(answers).reshape(rows * slots, 4, LANES)
        return unpack(at, back, before), recv[:, 3 * slots, 0, FULLEST]

    done, fullest = trip(0, FIRST, None)
    done = lax.cond(
        jnp.max(fullest) > FIRST,
        lambda held: trip(FIRST, most - FIRST, held)[0],
        lambda held: held,
        done,
    )
    return done.transpose(1, 0, 2).reshape(4, -1)


def solution(mesh):
    split = ("groups", "block", "seg", "sub")
    in_specs = (P(split, None, None), P(None, split), P(None, split), P(split))
    return jax.shard_map(
        shards, mesh=mesh, in_specs=in_specs, out_specs=P(None, split), check_vma=False
    )
```

time: 179 us -> 177 us (0.989)
  Pallas kernels: 10.4 us -> 7.47 us
  other arithmetic: 3.26 us -> 0.74 us
  starting transfers between devices: 72.5 us -> 74.7 us
  waiting for transfers between devices: 89.5 us -> 87.3 us
    all_to_all x2, waiting for transfers between devices: 73.8 us -> 69.5 us  [all_to_all(): lax.all_to_all(array, 'block', split_axis=0, concat_axis=0, tiled=True)]
    pallas_call x3, Pallas kernels: 10.4 us -> 7.47 us  [the longest x1 4.81 us: evaluate(): pl.pallas_call(functools.partial(evaluate_kernel, elems, slots), out_shap...]
    all_to_all x2, starting transfers between devices: 52.9 us -> 55.8 us  [all_to_all(): lax.all_to_all(array, 'block', split_axis=0, concat_axis=0, tiled=True)]
    unnamed x12 -> x22, local copies, waits for them, and re-layouts: 0.69 us -> 3.23 us
    convert_element_type x2 -> x0, other arithmetic: 1.89 us -> none  [trip(): meta = recv[:, 3 * slots, :ID_LANES].astype(jnp.int32)]
    ppermute x3, waiting for transfers between devices: 15.6 us -> 17.4 us  [along(): lax.ppermute(own, 'seg', [(i, (i + step) % segs) for i in range(segs)])]
  transfers between devices with their start and end apart: 9 -> 9, of which waited for: 4 -> 5; matrix products, arithmetic and copies ran while one was open for 2% -> 1% of each run, Pallas kernels for 0% -> 0%
where the time goes in v2:
time: 177 us; the launch traced here: 175 us
  waiting for transfers between devices  87.3 us (49%)
  starting transfers between devices  74.7 us (42%)
  Pallas kernels  7.47 us (4%)
  local copies, waits for them, and re-layouts  3.23 us (2%)
    all_to_all x2, waiting for transfers between devices, all_to_all(): lax.all_to_all(array, 'block', split_axis=0, concat_axis=0, tiled=True)  69.5 us
    all_to_all x2, starting transfers between devices, all_to_all(): lax.all_to_all(array, 'block', split_axis=0, concat_axis=0, tiled=True)  55.8 us
    ppermute x3, waiting for transfers between devices, along(): lax.ppermute(own, 'seg', [(i, (i + step) % segs) for i in range(segs)])  17.4 us
    ppermute x3, starting transfers between devices, along(): lax.ppermute(own, 'seg', [(i, (i + step) % segs) for i in range(segs)])  10.7 us
    ppermute x4, starting transfers between devices, row_pieces(): lax.ppermute(piece, 'sub', [(0, 1), (1, 0)])  8.27 us
    pallas_call x1, Pallas kernels, evaluate(): pl.pallas_call(functools.partial(evaluate_kernel, elems, slots), out_shap...  4.81 us
  transfers between devices with their start and end apart: 9, of which 5 were waited for; matrix products, arithmetic and copies ran while one was open for 1% of the time, Pallas kernels for 0%

profile of v2, /device:TPU:40, one launch (start us, length us, event | category | flops | bytes accessed | tf_op | source)
XLA Modules:
  0.0 174.5 jit_solution(12119465784466760089)
XLA Ops:
  0.0 0.0 copy-start
  0.0 0.0 copy-start.10
  0.0 0.0 copy-start.6
  0.0 0.7 copy-done.10
  0.7 2.1 %pack.3 = (f32[32,22,1,128]{3,2,1,0:T(1,128)}, s32[32]{0:T(128)S(1)}) custom-call(s32[32]{0:T(128)S(1)} %copy-done.10, f32[32,3,128]{2,1,0:T(4,128)} %bitcast.22), custom_call_target="tpu_custom_call" | custom-call | tf_op jit(solution)/shard_map/pack/pallas_call | solution.py:115
  2.8 0.0 copy-start.9
  2.8 0.0 copy-start.11
  2.8 45.8 %all-to-all-start.2 = ((f32[32,22,1,128]{3,2,1,0:T(1,128)}), f32[32,22,1,128]{3,2,1,0:T(1,128)S(1)}, u32[]{:S(2)}, u32[]{:S(2)}) async-start(f32[32,22,1,128]{3,2,1,0:T(1,128)} %get-tuple-element.49), calls=%async_computation.2 | async-start | bytes 720896 | tf_op jit(solution)/shard_map/all_to_all | solution.py:323
  48.6 0.0 copy-done
  48.6 0.0 copy-done.9
  48.6 0.0 copy-done.11
  48.6 0.2 fusion
  48.8 0.0 copy-done.6
  48.8 0.0 copy-start.5
  48.9 5.2 %collective-permute-start = (f32[1088,128]{1,0:T(8,128)S(1)}, f32[1088,128]{1,0:T(8,128)S(1)}, u32[]{:S(2)}, u32[]{:S(2)}) collective-permute-start(f32[1088,128]{1,0:T(8,128)S(1)} %select_maximum_fusion.refs_0_), channel_id=1, source_target_pairs={{0,6},{2,0},{4,2},{6,4},{1,7},{3,1},{5,3},{7,5},{8,14},{10,8},{12,... | collective-permute-start | bytes 1671176 | tf_op jit(solution)/shard_map/ppermute | solution.py:316
  54.1 2.5 %collective-permute-start.1 = (f32[1088,128]{1,0:T(8,128)S(1)}, f32[1088,128]{1,0:T(8,128)S(1)}, u32[]{:S(2)}, u32[]{:S(2)}) collective-permute-start(f32[1088,128]{1,0:T(8,128)S(1)} %select_maximum_fusion.refs_0_), channel_id=1, source_target_pairs={{0,4},{2,6},{4,0},{6,2},{1,5},{3,7},{5,1},{7,3},{8,12},{10,14},{12... | collective-permute-start | bytes 1671176 | tf_op jit(solution)/shard_map/ppermute | solution.py:316
  56.6 3.0 %collective-permute-start.2 = (f32[1088,128]{1,0:T(8,128)S(1)}, f32[1088,128]{1,0:T(8,128)S(1)}, u32[]{:S(2)}, u32[]{:S(2)}) collective-permute-start(f32[1088,128]{1,0:T(8,128)S(1)} %select_maximum_fusion.refs_0_), channel_id=1, source_target_pairs={{0,2},{2,4},{4,6},{6,0},{1,3},{3,5},{5,7},{7,1},{8,10},{10,12},{12... | collective-permute-start | bytes 1671176 | tf_op jit(solution)/shard_map/ppermute | solution.py:316
  59.6 2.0 %collective-permute-start.3 = (f32[1088,128]{1,0:T(8,128)S(1)}, f32[1088,128]{1,0:T(8,128)S(1)}, u32[]{:S(2)}, u32[]{:S(2)}) collective-permute-start(f32[1088,128]{1,0:T(8,128)S(1)} %select_maximum_fusion.refs_0_), channel_id=1, source_target_pairs={{0,1},{1,0},{2,3},{3,2},{4,5},{5,4},{6,7},{7,6},{8,9},{9,8},{10,11... | collective-permute-start | bytes 1671176 | tf_op jit(solution)/shard_map/ppermute | solution.py:319
  61.5 16.2 %collective-permute-done.refs_1_ = f32[1088,128]{1,0:T(8,128)S(1)} collective-permute-done((f32[1088,128]{1,0:T(8,128)S(1)}, f32[1088,128]{1,0:T(8,128)S(1)}, u32[]{:S(2)}, u32[]{:S(2)}) %collective-permute-start) | collective-permute-done | bytes 557088 | tf_op jit(solution)/shard_map/ppermute | solution.py:316
  77.7 1.9 %collective-permute-start.4 = (f32[1088,128]{1,0:T(8,128)S(1)}, f32[1088,128]{1,0:T(8,128)S(1)}, u32[]{:S(2)}, u32[]{:S(2)}) collective-permute-start(f32[1088,128]{1,0:T(8,128)S(1)} %collective-permute-done.refs_1_), channel_id=1, source_target_pairs={{0,1},{1,0},{2,3},{3,2},{4,5},{5,4},{6,7},{7,6},{8,9},{9,8},{10,11... | collective-permute-start | bytes 1671176 | tf_op jit(solution)/shard_map/ppermute | solution.py:319
  79.7 0.0 collective-permute-done.1.refs_2_
  79.7 2.4 %collective-permute-start.5 = (f32[1088,128]{1,0:T(8,128)S(1)}, f32[1088,128]{1,0:T(8,128)S(1)}, u32[]{:S(2)}, u32[]{:S(2)}) collective-permute-start(f32[1088,128]{1,0:T(8,128)S(1)} %collective-permute-done.1.refs_2_), channel_id=1, source_target_pairs={{0,1},{1,0},{2,3},{3,2},{4,5},{5,4},{6,7},{7,6},{8,9},{9,8},{10,11... | collective-permute-start | bytes 1671176 | tf_op jit(solution)/shard_map/ppermute | solution.py:319
  82.1 1.2 collective-permute-done.2.refs_3_
  83.4 1.9 %collective-permute-start.6 = (f32[1088,128]{1,0:T(8,128)S(1)}, f32[1088,128]{1,0:T(8,128)}, u32[]{:S(2)}, u32[]{:S(2)}) collective-permute-start(f32[1088,128]{1,0:T(8,128)S(1)} %collective-permute-done.2.refs_3_), channel_id=1, source_target_pairs={{0,1},{1,0},{2,3},{3,2},{4,5},{5,4},{6,7},{7,6},{8,9},{9,8},{10,11... | collective-permute-start | bytes 1671176 | tf_op jit(solution)/shard_map/ppermute | solution.py:319
  85.3 0.0 collective-permute-done.3.refs_4_
  85.4 0.0 copy-start.1
  85.4 0.0 collective-permute-done.4.refs_5_
  85.4 0.0 copy-start.3
  85.4 0.0 collective-permute-done.5.refs_6_
  85.4 0.8 copy-done.3
  86.2 0.0 copy-start.4
  86.2 0.8 copy-done.4
  87.0 0.3 collective-permute-done.6.refs_7_
  87.4 11.6 %all-to-all-done.2.recv_ref = f32[32,22,1,128]{3,2,1,0:T(1,128)S(1)} async-done(((f32[32,22,1,128]{3,2,1,0:T(1,128)}), f32[32,22,1,128]{3,2,1,0:T(1,128)S(1)}, u32[]{:S(2)}, u32[]{:S(2)}) %all-to-all-start.2) | async-done | bytes 360480 | tf_op jit(solution)/shard_map/all_to_all | solution.py:323
  99.0 0.0 copy-done.5
  99.0 4.8 %evaluate.3 = f32[224,4,128]{2,1,0:T(4,128)} custom-call(f32[32,22,1,128]{3,2,1,0:T(1,128)S(1)} %all-to-all-done.2.recv_ref, f32[5,8,8,128]{3,2,1,0:T(8,128)S(1)} %copy-done.5, f32[1088,128]{1,0:T(8,128)S(1)} %select_maximum_fusion.refs_0_, f32[1088,128]{1,0:T(8,128)S(1)} %collective-permute-done.refs_1_, f32[1088,128]{1,0:T(8,128)S(1)} %collective-permute-done.1.refs_2_, ...), custom_call_target="tpu_custom_call" | custom-call | tf_op jit(solution)/shard_map/evaluate/pallas_call | solution.py:263
  103.8 0.0 copy-done.1
  103.8 10.0 %all-to-all-start.3 = ((f32[32,7,4,128]{3,2,1,0:T(4,128)}), f32[32,7,4,128]{3,2,1,0:T(4,128)S(1)}, u32[]{:S(2)}, u32[]{:S(2)}) async-start(f32[32,7,4,128]{3,2,1,0:T(4,128)} %bitcast.8), calls=%async_computation.3 | async-start | bytes 917504 | tf_op jit(solution)/shard_map/all_to_all | solution.py:323
  113.9 0.7 slice_reduce_fusion
  115.2 57.9 %all-to-all-done.3 = f32[32,7,4,128]{3,2,1,0:T(4,128)S(1)} async-done(((f32[32,7,4,128]{3,2,1,0:T(4,128)}), f32[32,7,4,128]{3,2,1,0:T(4,128)S(1)}, u32[]{:S(2)}, u32[]{:S(2)}) %all-to-all-start.3) | async-done | bytes 458784 | tf_op jit(solution)/shard_map/all_to_all | solution.py:323
  173.1 0.0 copy-start.8
  173.1 0.6 unpack.3
  173.7 0.2 copy-done.8
  173.9 0.0 copy-start.7
  173.9 0.6 copy-done.7
  (2 shorter events, 0.0 us)
Async XLA Ops:
  0.0 48.6 %copy-start = (f32[24,64]{1,0:T(8,128)S(1)}, f32[24,64]{1,0:T(8,128)}, u32[]{:S(2)}) copy-start(f32[24,64]{1,0:T(8,128)} %param.11) | copy-start | bytes 18436
  0.0 0.7 copy-start.10
  0.0 48.8 %copy-start.6 = (f32[64,4,512]{2,1,0:T(4,128)S(1)}, f32[64,4,512]{2,1,0:T(4,128)}, u32[]{:S(2)}) copy-start(f32[64,4,512]{2,1,0:T(4,128)} %param.10) | copy-start | bytes 1572868
  2.8 45.8 %copy-start.9 = (f32[24,24]{1,0:T(8,128)S(1)}, f32[24,24]{1,0:T(8,128)}, u32[]{:S(2)}) copy-start(f32[24,24]{1,0:T(8,128)} %constant.13.clone) | copy-start | bytes 6916
  2.8 45.8 %copy-start.11 = (f32[24]{0:T(128)S(1)}, f32[24]{0:T(128)}, u32[]{:S(2)}) copy-start(f32[24]{0:T(128)} %constant.21) | copy-start | bytes 292
  2.8 96.2 %all-to-all-start.2 = ((f32[32,22,1,128]{3,2,1,0:T(1,128)}), f32[32,22,1,128]{3,2,1,0:T(1,128)S(1)}, u32[]{:S(2)}, u32[]{:S(2)}) async-start(f32[32,22,1,128]{3,2,1,0:T(1,128)} %get-tuple-element.49), calls=%async_computation.2 | async-start | bytes 720896 | tf_op jit(solution)/shard_map/all_to_all | solution.py:323
  48.8 50.2 %copy-start.5 = (f32[5,8,8,128]{3,2,1,0:T(8,128)S(1)}, f32[5,8,8,128]{3,2,1,0:T(8,128)}, u32[]{:S(2)}) copy-start(f32[5,8,8,128]{3,2,1,0:T(8,128)} %constant.15.clone.const_ref) | copy-start | bytes 491524
  48.9 28.8 %collective-permute-start = (f32[1088,128]{1,0:T(8,128)S(1)}, f32[1088,128]{1,0:T(8,128)S(1)}, u32[]{:S(2)}, u32[]{:S(2)}) collective-permute-start(f32[1088,128]{1,0:T(8,128)S(1)} %select_maximum_fusion.refs_0_), channel_id=1, source_target_pairs={{0,6},{2,0},{4,2},{6,4},{1,7},{3,1},{5,3},{7,5},{8,14},{10,8},{12,... | collective-permute-start | bytes 1671176 | tf_op jit(solution)/shard_map/ppermute | solution.py:316
  54.1 25.5 %collective-permute-start.1 = (f32[1088,128]{1,0:T(8,128)S(1)}, f32[1088,128]{1,0:T(8,128)S(1)}, u32[]{:S(2)}, u32[]{:S(2)}) collective-permute-start(f32[1088,128]{1,0:T(8,128)S(1)} %select_maximum_fusion.refs_0_), channel_id=1, source_target_pairs={{0,4},{2,6},{4,0},{6,2},{1,5},{3,7},{5,1},{7,3},{8,12},{10,14},{12... | collective-permute-start | bytes 1671176 | tf_op jit(solution)/shard_map/ppermute | solution.py:316
  56.6 26.8 %collective-permute-start.2 = (f32[1088,128]{1,0:T(8,128)S(1)}, f32[1088,128]{1,0:T(8,128)S(1)}, u32[]{:S(2)}, u32[]{:S(2)}) collective-permute-start(f32[1088,128]{1,0:T(8,128)S(1)} %select_maximum_fusion.refs_0_), channel_id=1, source_target_pairs={{0,2},{2,4},{4,6},{6,0},{1,3},{3,5},{5,7},{7,1},{8,10},{10,12},{12... | collective-permute-start | bytes 1671176 | tf_op jit(solution)/shard_map/ppermute | solution.py:316
  59.6 25.8 %collective-permute-start.3 = (f32[1088,128]{1,0:T(8,128)S(1)}, f32[1088,128]{1,0:T(8,128)S(1)}, u32[]{:S(2)}, u32[]{:S(2)}) collective-permute-start(f32[1088,128]{1,0:T(8,128)S(1)} %select_maximum_fusion.refs_0_), channel_id=1, source_target_pairs={{0,1},{1,0},{2,3},{3,2},{4,5},{5,4},{6,7},{7,6},{8,9},{9,8},{10,11... | collective-permute-start | bytes 1671176 | tf_op jit(solution)/shard_map/ppermute | solution.py:319
  77.7 7.6 %collective-permute-start.4 = (f32[1088,128]{1,0:T(8,128)S(1)}, f32[1088,128]{1,0:T(8,128)S(1)}, u32[]{:S(2)}, u32[]{:S(2)}) collective-permute-start(f32[1088,128]{1,0:T(8,128)S(1)} %collective-permute-done.refs_1_), channel_id=1, source_target_pairs={{0,1},{1,0},{2,3},{3,2},{4,5},{5,4},{6,7},{7,6},{8,9},{9,8},{10,11... | collective-permute-start | bytes 1671176 | tf_op jit(solution)/shard_map/ppermute | solution.py:319
  79.7 5.7 %collective-permute-start.5 = (f32[1088,128]{1,0:T(8,128)S(1)}, f32[1088,128]{1,0:T(8,128)S(1)}, u32[]{:S(2)}, u32[]{:S(2)}) collective-permute-start(f32[1088,128]{1,0:T(8,128)S(1)} %collective-permute-done.1.refs_2_), channel_id=1, source_target_pairs={{0,1},{1,0},{2,3},{3,2},{4,5},{5,4},{6,7},{7,6},{8,9},{9,8},{10,11... | collective-permute-start | bytes 1671176 | tf_op jit(solution)/shard_map/ppermute | solution.py:319
  83.4 4.0 %collective-permute-start.6 = (f32[1088,128]{1,0:T(8,128)S(1)}, f32[1088,128]{1,0:T(8,128)}, u32[]{:S(2)}, u32[]{:S(2)}) collective-permute-start(f32[1088,128]{1,0:T(8,128)S(1)} %collective-permute-done.2.refs_3_), channel_id=1, source_target_pairs={{0,1},{1,0},{2,3},{3,2},{4,5},{5,4},{6,7},{7,6},{8,9},{9,8},{10,11... | collective-permute-start | bytes 1671176 | tf_op jit(solution)/shard_map/ppermute | solution.py:319
  85.4 18.5 %copy-start.1 = (f32[1088,128]{1,0:T(8,128)}, f32[1088,128]{1,0:T(8,128)S(1)}, u32[]{:S(2)}) copy-start(f32[1088,128]{1,0:T(8,128)S(1)} %collective-permute-done.3.refs_4_) | copy-start | bytes 1671172
  85.4 0.9 copy-start.3
  86.2 0.8 copy-start.4
  103.8 69.2 %all-to-all-start.3 = ((f32[32,7,4,128]{3,2,1,0:T(4,128)}), f32[32,7,4,128]{3,2,1,0:T(4,128)S(1)}, u32[]{:S(2)}, u32[]{:S(2)}) async-start(f32[32,7,4,128]{3,2,1,0:T(4,128)} %bitcast.8), calls=%async_computation.3 | async-start | bytes 917504 | tf_op jit(solution)/shard_map/all_to_all | solution.py:323
  173.1 0.8 copy-start.8
  173.9 0.6 copy-start.7

commit v3 on v2

--- a/solution.py
+++ b/solution.py
@@ -45,19 +45,10 @@
 
 def lagrange_constants():
     nodes = np.array(GLL_POINTS, np.float64)
-    plain = [0, 1, 2, 3, 4, 5, 6, 7]
-    orders = [plain] + [[i] * 4 + [i + 2] * 4 for i in (0, 4, 1, 5)]
-    blocks = []
-    for order in orders:
-        for k in range(7):
-            blocks.append([nodes[[m for m in range(8) if m != i][k]] for i in order])
-        factor = []
-        for i in order:
-            others = [nodes[i] - nodes[m] for m in range(8) if m != i]
-            factor.append(1.0 / np.prod(others))
-        blocks.append(factor)
-    table = np.array(blocks, np.float32).reshape(len(orders), 8, 8)
-    return np.repeat(table[..., None], LANES, axis=-1)
+    others = [[nodes[m] for m in range(8) if m != n] for n in range(8)]
+    factor = [1.0 / np.prod([nodes[n] - other for other in others[n]]) for n in range(8)]
+    table = np.concatenate([np.array(others).T, np.array(factor)[None]], axis=0)
+    return np.repeat(table.astype(np.float32)[..., None], LANES, axis=-1)
 
 
 def divided(value, by):
@@ -184,22 +175,33 @@
     return high, (value - high.astype(jnp.float32)).astype(jnp.bfloat16)
 
 
-def evaluate_kernel(elems, slots, recv_ref, const_ref, *refs):
-    pieces, (out_ref, fields, shapes, points, coefs, meta, live, sems) = refs[:8], refs[8:]
+def segments(elems, lengths):
+    size, found, piece, row = elems * 16, [], 0, 0
+    for index, length in enumerate(lengths):
+        here = 0
+        while here < length:
+            end = size if row < size else size + elems
+            count = min(length - here, end - row)
+            base = piece * size + row if row < size else piece * elems + row - size
+            found.append((index, here, count, row >= size, base))
+            here, row = here + count, row + count
+            if row == size + elems:
+                piece, row = piece + 1, 0
+    return found
+
+
+def evaluate_kernel(elems, slots, arrays, recv_ref, const_ref, *refs):
+    pieces, (out_ref, fields, shapes, points, coefs, meta, live, sems) = refs[:arrays], refs[arrays:]
     senders = recv_ref.shape[0]
     ids = pltpu.make_async_copy(recv_ref.at[:, 3 * slots, 0, :], meta, sems.at[0])
     ids.start()
     copies = []
-    for k, piece in enumerate(pieces):
-        size = elems * 16
-        copies += [
-            pltpu.make_async_copy(
-                piece.at[pl.ds(0, size)], fields.at[pl.ds(k * size, size)], sems.at[2 * k + 1]
-            ),
-            pltpu.make_async_copy(
-                piece.at[pl.ds(size, elems)], shapes.at[pl.ds(k * elems, elems)], sems.at[2 * k + 2]
-            ),
-        ]
+    for n, (index, row, count, of_coefs, there) in enumerate(
+        segments(elems, [piece.shape[0] for piece in pieces])
+    ):
+        target = (shapes if of_coefs else fields).at[pl.ds(there, count)]
+        source = pieces[index].at[pl.ds(row, count)]
+        copies.append(pltpu.make_async_copy(source, target, sems.at[n + 1]))
     for copy in copies:
         copy.start()
     ids.wait()
@@ -219,24 +221,29 @@
         copy.wait()
 
     lane = lax.broadcasted_iota(jnp.int32, (16, LANES), 1)
-
-    def group(g, carry):
+    upper = lax.broadcasted_iota(jnp.int32, (8, LANES), 0) < 4
+
+    def gather(g):
         where = []
         for u in range(8):
-            s, k = divided(live[jnp.minimum(g * 8 + u, total - 1)], ID_LANES)
+            s, k = divided(live[jnp.clip(g * 8 + u, 0, jnp.maximum(total - 1, 0))], ID_LANES)
             code = meta[s, k].astype(jnp.int32)
-            where.append((s * slots + k, code * 16))
+            where += [s * slots + k, code * 16]
             for a in range(3):
                 points[a, pl.ds(u, 1), :] = recv_ref[s, k * 3 + a]
             coefs[pl.ds(u, 1), :] = shapes[pl.ds(code, 1), :]
-        all_coefs = coefs[...]
+        return tuple(where) + (points[0], points[1], points[2], coefs[...])
+
+    def group(g, held):
+        where, target, all_coefs = held[:16], held[16:19], held[19]
+        following = gather(g + 1)
         coef = [jnp.broadcast_to(all_coefs[:, m : m + 1], (8, LANES)) for m in range(24)]
-        pos = newton(coef, [points[a] for a in range(3)])
+        pos = newton(coef, target)
         for u in range(8):
-            slot, start = where[u]
-            rows = [jnp.broadcast_to(p[u : u + 1], (8, LANES)) for p in pos]
-            along_y = lagrange(rows[1], const_ref[0])
-            along_z = lagrange(rows[2], const_ref[0])
+            slot, start = where[2 * u : 2 * u + 2]
+            along_x, along_y, along_z = [
+                lagrange(jnp.broadcast_to(p[u : u + 1], (8, LANES)), const_ref) for p in pos
+            ]
             weights = jnp.concatenate(
                 [jnp.broadcast_to(along_y[j : j + 1], (8, LANES)) * along_z for j in range(8)], axis=0
             )
@@ -248,23 +255,26 @@
             both = jnp.concatenate(halves(jnp.concatenate([even, odd], axis=0)), axis=0)
             sums = jnp.dot(both, weights, preferred_element_type=jnp.float32)
             total_x = None
-            for q in range(4):
+            for q, i in enumerate((0, 4, 1, 5)):
                 term = sums[8 * q : 8 * q + 8] + sums[32 + 8 * q : 40 + 8 * q]
-                term = term * lagrange(rows[0], const_ref[1 + q])
+                rows = [jnp.broadcast_to(along_x[r : r + 1], (8, LANES)) for r in (i, i + 2)]
+                term = term * jnp.where(upper, rows[0], rows[1])
                 total_x = term if total_x is None else total_x + term
             out_ref[slot] = total_x[0:4] + total_x[4:8]
-        return carry
-
-    lax.fori_loop(0, (total + 7) // 8, group, 0)
+        return following
+
+    @pl.when(total > 0)
+    def _():
+        lax.fori_loop(0, (total + 7) // 8, group, gather(jnp.int32(0)))
 
 
 def evaluate(recv, pieces, slots, elems):
     senders = recv.shape[0]
     return pl.pallas_call(
-        functools.partial(evaluate_kernel, elems, slots),
+        functools.partial(evaluate_kernel, elems, slots, len(pieces)),
         out_shape=jax.ShapeDtypeStruct((senders * slots, 4, LANES), jnp.float32),
         in_specs=[pl.BlockSpec(memory_space=pltpu.VMEM)] * 2
-        + [pl.BlockSpec(memory_space=pl.ANY)] * 8,
+        + [pl.BlockSpec(memory_space=pl.ANY)] * len(pieces),
         out_specs=pl.BlockSpec(memory_space=pltpu.VMEM),
         scratch_shapes=[
             pltpu.VMEM((8 * elems * 16, LANES), jnp.float32),
@@ -273,7 +283,7 @@
             pltpu.VMEM((8, LANES), jnp.float32),
             pltpu.SMEM((senders, LANES), jnp.float32),
             pltpu.SMEM((senders * ID_LANES,), jnp.int32),
-            pltpu.SemaphoreType.DMA((17,)),
+            pltpu.SemaphoreType.DMA((1 + len(segments(elems, [p.shape[0] for p in pieces])),)),
         ],
         compiler_params=pltpu.CompilerParams(vmem_limit_bytes=12 << 20),
         name="evaluate",
@@ -311,11 +321,15 @@
     fields = old_fields.reshape(elems, 4, 4, LANES).transpose(0, 2, 1, 3).reshape(-1, LANES)
     own = jnp.concatenate([fields, coefs], axis=0)
     segs = lax.axis_size("seg")
-
-    def along(step):
-        return lax.ppermute(own, "seg", [(i, (i + step) % segs) for i in range(segs)])
-
-    half = [own] + [along(segs - apart) for apart in range(1, segs)]
+    middle = own.shape[0] // 16 * 8
+
+    def along(array, step):
+        return lax.ppermute(array, "seg", [(i, (i + step) % segs) for i in range(segs)])
+
+    before = along(own, 1)
+    after = along(own, segs - 1)
+    opposite = [along(own[:middle], 2), along(before[middle:], 1)]
+    half = [own, after, *opposite, before]
     return half + [lax.ppermute(piece, "sub", [(0, 1), (1, 0)]) for piece in half]
 
 

time: 177 us -> 173 us (0.977)
  waiting for transfers between devices: 87.3 us -> 81.9 us
  starting transfers between devices: 74.7 us -> 78.4 us
    ppermute x3 -> x4, waiting for transfers between devices: 17.4 us -> 8.23 us  [along(): lax.ppermute(array, 'seg', [(i, (i + step) % segs) for i in range(segs)])]
    ppermute x3 -> x4, starting transfers between devices: 10.7 us -> 14.4 us  [along(): lax.ppermute(array, 'seg', [(i, (i + step) % segs) for i in range(segs)])]
    all_to_all x2, waiting for transfers between devices: 69.5 us -> 72.6 us  [all_to_all(): lax.all_to_all(array, 'block', split_axis=0, concat_axis=0, tiled=True)]
    all_to_all x2, starting transfers between devices: 55.8 us -> 53.2 us  [all_to_all(): lax.all_to_all(array, 'block', split_axis=0, concat_axis=0, tiled=True)]
    ppermute x4 -> x5, starting transfers between devices: 8.27 us -> 10.7 us  [row_pieces(): lax.ppermute(piece, 'sub', [(0, 1), (1, 0)])]
  transfers between devices with their start and end apart: 9 -> 11, of which waited for: 5 -> 5; matrix products, arithmetic and copies ran while one was open for 1% -> 1% of each run, Pallas kernels for 0% -> 0%
where the time goes in v3:
time: 173 us; the launch traced here: 171 us
  waiting for transfers between devices  81.9 us (47%)
  starting transfers between devices  78.4 us (45%)
  Pallas kernels  6.45 us (4%)
  local copies, waits for them, and re-layouts  2.32 us (1%)
    all_to_all x2, waiting for transfers between devices, all_to_all(): lax.all_to_all(array, 'block', split_axis=0, concat_axis=0, tiled=True)  72.6 us
    all_to_all x2, starting transfers between devices, all_to_all(): lax.all_to_all(array, 'block', split_axis=0, concat_axis=0, tiled=True)  53.2 us
    ppermute x4, starting transfers between devices, along(): lax.ppermute(array, 'seg', [(i, (i + step) % segs) for i in range(segs)])  14.4 us
    ppermute x5, starting transfers between devices, row_pieces(): lax.ppermute(piece, 'sub', [(0, 1), (1, 0)])  10.7 us
    ppermute x4, waiting for transfers between devices, along(): lax.ppermute(array, 'seg', [(i, (i + step) % segs) for i in range(segs)])  8.23 us
    pallas_call x1, Pallas kernels, evaluate(): pl.pallas_call(functools.partial(evaluate_kernel, elems, slots, len(piece...  3.79 us
  transfers between devices with their start and end apart: 11, of which 5 were waited for; matrix products, arithmetic and copies ran while one was open for 1% of the time, Pallas kernels for 0%

profile of v3, /device:TPU:40, one launch (start us, length us, event | category | flops | bytes accessed | tf_op | source)
XLA Modules:
  0.0 171.0 jit_solution(9926185598786909328)
XLA Ops:
  0.0 0.0 copy-start
  0.0 0.0 copy-start.13
  0.0 0.7 copy-done.13
  0.7 2.1 %pack.3 = (f32[32,22,1,128]{3,2,1,0:T(1,128)}, s32[32]{0:T(128)S(1)}) custom-call(s32[32]{0:T(128)S(1)} %copy-done.13, f32[32,3,128]{2,1,0:T(4,128)} %bitcast.25), custom_call_target="tpu_custom_call" | custom-call | tf_op jit(solution)/shard_map/pack/pallas_call | solution.py:106
  2.8 0.0 copy-start.12
  2.8 0.0 copy-start.14
  2.8 45.8 %all-to-all-start.2 = ((f32[32,22,1,128]{3,2,1,0:T(1,128)}), f32[32,22,1,128]{3,2,1,0:T(1,128)S(1)}, u32[]{:S(2)}, u32[]{:S(2)}) async-start(f32[32,22,1,128]{3,2,1,0:T(1,128)} %get-tuple-element.55), calls=%async_computation.2 | async-start | bytes 720896 | tf_op jit(solution)/shard_map/all_to_all | solution.py:337
  48.6 0.0 copy-done
  48.6 0.0 copy-done.12
  48.6 0.0 copy-done.14
  48.6 0.2 fusion
  48.8 0.0 copy-done.3
  48.9 3.6 %collective-permute-start.2 = (f32[1088,128]{1,0:T(8,128)S(1)}, f32[1088,128]{1,0:T(8,128)S(1)}, u32[]{:S(2)}, u32[]{:S(2)}) collective-permute-start(f32[1088,128]{1,0:T(8,128)S(1)} %select_maximum_fusion.refs_0_), channel_id=1, source_target_pairs={{0,2},{2,4},{4,6},{6,0},{1,3},{3,5},{5,7},{7,1},{8,10},{10,12},{12... | collective-permute-start | bytes 1671176 | tf_op jit(solution)/shard_map/ppermute | solution.py:327
  52.5 3.5 %collective-permute-start = (f32[1088,128]{1,0:T(8,128)S(1)}, f32[1088,128]{1,0:T(8,128)S(1)}, u32[]{:S(2)}, u32[]{:S(2)}) collective-permute-start(f32[1088,128]{1,0:T(8,128)S(1)} %select_maximum_fusion.refs_0_), channel_id=1, source_target_pairs={{0,6},{2,0},{4,2},{6,4},{1,7},{3,1},{5,3},{7,5},{8,14},{10,8},{12,... | collective-permute-start | bytes 1671176 | tf_op jit(solution)/shard_map/ppermute | solution.py:327
  56.0 2.0 %collective-permute-start.4 = (f32[1088,128]{1,0:T(8,128)S(1)}, f32[1088,128]{1,0:T(8,128)S(1)}, u32[]{:S(2)}, u32[]{:S(2)}) collective-permute-start(f32[1088,128]{1,0:T(8,128)S(1)} %select_maximum_fusion.refs_0_), channel_id=1, source_target_pairs={{0,1},{1,0},{2,3},{3,2},{4,5},{5,4},{6,7},{7,6},{8,9},{9,8},{10,11... | collective-permute-start | bytes 1671176 | tf_op jit(solution)/shard_map/ppermute | solution.py:333
  58.0 0.0 copy-start.11
  58.0 4.0 %collective-permute-start.1 = (f32[544,128]{1,0:T(8,128)S(1)}, f32[544,128]{1,0:T(8,128)S(1)}, u32[]{:S(2)}, u32[]{:S(2)}) collective-permute-start(f32[544,128]{1,0:T(8,128)S(1)} %bitcast.24), channel_id=1, source_target_pairs={{0,4},{2,6},{4,0},{6,2},{1,5},{3,7},{5,1},{7,3},{8,12},{10,14},{12... | collective-permute-start | bytes 835592 | tf_op jit(solution)/shard_map/ppermute | solution.py:327
  62.1 4.5 %collective-permute-done.2.refs_4_ = f32[1088,128]{1,0:T(8,128)S(1)} collective-permute-done((f32[1088,128]{1,0:T(8,128)S(1)}, f32[1088,128]{1,0:T(8,128)S(1)}, u32[]{:S(2)}, u32[]{:S(2)}) %collective-permute-start.2) | collective-permute-done | bytes 557088 | tf_op jit(solution)/shard_map/ppermute | solution.py:327
  66.6 3.3 %collective-permute-start.3 = (f32[544,128]{1,0:T(8,128)S(1)}, f32[544,128]{1,0:T(8,128)S(1)}, u32[]{:S(2)}, u32[]{:S(2)}) collective-permute-start(f32[544,128]{1,0:T(8,128)S(1)} %slice.18), channel_id=1, source_target_pairs={{0,2},{2,4},{4,6},{6,0},{1,3},{3,5},{5,7},{7,1},{8,10},{10,12},{12... | collective-permute-start | bytes 835592 | tf_op jit(solution)/shard_map/ppermute | solution.py:327
  69.9 3.7 %collective-permute-done.refs_1_ = f32[1088,128]{1,0:T(8,128)S(1)} collective-permute-done((f32[1088,128]{1,0:T(8,128)S(1)}, f32[1088,128]{1,0:T(8,128)S(1)}, u32[]{:S(2)}, u32[]{:S(2)}) %collective-permute-start) | collective-permute-done | bytes 557088 | tf_op jit(solution)/shard_map/ppermute | solution.py:327
  73.6 1.9 %collective-permute-start.5 = (f32[1088,128]{1,0:T(8,128)S(1)}, f32[1088,128]{1,0:T(8,128)S(1)}, u32[]{:S(2)}, u32[]{:S(2)}) collective-permute-start(f32[1088,128]{1,0:T(8,128)S(1)} %collective-permute-done.refs_1_), channel_id=1, source_target_pairs={{0,1},{1,0},{2,3},{3,2},{4,5},{5,4},{6,7},{7,6},{8,9},{9,8},{10,11... | collective-permute-start | bytes 1671176 | tf_op jit(solution)/shard_map/ppermute | solution.py:333
  75.6 2.4 %collective-permute-start.8 = (f32[1088,128]{1,0:T(8,128)S(1)}, f32[1088,128]{1,0:T(8,128)}, u32[]{:S(2)}, u32[]{:S(2)}) collective-permute-start(f32[1088,128]{1,0:T(8,128)S(1)} %collective-permute-done.2.refs_4_), channel_id=1, source_target_pairs={{0,1},{1,0},{2,3},{3,2},{4,5},{5,4},{6,7},{7,6},{8,9},{9,8},{10,11... | collective-permute-start | bytes 1671176 | tf_op jit(solution)/shard_map/ppermute | solution.py:333
  78.0 0.0 collective-permute-done.1.refs_2_
  78.0 2.0 %collective-permute-start.6 = (f32[544,128]{1,0:T(8,128)S(1)}, f32[544,128]{1,0:T(8,128)S(1)}, u32[]{:S(2)}, u32[]{:S(2)}) collective-permute-start(f32[544,128]{1,0:T(8,128)S(1)} %collective-permute-done.1.refs_2_), channel_id=1, source_target_pairs={{0,1},{1,0},{2,3},{3,2},{4,5},{5,4},{6,7},{7,6},{8,9},{9,8},{10,11... | collective-permute-start | bytes 835592 | tf_op jit(solution)/shard_map/ppermute | solution.py:333
  80.0 0.0 collective-permute-done.3.refs_3_
  80.0 0.0 copy-start.4
  80.0 2.4 %collective-permute-start.7 = (f32[544,128]{1,0:T(8,128)S(1)}, f32[544,128]{1,0:T(8,128)S(1)}, u32[]{:S(2)}, u32[]{:S(2)}) collective-permute-start(f32[544,128]{1,0:T(8,128)S(1)} %collective-permute-done.3.refs_3_), channel_id=1, source_target_pairs={{0,1},{1,0},{2,3},{3,2},{4,5},{5,4},{6,7},{7,6},{8,9},{9,8},{10,11... | collective-permute-start | bytes 835592 | tf_op jit(solution)/shard_map/ppermute | solution.py:333
  82.5 0.0 collective-permute-done.4.refs_5_
  82.5 0.0 collective-permute-done.6.refs_7_
  82.5 0.0 copy-start.6
  82.5 0.0 collective-permute-done.5.refs_6_
  82.5 0.0 copy-start.1
  82.5 1.1 collective-permute-done.7.refs_8_
  83.6 0.0 copy-done.4
  83.6 0.0 copy-done.6
  83.6 0.7 copy-done.8
  84.3 0.0 collective-permute-done.8.refs_9_
  84.3 14.7 %all-to-all-done.2.recv_ref = f32[32,22,1,128]{3,2,1,0:T(1,128)S(1)} async-done(((f32[32,22,1,128]{3,2,1,0:T(1,128)}), f32[32,22,1,128]{3,2,1,0:T(1,128)S(1)}, u32[]{:S(2)}, u32[]{:S(2)}) %all-to-all-start.2) | async-done | bytes 360480 | tf_op jit(solution)/shard_map/all_to_all | solution.py:337
  99.0 0.0 copy-done.11
  99.0 3.8 %evaluate.3 = f32[224,4,128]{2,1,0:T(4,128)} custom-call(f32[32,22,1,128]{3,2,1,0:T(1,128)S(1)} %all-to-all-done.2.recv_ref, f32[8,8,128]{2,1,0:T(8,128)S(1)} %copy-done.11, f32[1088,128]{1,0:T(8,128)S(1)} %select_maximum_fusion.refs_0_, f32[1088,128]{1,0:T(8,128)S(1)} %collective-permute-done.refs_1_, f32[544,128]{1,0:T(8,128)S(1)} %collective-permute-done.1.refs_2_, ...), custom_call_target="tpu_custom_call" | custom-call | tf_op jit(solution)/shard_map/evaluate/pallas_call | solution.py:273
  102.8 0.0 copy-done.1
  102.8 7.5 %all-to-all-start.3 = ((f32[32,7,4,128]{3,2,1,0:T(4,128)}), f32[32,7,4,128]{3,2,1,0:T(4,128)S(1)}, u32[]{:S(2)}, u32[]{:S(2)}) async-start(f32[32,7,4,128]{3,2,1,0:T(4,128)} %bitcast.10), calls=%async_computation.3 | async-start | bytes 917504 | tf_op jit(solution)/shard_map/all_to_all | solution.py:337
  110.3 0.7 slice_reduce_fusion
  111.7 57.9 %all-to-all-done.3 = f32[32,7,4,128]{3,2,1,0:T(4,128)S(1)} async-done(((f32[32,7,4,128]{3,2,1,0:T(4,128)}), f32[32,7,4,128]{3,2,1,0:T(4,128)S(1)}, u32[]{:S(2)}, u32[]{:S(2)}) %all-to-all-start.3) | async-done | bytes 458784 | tf_op jit(solution)/shard_map/all_to_all | solution.py:337
  169.6 0.6 unpack.3
  170.2 0.0 copy-done.5
  170.2 0.2 copy-done.10
  170.4 0.6 copy-done.9
  (9 shorter events, 0.1 us)
Async XLA Ops:
  0.0 48.6 %copy-start = (f32[24,64]{1,0:T(8,128)S(1)}, f32[24,64]{1,0:T(8,128)}, u32[]{:S(2)}) copy-start(f32[24,64]{1,0:T(8,128)} %param.11) | copy-start | bytes 18436
  0.0 0.7 copy-start.13
  0.0 48.8 %copy-start.3 = (f32[64,4,512]{2,1,0:T(4,128)S(1)}, f32[64,4,512]{2,1,0:T(4,128)}, u32[]{:S(2)}) copy-start(f32[64,4,512]{2,1,0:T(4,128)} %param.10) | copy-start | bytes 1572868
  2.8 45.8 %copy-start.12 = (f32[24,24]{1,0:T(8,128)S(1)}, f32[24,24]{1,0:T(8,128)}, u32[]{:S(2)}) copy-start(f32[24,24]{1,0:T(8,128)} %constant.13.clone) | copy-start | bytes 6916
  2.8 45.8 %copy-start.14 = (f32[24]{0:T(128)S(1)}, f32[24]{0:T(128)}, u32[]{:S(2)}) copy-start(f32[24]{0:T(128)} %constant.21) | copy-start | bytes 292
  2.8 96.2 %all-to-all-start.2 = ((f32[32,22,1,128]{3,2,1,0:T(1,128)}), f32[32,22,1,128]{3,2,1,0:T(1,128)S(1)}, u32[]{:S(2)}, u32[]{:S(2)}) async-start(f32[32,22,1,128]{3,2,1,0:T(1,128)} %get-tuple-element.55), calls=%async_computation.2 | async-start | bytes 720896 | tf_op jit(solution)/shard_map/all_to_all | solution.py:337
  48.9 17.7 %collective-permute-start.2 = (f32[1088,128]{1,0:T(8,128)S(1)}, f32[1088,128]{1,0:T(8,128)S(1)}, u32[]{:S(2)}, u32[]{:S(2)}) collective-permute-start(f32[1088,128]{1,0:T(8,128)S(1)} %select_maximum_fusion.refs_0_), channel_id=1, source_target_pairs={{0,2},{2,4},{4,6},{6,0},{1,3},{3,5},{5,7},{7,1},{8,10},{10,12},{12... | collective-permute-start | bytes 1671176 | tf_op jit(solution)/shard_map/ppermute | solution.py:327
  52.5 21.2 %collective-permute-start = (f32[1088,128]{1,0:T(8,128)S(1)}, f32[1088,128]{1,0:T(8,128)S(1)}, u32[]{:S(2)}, u32[]{:S(2)}) collective-permute-start(f32[1088,128]{1,0:T(8,128)S(1)} %select_maximum_fusion.refs_0_), channel_id=1, source_target_pairs={{0,6},{2,0},{4,2},{6,4},{1,7},{3,1},{5,3},{7,5},{8,14},{10,8},{12,... | collective-permute-start | bytes 1671176 | tf_op jit(solution)/shard_map/ppermute | solution.py:327
  56.0 26.4 %collective-permute-start.4 = (f32[1088,128]{1,0:T(8,128)S(1)}, f32[1088,128]{1,0:T(8,128)S(1)}, u32[]{:S(2)}, u32[]{:S(2)}) collective-permute-start(f32[1088,128]{1,0:T(8,128)S(1)} %select_maximum_fusion.refs_0_), channel_id=1, source_target_pairs={{0,1},{1,0},{2,3},{3,2},{4,5},{5,4},{6,7},{7,6},{8,9},{9,8},{10,11... | collective-permute-start | bytes 1671176 | tf_op jit(solution)/shard_map/ppermute | solution.py:333
  58.0 41.0 %copy-start.11 = (f32[8,8,128]{2,1,0:T(8,128)S(1)}, f32[8,8,128]{2,1,0:T(8,128)}, u32[]{:S(2)}) copy-start(f32[8,8,128]{2,1,0:T(8,128)} %constant.15.clone.const_ref) | copy-start | bytes 98308
  58.0 20.0 %collective-permute-start.1 = (f32[544,128]{1,0:T(8,128)S(1)}, f32[544,128]{1,0:T(8,128)S(1)}, u32[]{:S(2)}, u32[]{:S(2)}) collective-permute-start(f32[544,128]{1,0:T(8,128)S(1)} %bitcast.24), channel_id=1, source_target_pairs={{0,4},{2,6},{4,0},{6,2},{1,5},{3,7},{5,1},{7,3},{8,12},{10,14},{12... | collective-permute-start | bytes 835592 | tf_op jit(solution)/shard_map/ppermute | solution.py:327
  66.6 13.4 %collective-permute-start.3 = (f32[544,128]{1,0:T(8,128)S(1)}, f32[544,128]{1,0:T(8,128)S(1)}, u32[]{:S(2)}, u32[]{:S(2)}) collective-permute-start(f32[544,128]{1,0:T(8,128)S(1)} %slice.18), channel_id=1, source_target_pairs={{0,2},{2,4},{4,6},{6,0},{1,3},{3,5},{5,7},{7,1},{8,10},{10,12},{12... | collective-permute-start | bytes 835592 | tf_op jit(solution)/shard_map/ppermute | solution.py:327
  73.6 8.9 %collective-permute-start.5 = (f32[1088,128]{1,0:T(8,128)S(1)}, f32[1088,128]{1,0:T(8,128)S(1)}, u32[]{:S(2)}, u32[]{:S(2)}) collective-permute-start(f32[1088,128]{1,0:T(8,128)S(1)} %collective-permute-done.refs_1_), channel_id=1, source_target_pairs={{0,1},{1,0},{2,3},{3,2},{4,5},{5,4},{6,7},{7,6},{8,9},{9,8},{10,11... | collective-permute-start | bytes 1671176 | tf_op jit(solution)/shard_map/ppermute | solution.py:333
  75.6 8.8 %collective-permute-start.8 = (f32[1088,128]{1,0:T(8,128)S(1)}, f32[1088,128]{1,0:T(8,128)}, u32[]{:S(2)}, u32[]{:S(2)}) collective-permute-start(f32[1088,128]{1,0:T(8,128)S(1)} %collective-permute-done.2.refs_4_), channel_id=1, source_target_pairs={{0,1},{1,0},{2,3},{3,2},{4,5},{5,4},{6,7},{7,6},{8,9},{9,8},{10,11... | collective-permute-start | bytes 1671176 | tf_op jit(solution)/shard_map/ppermute | solution.py:333
  78.0 4.4 %collective-permute-start.6 = (f32[544,128]{1,0:T(8,128)S(1)}, f32[544,128]{1,0:T(8,128)S(1)}, u32[]{:S(2)}, u32[]{:S(2)}) collective-permute-start(f32[544,128]{1,0:T(8,128)S(1)} %collective-permute-done.1.refs_2_), channel_id=1, source_target_pairs={{0,1},{1,0},{2,3},{3,2},{4,5},{5,4},{6,7},{7,6},{8,9},{9,8},{10,11... | collective-permute-start | bytes 835592 | tf_op jit(solution)/shard_map/ppermute | solution.py:333
  80.0 3.6 %copy-start.4 = (f32[544,128]{1,0:T(8,128)}, f32[544,128]{1,0:T(8,128)S(1)}, u32[]{:S(2)}) copy-start(f32[544,128]{1,0:T(8,128)S(1)} %collective-permute-done.3.refs_3_) | copy-start | bytes 835588
  80.0 3.6 %collective-permute-start.7 = (f32[544,128]{1,0:T(8,128)S(1)}, f32[544,128]{1,0:T(8,128)S(1)}, u32[]{:S(2)}, u32[]{:S(2)}) collective-permute-start(f32[544,128]{1,0:T(8,128)S(1)} %collective-permute-done.3.refs_3_), channel_id=1, source_target_pairs={{0,1},{1,0},{2,3},{3,2},{4,5},{5,4},{6,7},{7,6},{8,9},{9,8},{10,11... | collective-permute-start | bytes 835592 | tf_op jit(solution)/shard_map/ppermute | solution.py:333
  82.5 1.1 copy-start.6
  82.5 20.3 %copy-start.1 = (f32[1088,128]{1,0:T(8,128)}, f32[1088,128]{1,0:T(8,128)S(1)}, u32[]{:S(2)}) copy-start(f32[1088,128]{1,0:T(8,128)S(1)} %collective-permute-done.5.refs_6_) | copy-start | bytes 1671172
  83.6 0.7 copy-start.8
  102.8 66.8 %all-to-all-start.3 = ((f32[32,7,4,128]{3,2,1,0:T(4,128)}), f32[32,7,4,128]{3,2,1,0:T(4,128)S(1)}, u32[]{:S(2)}, u32[]{:S(2)}) async-start(f32[32,7,4,128]{3,2,1,0:T(4,128)} %bitcast.10), calls=%async_computation.3 | async-start | bytes 917504 | tf_op jit(solution)/shard_map/all_to_all | solution.py:337
  111.0 59.2 %copy-start.5 = (f32[544,128]{1,0:T(8,128)S(1)}, f32[544,128]{1,0:T(8,128)}, u32[]{:S(2)}) copy-start(f32[544,128]{1,0:T(8,128)} %copy-done.4) | copy-start | bytes 835588
  169.6 0.8 copy-start.10
  170.4 0.6 copy-start.9

commit v4 on v3

--- a/solution.py
+++ b/solution.py
@@ -328,7 +328,7 @@
 
     before = along(own, 1)
     after = along(own, segs - 1)
-    opposite = [along(own[:middle], 2), along(before[middle:], 1)]
+    opposite = [along(after[:middle], segs - 1), along(before[middle:], 1)]
     half = [own, after, *opposite, before]
     return half + [lax.ppermute(piece, "sub", [(0, 1), (1, 0)]) for piece in half]
 

time: 173 us -> 177 us (1.023)
  starting transfers between devices: 78.4 us -> 82.8 us
    ppermute x4, waiting for transfers between devices: 8.23 us -> 13.6 us  [along(): lax.ppermute(array, 'seg', [(i, (i + step) % segs) for i in range(segs)])]
    all_to_all x2, waiting for transfers between devices: 72.6 us -> 67.6 us  [all_to_all(): lax.all_to_all(array, 'block', split_axis=0, concat_axis=0, tiled=True)]
    all_to_all x2, starting transfers between devices: 53.2 us -> 57.9 us  [all_to_all(): lax.all_to_all(array, 'block', split_axis=0, concat_axis=0, tiled=True)]
where the time goes in v4:
time: 177 us
  starting transfers between devices  82.8 us (47%)
  waiting for transfers between devices  82.7 us (47%)
  Pallas kernels  6.82 us (4%)
  local copies, waits for them, and re-layouts  2.32 us (1%)
    all_to_all x2, waiting for transfers between devices, all_to_all(): lax.all_to_all(array, 'block', split_axis=0, concat_axis=0, tiled=True)  67.6 us
    all_to_all x2, starting transfers between devices, all_to_all(): lax.all_to_all(array, 'block', split_axis=0, concat_axis=0, tiled=True)  57.9 us
    ppermute x4, starting transfers between devices, along(): lax.ppermute(array, 'seg', [(i, (i + step) % segs) for i in range(segs)])  14.6 us
    ppermute x4, waiting for transfers between devices, along(): lax.ppermute(array, 'seg', [(i, (i + step) % segs) for i in range(segs)])  13.6 us
    ppermute x5, starting transfers between devices, row_pieces(): lax.ppermute(piece, 'sub', [(0, 1), (1, 0)])  10.2 us
    pallas_call x1, Pallas kernels, evaluate(): pl.pallas_call(functools.partial(evaluate_kernel, elems, slots, len(piece...  4.16 us
  transfers between devices with their start and end apart: 11, of which 5 were waited for; matrix products, arithmetic and copies ran while one was open for 1% of the time, Pallas kernels for 0%

profile of v4, /device:TPU:40, one launch (start us, length us, event | category | flops | bytes accessed | tf_op | source)
XLA Modules:
  0.0 176.5 jit_solution(15220924256046740773)
XLA Ops:
  0.0 0.0 copy-start
  0.0 0.0 copy-start.13
  0.0 0.0 copy-start.8
  0.0 0.7 copy-done.13
  0.7 2.1 %pack.3 = (f32[32,22,1,128]{3,2,1,0:T(1,128)}, s32[32]{0:T(128)S(1)}) custom-call(s32[32]{0:T(128)S(1)} %copy-done.13, f32[32,3,128]{2,1,0:T(4,128)} %bitcast.22), custom_call_target="tpu_custom_call" | custom-call | tf_op jit(solution)/shard_map/pack/pallas_call | solution.py:106
  2.8 0.0 copy-start.12
  2.8 0.0 copy-start.14
  2.8 45.8 %all-to-all-start.2 = ((f32[32,22,1,128]{3,2,1,0:T(1,128)}), f32[32,22,1,128]{3,2,1,0:T(1,128)S(1)}, u32[]{:S(2)}, u32[]{:S(2)}) async-start(f32[32,22,1,128]{3,2,1,0:T(1,128)} %get-tuple-element.55), calls=%async_computation.2 | async-start | bytes 720896 | tf_op jit(solution)/shard_map/all_to_all | solution.py:337
  48.6 0.0 copy-done
  48.6 0.0 copy-done.12
  48.6 0.0 copy-done.14
  48.6 0.2 fusion
  48.8 0.0 copy-done.8
  48.9 5.1 %collective-permute-start = (f32[1088,128]{1,0:T(8,128)S(1)}, f32[1088,128]{1,0:T(8,128)S(1)}, u32[]{:S(2)}, u32[]{:S(2)}) collective-permute-start(f32[1088,128]{1,0:T(8,128)S(1)} %select_maximum_fusion.refs_0_), channel_id=1, source_target_pairs={{0,6},{2,0},{4,2},{6,4},{1,7},{3,1},{5,3},{7,5},{8,14},{10,8},{12,... | collective-permute-start | bytes 1671176 | tf_op jit(solution)/shard_map/ppermute | solution.py:327
  54.0 2.0 %collective-permute-start.2 = (f32[1088,128]{1,0:T(8,128)S(1)}, f32[1088,128]{1,0:T(8,128)S(1)}, u32[]{:S(2)}, u32[]{:S(2)}) collective-permute-start(f32[1088,128]{1,0:T(8,128)S(1)} %select_maximum_fusion.refs_0_), channel_id=1, source_target_pairs={{0,2},{2,4},{4,6},{6,0},{1,3},{3,5},{5,7},{7,1},{8,10},{10,12},{12... | collective-permute-start | bytes 1671176 | tf_op jit(solution)/shard_map/ppermute | solution.py:327
  56.0 2.0 %collective-permute-start.4 = (f32[1088,128]{1,0:T(8,128)S(1)}, f32[1088,128]{1,0:T(8,128)S(1)}, u32[]{:S(2)}, u32[]{:S(2)}) collective-permute-start(f32[1088,128]{1,0:T(8,128)S(1)} %select_maximum_fusion.refs_0_), channel_id=1, source_target_pairs={{0,1},{1,0},{2,3},{3,2},{4,5},{5,4},{6,7},{7,6},{8,9},{9,8},{10,11... | collective-permute-start | bytes 1671176 | tf_op jit(solution)/shard_map/ppermute | solution.py:333
  57.9 7.7 %collective-permute-done.refs_1_ = f32[1088,128]{1,0:T(8,128)S(1)} collective-permute-done((f32[1088,128]{1,0:T(8,128)S(1)}, f32[1088,128]{1,0:T(8,128)S(1)}, u32[]{:S(2)}, u32[]{:S(2)}) %collective-permute-start) | collective-permute-done | bytes 557088 | tf_op jit(solution)/shard_map/ppermute | solution.py:327
  65.7 0.0 copy-start.11
  65.7 5.6 %collective-permute-start.1 = (f32[544,128]{1,0:T(8,128)S(1)}, f32[544,128]{1,0:T(8,128)S(1)}, u32[]{:S(2)}, u32[]{:S(2)}) collective-permute-start(f32[544,128]{1,0:T(8,128)S(1)} %slice.13), channel_id=1, source_target_pairs={{0,6},{2,0},{4,2},{6,4},{1,7},{3,1},{5,3},{7,5},{8,14},{10,8},{12,... | collective-permute-start | bytes 835592 | tf_op jit(solution)/shard_map/ppermute | solution.py:327
  71.3 2.0 %collective-permute-start.5 = (f32[1088,128]{1,0:T(8,128)S(1)}, f32[1088,128]{1,0:T(8,128)S(1)}, u32[]{:S(2)}, u32[]{:S(2)}) collective-permute-start(f32[1088,128]{1,0:T(8,128)S(1)} %collective-permute-done.refs_1_), channel_id=1, source_target_pairs={{0,1},{1,0},{2,3},{3,2},{4,5},{5,4},{6,7},{7,6},{8,9},{9,8},{10,11... | collective-permute-start | bytes 1671176 | tf_op jit(solution)/shard_map/ppermute | solution.py:333
  73.3 0.0 collective-permute-done.2.refs_4_
  73.3 2.0 %collective-permute-start.3 = (f32[544,128]{1,0:T(8,128)S(1)}, f32[544,128]{1,0:T(8,128)S(1)}, u32[]{:S(2)}, u32[]{:S(2)}) collective-permute-start(f32[544,128]{1,0:T(8,128)S(1)} %slice.14), channel_id=1, source_target_pairs={{0,2},{2,4},{4,6},{6,0},{1,3},{3,5},{5,7},{7,1},{8,10},{10,12},{12... | collective-permute-start | bytes 835592 | tf_op jit(solution)/shard_map/ppermute | solution.py:327
  75.3 2.4 %collective-permute-start.8 = (f32[1088,128]{1,0:T(8,128)S(1)}, f32[1088,128]{1,0:T(8,128)}, u32[]{:S(2)}, u32[]{:S(2)}) collective-permute-start(f32[1088,128]{1,0:T(8,128)S(1)} %collective-permute-done.2.refs_4_), channel_id=1, source_target_pairs={{0,1},{1,0},{2,3},{3,2},{4,5},{5,4},{6,7},{7,6},{8,9},{9,8},{10,11... | collective-permute-start | bytes 1671176 | tf_op jit(solution)/shard_map/ppermute | solution.py:333
  77.7 0.0 collective-permute-done.1.refs_2_
  77.8 2.0 %collective-permute-start.6 = (f32[544,128]{1,0:T(8,128)S(1)}, f32[544,128]{1,0:T(8,128)S(1)}, u32[]{:S(2)}, u32[]{:S(2)}) collective-permute-start(f32[544,128]{1,0:T(8,128)S(1)} %collective-permute-done.1.refs_2_), channel_id=1, source_target_pairs={{0,1},{1,0},{2,3},{3,2},{4,5},{5,4},{6,7},{7,6},{8,9},{9,8},{10,11... | collective-permute-start | bytes 835592 | tf_op jit(solution)/shard_map/ppermute | solution.py:333
  79.7 5.8 %collective-permute-done.3.refs_3_ = f32[544,128]{1,0:T(8,128)S(1)} collective-permute-done((f32[544,128]{1,0:T(8,128)S(1)}, f32[544,128]{1,0:T(8,128)S(1)}, u32[]{:S(2)}, u32[]{:S(2)}) %collective-permute-start.3) | collective-permute-done | bytes 278560 | tf_op jit(solution)/shard_map/ppermute | solution.py:327
  85.5 1.9 %collective-permute-start.7 = (f32[544,128]{1,0:T(8,128)S(1)}, f32[544,128]{1,0:T(8,128)S(1)}, u32[]{:S(2)}, u32[]{:S(2)}) collective-permute-start(f32[544,128]{1,0:T(8,128)S(1)} %collective-permute-done.3.refs_3_), channel_id=1, source_target_pairs={{0,1},{1,0},{2,3},{3,2},{4,5},{5,4},{6,7},{7,6},{8,9},{9,8},{10,11... | collective-permute-start | bytes 835592 | tf_op jit(solution)/shard_map/ppermute | solution.py:333
  87.5 0.0 collective-permute-done.4.refs_5_
  87.5 0.0 collective-permute-done.5.refs_6_
  87.5 0.0 copy-start.1
  87.5 0.0 collective-permute-done.6.refs_7_
  87.5 0.0 copy-start.5
  87.5 1.5 collective-permute-done.7.refs_8_
  89.0 0.0 copy-done.3
  89.0 0.0 copy-done.5
  89.0 0.7 copy-done.7
  89.7 0.0 collective-permute-done.8.refs_9_
  89.7 9.3 %all-to-all-done.2.recv_ref = f32[32,22,1,128]{3,2,1,0:T(1,128)S(1)} async-done(((f32[32,22,1,128]{3,2,1,0:T(1,128)}), f32[32,22,1,128]{3,2,1,0:T(1,128)S(1)}, u32[]{:S(2)}, u32[]{:S(2)}) %all-to-all-start.2) | async-done | bytes 360480 | tf_op jit(solution)/shard_map/all_to_all | solution.py:337
  99.0 0.0 copy-done.11
  99.0 4.2 %evaluate.3 = f32[224,4,128]{2,1,0:T(4,128)} custom-call(f32[32,22,1,128]{3,2,1,0:T(1,128)S(1)} %all-to-all-done.2.recv_ref, f32[8,8,128]{2,1,0:T(8,128)S(1)} %copy-done.11, f32[1088,128]{1,0:T(8,128)S(1)} %select_maximum_fusion.refs_0_, f32[1088,128]{1,0:T(8,128)S(1)} %collective-permute-done.refs_1_, f32[544,128]{1,0:T(8,128)S(1)} %collective-permute-done.1.refs_2_, ...), custom_call_target="tpu_custom_call" | custom-call | tf_op jit(solution)/shard_map/evaluate/pallas_call | solution.py:273
  103.2 0.0 copy-done.1
  103.2 12.1 %all-to-all-start.3 = ((f32[32,7,4,128]{3,2,1,0:T(4,128)}), f32[32,7,4,128]{3,2,1,0:T(4,128)S(1)}, u32[]{:S(2)}, u32[]{:S(2)}) async-start(f32[32,7,4,128]{3,2,1,0:T(4,128)} %bitcast.8), calls=%async_computation.3 | async-start | bytes 917504 | tf_op jit(solution)/shard_map/all_to_all | solution.py:337
  115.3 0.7 slice_reduce_fusion
  116.7 58.3 %all-to-all-done.3 = f32[32,7,4,128]{3,2,1,0:T(4,128)S(1)} async-done(((f32[32,7,4,128]{3,2,1,0:T(4,128)}), f32[32,7,4,128]{3,2,1,0:T(4,128)S(1)}, u32[]{:S(2)}, u32[]{:S(2)}) %all-to-all-start.3) | async-done | bytes 458784 | tf_op jit(solution)/shard_map/all_to_all | solution.py:337
  175.0 0.6 unpack.3
  175.6 0.0 copy-done.4
  175.6 0.2 copy-done.10
  175.9 0.6 copy-done.9
  (9 shorter events, 0.1 us)
Async XLA Ops:
  0.0 48.6 %copy-start = (f32[24,64]{1,0:T(8,128)S(1)}, f32[24,64]{1,0:T(8,128)}, u32[]{:S(2)}) copy-start(f32[24,64]{1,0:T(8,128)} %param.11) | copy-start | bytes 18436
  0.0 0.7 copy-start.13
  0.0 48.8 %copy-start.8 = (f32[64,4,512]{2,1,0:T(4,128)S(1)}, f32[64,4,512]{2,1,0:T(4,128)}, u32[]{:S(2)}) copy-start(f32[64,4,512]{2,1,0:T(4,128)} %param.10) | copy-start | bytes 1572868
  2.8 45.8 %copy-start.12 = (f32[24,24]{1,0:T(8,128)S(1)}, f32[24,24]{1,0:T(8,128)}, u32[]{:S(2)}) copy-start(f32[24,24]{1,0:T(8,128)} %constant.13.clone) | copy-start | bytes 6916
  2.8 45.8 %copy-start.14 = (f32[24]{0:T(128)S(1)}, f32[24]{0:T(128)}, u32[]{:S(2)}) copy-start(f32[24]{0:T(128)} %constant.21) | copy-start | bytes 292
  2.8 96.2 %all-to-all-start.2 = ((f32[32,22,1,128]{3,2,1,0:T(1,128)}), f32[32,22,1,128]{3,2,1,0:T(1,128)S(1)}, u32[]{:S(2)}, u32[]{:S(2)}) async-start(f32[32,22,1,128]{3,2,1,0:T(1,128)} %get-tuple-element.55), calls=%async_computation.2 | async-start | bytes 720896 | tf_op jit(solution)/shard_map/all_to_all | solution.py:337
  48.9 16.8 %collective-permute-start = (f32[1088,128]{1,0:T(8,128)S(1)}, f32[1088,128]{1,0:T(8,128)S(1)}, u32[]{:S(2)}, u32[]{:S(2)}) collective-permute-start(f32[1088,128]{1,0:T(8,128)S(1)} %select_maximum_fusion.refs_0_), channel_id=1, source_target_pairs={{0,6},{2,0},{4,2},{6,4},{1,7},{3,1},{5,3},{7,5},{8,14},{10,8},{12,... | collective-permute-start | bytes 1671176 | tf_op jit(solution)/shard_map/ppermute | solution.py:327
  54.0 19.3 %collective-permute-start.2 = (f32[1088,128]{1,0:T(8,128)S(1)}, f32[1088,128]{1,0:T(8,128)S(1)}, u32[]{:S(2)}, u32[]{:S(2)}) collective-permute-start(f32[1088,128]{1,0:T(8,128)S(1)} %select_maximum_fusion.refs_0_), channel_id=1, source_target_pairs={{0,2},{2,4},{4,6},{6,0},{1,3},{3,5},{5,7},{7,1},{8,10},{10,12},{12... | collective-permute-start | bytes 1671176 | tf_op jit(solution)/shard_map/ppermute | solution.py:327
  56.0 31.5 %collective-permute-start.4 = (f32[1088,128]{1,0:T(8,128)S(1)}, f32[1088,128]{1,0:T(8,128)S(1)}, u32[]{:S(2)}, u32[]{:S(2)}) collective-permute-start(f32[1088,128]{1,0:T(8,128)S(1)} %select_maximum_fusion.refs_0_), channel_id=1, source_target_pairs={{0,1},{1,0},{2,3},{3,2},{4,5},{5,4},{6,7},{7,6},{8,9},{9,8},{10,11... | collective-permute-start | bytes 1671176 | tf_op jit(solution)/shard_map/ppermute | solution.py:333
  65.7 33.3 %copy-start.11 = (f32[8,8,128]{2,1,0:T(8,128)S(1)}, f32[8,8,128]{2,1,0:T(8,128)}, u32[]{:S(2)}) copy-start(f32[8,8,128]{2,1,0:T(8,128)} %constant.15.clone.const_ref) | copy-start | bytes 98308
  65.7 12.0 %collective-permute-start.1 = (f32[544,128]{1,0:T(8,128)S(1)}, f32[544,128]{1,0:T(8,128)S(1)}, u32[]{:S(2)}, u32[]{:S(2)}) collective-permute-start(f32[544,128]{1,0:T(8,128)S(1)} %slice.13), channel_id=1, source_target_pairs={{0,6},{2,0},{4,2},{6,4},{1,7},{3,1},{5,3},{7,5},{8,14},{10,8},{12,... | collective-permute-start | bytes 835592 | tf_op jit(solution)/shard_map/ppermute | solution.py:327
  71.3 16.2 %collective-permute-start.5 = (f32[1088,128]{1,0:T(8,128)S(1)}, f32[1088,128]{1,0:T(8,128)S(1)}, u32[]{:S(2)}, u32[]{:S(2)}) collective-permute-start(f32[1088,128]{1,0:T(8,128)S(1)} %collective-permute-done.refs_1_), channel_id=1, source_target_pairs={{0,1},{1,0},{2,3},{3,2},{4,5},{5,4},{6,7},{7,6},{8,9},{9,8},{10,11... | collective-permute-start | bytes 1671176 | tf_op jit(solution)/shard_map/ppermute | solution.py:333
  73.3 12.2 %collective-permute-start.3 = (f32[544,128]{1,0:T(8,128)S(1)}, f32[544,128]{1,0:T(8,128)S(1)}, u32[]{:S(2)}, u32[]{:S(2)}) collective-permute-start(f32[544,128]{1,0:T(8,128)S(1)} %slice.14), channel_id=1, source_target_pairs={{0,2},{2,4},{4,6},{6,0},{1,3},{3,5},{5,7},{7,1},{8,10},{10,12},{12... | collective-permute-start | bytes 835592 | tf_op jit(solution)/shard_map/ppermute | solution.py:327
  75.3 14.4 %collective-permute-start.8 = (f32[1088,128]{1,0:T(8,128)S(1)}, f32[1088,128]{1,0:T(8,128)}, u32[]{:S(2)}, u32[]{:S(2)}) collective-permute-start(f32[1088,128]{1,0:T(8,128)S(1)} %collective-permute-done.2.refs_4_), channel_id=1, source_target_pairs={{0,1},{1,0},{2,3},{3,2},{4,5},{5,4},{6,7},{7,6},{8,9},{9,8},{10,11... | collective-permute-start | bytes 1671176 | tf_op jit(solution)/shard_map/ppermute | solution.py:333
  77.8 9.8 %collective-permute-start.6 = (f32[544,128]{1,0:T(8,128)S(1)}, f32[544,128]{1,0:T(8,128)S(1)}, u32[]{:S(2)}, u32[]{:S(2)}) collective-permute-start(f32[544,128]{1,0:T(8,128)S(1)} %collective-permute-done.1.refs_2_), channel_id=1, source_target_pairs={{0,1},{1,0},{2,3},{3,2},{4,5},{5,4},{6,7},{7,6},{8,9},{9,8},{10,11... | collective-permute-start | bytes 835592 | tf_op jit(solution)/shard_map/ppermute | solution.py:333
  85.5 3.5 %copy-start.3 = (f32[544,128]{1,0:T(8,128)}, f32[544,128]{1,0:T(8,128)S(1)}, u32[]{:S(2)}) copy-start(f32[544,128]{1,0:T(8,128)S(1)} %collective-permute-done.3.refs_3_) | copy-start | bytes 835588
  85.5 3.5 %collective-permute-start.7 = (f32[544,128]{1,0:T(8,128)S(1)}, f32[544,128]{1,0:T(8,128)S(1)}, u32[]{:S(2)}, u32[]{:S(2)}) collective-permute-start(f32[544,128]{1,0:T(8,128)S(1)} %collective-permute-done.3.refs_3_), channel_id=1, source_target_pairs={{0,1},{1,0},{2,3},{3,2},{4,5},{5,4},{6,7},{7,6},{8,9},{9,8},{10,11... | collective-permute-start | bytes 835592 | tf_op jit(solution)/shard_map/ppermute | solution.py:333
  87.5 15.7 %copy-start.1 = (f32[1088,128]{1,0:T(8,128)}, f32[1088,128]{1,0:T(8,128)S(1)}, u32[]{:S(2)}) copy-start(f32[1088,128]{1,0:T(8,128)S(1)} %collective-permute-done.5.refs_6_) | copy-start | bytes 1671172
  87.5 1.5 copy-start.5
  89.0 0.7 copy-start.7
  103.2 71.9 %all-to-all-start.3 = ((f32[32,7,4,128]{3,2,1,0:T(4,128)}), f32[32,7,4,128]{3,2,1,0:T(4,128)S(1)}, u32[]{:S(2)}, u32[]{:S(2)}) async-start(f32[32,7,4,128]{3,2,1,0:T(4,128)} %bitcast.8), calls=%async_computation.3 | async-start | bytes 917504 | tf_op jit(solution)/shard_map/all_to_all | solution.py:337
  116.0 59.6 %copy-start.4 = (f32[544,128]{1,0:T(8,128)S(1)}, f32[544,128]{1,0:T(8,128)}, u32[]{:S(2)}) copy-start(f32[544,128]{1,0:T(8,128)} %copy-done.3) | copy-start | bytes 835588
  175.0 0.8 copy-start.10
  175.9 0.6 copy-start.9

commit v5 on v4

--- a/solution.py
+++ b/solution.py
@@ -321,16 +321,21 @@
     fields = old_fields.reshape(elems, 4, 4, LANES).transpose(0, 2, 1, 3).reshape(-1, LANES)
     own = jnp.concatenate([fields, coefs], axis=0)
     segs = lax.axis_size("seg")
-    middle = own.shape[0] // 16 * 8
+    middle = own.shape[0] * 2 // 40 * 8
 
     def along(array, step):
         return lax.ppermute(array, "seg", [(i, (i + step) % segs) for i in range(segs)])
 
+    def swapped(array):
+        return lax.ppermute(array, "sub", [(0, 1), (1, 0)])
+
     before = along(own, 1)
     after = along(own, segs - 1)
-    opposite = [along(after[:middle], segs - 1), along(before[middle:], 1)]
-    half = [own, after, *opposite, before]
-    return half + [lax.ppermute(piece, "sub", [(0, 1), (1, 0)]) for piece in half]
+    near = along(own[:middle], 2)
+    far = along(before[middle:], 1)
+    opposite = jnp.concatenate([near, far], axis=0)
+    half = [own, after, opposite, before]
+    return half + [swapped(piece) for piece in half]
 
 
 def all_to_all(array):

time: 177 us -> 172 us (0.972)
  starting transfers between devices: 82.8 us -> 75.7 us
    all_to_all x2, waiting for transfers between devices: 67.6 us -> 73.5 us  [all_to_all(): lax.all_to_all(array, 'block', split_axis=0, concat_axis=0, tiled=True)]
    all_to_all x2, starting transfers between devices: 57.9 us -> 53 us  [all_to_all(): lax.all_to_all(array, 'block', split_axis=0, concat_axis=0, tiled=True)]
    ppermute x4, waiting for transfers between devices: 13.6 us -> 9.78 us  [along(): lax.ppermute(array, 'seg', [(i, (i + step) % segs) for i in range(segs)])]
    ppermute x5 -> x4, starting transfers between devices: 10.2 us -> 8.29 us  [swapped(): return lax.ppermute(array, 'sub', [(0, 1), (1, 0)])]
  transfers between devices with their start and end apart: 11 -> 10, of which waited for: 5 -> 6; matrix products, arithmetic and copies ran while one was open for 1% -> 1% of each run, Pallas kernels for 0% -> 0%
where the time goes in v5:
time: 172 us; the launch traced here: 171 us
  waiting for transfers between devices  83.6 us (49%)
  starting transfers between devices  75.7 us (44%)
  Pallas kernels  6.89 us (4%)
  local copies, waits for them, and re-layouts  3.29 us (2%)
    all_to_all x2, waiting for transfers between devices, all_to_all(): lax.all_to_all(array, 'block', split_axis=0, concat_axis=0, tiled=True)  73.5 us
    all_to_all x2, starting transfers between devices, all_to_all(): lax.all_to_all(array, 'block', split_axis=0, concat_axis=0, tiled=True)  53 us
    ppermute x4, starting transfers between devices, along(): lax.ppermute(array, 'seg', [(i, (i + step) % segs) for i in range(segs)])  14.4 us
    ppermute x4, waiting for transfers between devices, along(): lax.ppermute(array, 'seg', [(i, (i + step) % segs) for i in range(segs)])  9.78 us
    ppermute x4, starting transfers between devices, swapped(): return lax.ppermute(array, 'sub', [(0, 1), (1, 0)])  8.29 us
    pallas_call x1, Pallas kernels, evaluate(): pl.pallas_call(functools.partial(evaluate_kernel, elems, slots, len(piece...  4.24 us
  transfers between devices with their start and end apart: 10, of which 6 were waited for; matrix products, arithmetic and copies ran while one was open for 1% of the time, Pallas kernels for 0%

profile of v5, /device:TPU:40, one launch (start us, length us, event | category | flops | bytes accessed | tf_op | source)
XLA Modules:
  0.0 171.4 jit_solution(7247100019874777017)
XLA Ops:
  0.0 0.0 copy-start
  0.0 0.0 copy-start.10
  0.0 0.0 copy-start.5
  0.0 0.7 copy-done.10
  0.7 2.1 %pack.3 = (f32[32,22,1,128]{3,2,1,0:T(1,128)}, s32[32]{0:T(128)S(1)}) custom-call(s32[32]{0:T(128)S(1)} %copy-done.10, f32[32,3,128]{2,1,0:T(4,128)} %bitcast.24), custom_call_target="tpu_custom_call" | custom-call | tf_op jit(solution)/shard_map/pack/pallas_call | solution.py:106
  2.7 0.0 copy-start.9
  2.8 0.0 copy-start.11
  2.8 45.8 %all-to-all-start.2 = ((f32[32,22,1,128]{3,2,1,0:T(1,128)}), f32[32,22,1,128]{3,2,1,0:T(1,128)S(1)}, u32[]{:S(2)}, u32[]{:S(2)}) async-start(f32[32,22,1,128]{3,2,1,0:T(1,128)} %get-tuple-element.49), calls=%async_computation.2 | async-start | bytes 720896 | tf_op jit(solution)/shard_map/all_to_all | solution.py:342
  48.6 0.0 copy-done
  48.6 0.0 copy-done.9
  48.6 0.0 copy-done.11
  48.6 0.2 fusion
  48.8 0.0 copy-done.5
  48.9 3.6 %collective-permute-start.2 = (f32[1088,128]{1,0:T(8,128)S(1)}, f32[1088,128]{1,0:T(8,128)S(1)}, u32[]{:S(2)}, u32[]{:S(2)}) collective-permute-start(f32[1088,128]{1,0:T(8,128)S(1)} %select_maximum_fusion.refs_0_), channel_id=1, source_target_pairs={{0,2},{2,4},{4,6},{6,0},{1,3},{3,5},{5,7},{7,1},{8,10},{10,12},{12... | collective-permute-start | bytes 1671176 | tf_op jit(solution)/shard_map/ppermute | solution.py:327
  52.5 3.5 %collective-permute-start = (f32[1088,128]{1,0:T(8,128)S(1)}, f32[1088,128]{1,0:T(8,128)S(1)}, u32[]{:S(2)}, u32[]{:S(2)}) collective-permute-start(f32[1088,128]{1,0:T(8,128)S(1)} %select_maximum_fusion.refs_0_), channel_id=1, source_target_pairs={{0,6},{2,0},{4,2},{6,4},{1,7},{3,1},{5,3},{7,5},{8,14},{10,8},{12,... | collective-permute-start | bytes 1671176 | tf_op jit(solution)/shard_map/ppermute | solution.py:327
  56.0 4.0 %collective-permute-start.1 = (f32[432,128]{1,0:T(8,128)S(1)}, f32[432,128]{1,0:T(8,128)S(1)}, u32[]{:S(2)}, u32[]{:S(2)}) collective-permute-start(f32[432,128]{1,0:T(8,128)S(1)} %bitcast.26), channel_id=1, source_target_pairs={{0,4},{2,6},{4,0},{6,2},{1,5},{3,7},{5,1},{7,3},{8,12},{10,14},{12... | collective-permute-start | bytes 663560 | tf_op jit(solution)/shard_map/ppermute | solution.py:327
  60.1 6.5 %collective-permute-done.2.refs_3_ = f32[1088,128]{1,0:T(8,128)S(1)} collective-permute-done((f32[1088,128]{1,0:T(8,128)S(1)}, f32[1088,128]{1,0:T(8,128)S(1)}, u32[]{:S(2)}, u32[]{:S(2)}) %collective-permute-start.2) | collective-permute-done | bytes 557088 | tf_op jit(solution)/shard_map/ppermute | solution.py:327
  66.6 3.3 %collective-permute-start.3 = (f32[656,128]{1,0:T(8,128)S(1)}, f32[656,128]{1,0:T(8,128)S(1)}, u32[]{:S(2)}, u32[]{:S(2)}) collective-permute-start(f32[656,128]{1,0:T(8,128)S(1)} %slice.18), channel_id=1, source_target_pairs={{0,2},{2,4},{4,6},{6,0},{1,3},{3,5},{5,7},{7,1},{8,10},{10,12},{12... | collective-permute-start | bytes 1007624 | tf_op jit(solution)/shard_map/ppermute | solution.py:327
  69.9 2.0 %collective-permute-start.4 = (f32[1088,128]{1,0:T(8,128)S(1)}, f32[1088,128]{1,0:T(8,128)S(1)}, u32[]{:S(2)}, u32[]{:S(2)}) collective-permute-start(f32[1088,128]{1,0:T(8,128)S(1)} %select_maximum_fusion.refs_0_), channel_id=1, source_target_pairs={{0,1},{1,0},{2,3},{3,2},{4,5},{5,4},{6,7},{7,6},{8,9},{9,8},{10,11... | collective-permute-start | bytes 1671176 | tf_op jit(solution)/shard_map/ppermute | solution.py:330
  71.9 1.8 %collective-permute-done.1 = f32[432,128]{1,0:T(8,128)S(1)} collective-permute-done((f32[432,128]{1,0:T(8,128)S(1)}, f32[432,128]{1,0:T(8,128)S(1)}, u32[]{:S(2)}, u32[]{:S(2)}) %collective-permute-start.1) | collective-permute-done | bytes 221216 | tf_op jit(solution)/shard_map/ppermute | solution.py:327
  73.7 0.0 copy-start.8
  73.7 2.0 %collective-permute-start.7 = (f32[1088,128]{1,0:T(8,128)S(1)}, f32[1088,128]{1,0:T(8,128)S(1)}, u32[]{:S(2)}, u32[]{:S(2)}) collective-permute-start(f32[1088,128]{1,0:T(8,128)S(1)} %collective-permute-done.2.refs_3_), channel_id=1, source_target_pairs={{0,1},{1,0},{2,3},{3,2},{4,5},{5,4},{6,7},{7,6},{8,9},{9,8},{10,11... | collective-permute-start | bytes 1671176 | tf_op jit(solution)/shard_map/ppermute | solution.py:330
  75.6 0.0 collective-permute-done.refs_1_
  75.7 2.4 %collective-permute-start.5 = (f32[1088,128]{1,0:T(8,128)S(1)}, f32[1088,128]{1,0:T(8,128)S(1)}, u32[]{:S(2)}, u32[]{:S(2)}) collective-permute-start(f32[1088,128]{1,0:T(8,128)S(1)} %collective-permute-done.refs_1_), channel_id=1, source_target_pairs={{0,1},{1,0},{2,3},{3,2},{4,5},{5,4},{6,7},{7,6},{8,9},{9,8},{10,11... | collective-permute-start | bytes 1671176 | tf_op jit(solution)/shard_map/ppermute | solution.py:330
  78.1 1.5 collective-permute-done.3
  79.6 2.0 %collective-permute-start.6 = (f32[1088,128]{1,0:T(8,128)S(1)}, f32[1088,128]{1,0:T(8,128)}, u32[]{:S(2)}, u32[]{:S(2)}) collective-permute-start(f32[1088,128]{1,0:T(8,128)S(1)} %constant_dynamic-update-slice_fusion.refs_2_), channel_id=1, source_target_pairs={{0,1},{1,0},{2,3},{3,2},{4,5},{5,4},{6,7},{7,6},{8,9},{9,8},{10,11... | collective-permute-start | bytes 1671176 | tf_op jit(solution)/shard_map/ppermute | solution.py:330
  81.6 0.0 collective-permute-done.4.refs_4_
  81.6 0.0 copy-start.1
  81.6 0.0 collective-permute-done.5.refs_5_
  81.6 0.0 copy-start.4
  81.6 0.0 collective-permute-done.7.refs_7_
  81.6 0.8 copy-done.4
  82.5 0.0 copy-start.3
  82.5 0.8 copy-done.3
  83.3 0.4 collective-permute-done.6.refs_6_
  83.6 15.4 %all-to-all-done.2.recv_ref = f32[32,22,1,128]{3,2,1,0:T(1,128)S(1)} async-done(((f32[32,22,1,128]{3,2,1,0:T(1,128)}), f32[32,22,1,128]{3,2,1,0:T(1,128)S(1)}, u32[]{:S(2)}, u32[]{:S(2)}) %all-to-all-start.2) | async-done | bytes 360480 | tf_op jit(solution)/shard_map/all_to_all | solution.py:342
  99.0 0.0 copy-done.8
  99.0 4.2 %evaluate.3 = f32[224,4,128]{2,1,0:T(4,128)} custom-call(f32[32,22,1,128]{3,2,1,0:T(1,128)S(1)} %all-to-all-done.2.recv_ref, f32[8,8,128]{2,1,0:T(8,128)S(1)} %copy-done.8, f32[1088,128]{1,0:T(8,128)S(1)} %select_maximum_fusion.refs_0_, f32[1088,128]{1,0:T(8,128)S(1)} %collective-permute-done.refs_1_, ...), custom_call_target="tpu_custom_call" | custom-call | tf_op jit(solution)/shard_map/evaluate/pallas_call | solution.py:273
  103.2 0.0 copy-done.1
  103.3 7.2 %all-to-all-start.3 = ((f32[32,7,4,128]{3,2,1,0:T(4,128)}), f32[32,7,4,128]{3,2,1,0:T(4,128)S(1)}, u32[]{:S(2)}, u32[]{:S(2)}) async-start(f32[32,7,4,128]{3,2,1,0:T(4,128)} %bitcast.10), calls=%async_computation.3 | async-start | bytes 917504 | tf_op jit(solution)/shard_map/all_to_all | solution.py:342
  110.5 0.7 slice_reduce_fusion
  111.8 58.1 %all-to-all-done.3 = f32[32,7,4,128]{3,2,1,0:T(4,128)S(1)} async-done(((f32[32,7,4,128]{3,2,1,0:T(4,128)}), f32[32,7,4,128]{3,2,1,0:T(4,128)S(1)}, u32[]{:S(2)}, u32[]{:S(2)}) %all-to-all-start.3) | async-done | bytes 458784 | tf_op jit(solution)/shard_map/all_to_all | solution.py:342
  169.9 0.0 copy-start.7
  169.9 0.6 unpack.3
  170.5 0.2 copy-done.7
  170.8 0.0 copy-start.6
  170.8 0.6 copy-done.6
  (6 shorter events, 0.1 us)
Async XLA Ops:
  0.0 48.6 %copy-start = (f32[24,64]{1,0:T(8,128)S(1)}, f32[24,64]{1,0:T(8,128)}, u32[]{:S(2)}) copy-start(f32[24,64]{1,0:T(8,128)} %param.11) | copy-start | bytes 18436
  0.0 0.7 copy-start.10
  0.0 48.8 %copy-start.5 = (f32[64,4,512]{2,1,0:T(4,128)S(1)}, f32[64,4,512]{2,1,0:T(4,128)}, u32[]{:S(2)}) copy-start(f32[64,4,512]{2,1,0:T(4,128)} %param.10) | copy-start | bytes 1572868
  2.7 45.8 %copy-start.9 = (f32[24,24]{1,0:T(8,128)S(1)}, f32[24,24]{1,0:T(8,128)}, u32[]{:S(2)}) copy-start(f32[24,24]{1,0:T(8,128)} %constant.13.clone) | copy-start | bytes 6916
  2.8 45.8 %copy-start.11 = (f32[24]{0:T(128)S(1)}, f32[24]{0:T(128)}, u32[]{:S(2)}) copy-start(f32[24]{0:T(128)} %constant.21) | copy-start | bytes 292
  2.8 96.2 %all-to-all-start.2 = ((f32[32,22,1,128]{3,2,1,0:T(1,128)}), f32[32,22,1,128]{3,2,1,0:T(1,128)S(1)}, u32[]{:S(2)}, u32[]{:S(2)}) async-start(f32[32,22,1,128]{3,2,1,0:T(1,128)} %get-tuple-element.49), calls=%async_computation.2 | async-start | bytes 720896 | tf_op jit(solution)/shard_map/all_to_all | solution.py:342
  48.9 17.7 %collective-permute-start.2 = (f32[1088,128]{1,0:T(8,128)S(1)}, f32[1088,128]{1,0:T(8,128)S(1)}, u32[]{:S(2)}, u32[]{:S(2)}) collective-permute-start(f32[1088,128]{1,0:T(8,128)S(1)} %select_maximum_fusion.refs_0_), channel_id=1, source_target_pairs={{0,2},{2,4},{4,6},{6,0},{1,3},{3,5},{5,7},{7,1},{8,10},{10,12},{12... | collective-permute-start | bytes 1671176 | tf_op jit(solution)/shard_map/ppermute | solution.py:327
  52.5 23.2 %collective-permute-start = (f32[1088,128]{1,0:T(8,128)S(1)}, f32[1088,128]{1,0:T(8,128)S(1)}, u32[]{:S(2)}, u32[]{:S(2)}) collective-permute-start(f32[1088,128]{1,0:T(8,128)S(1)} %select_maximum_fusion.refs_0_), channel_id=1, source_target_pairs={{0,6},{2,0},{4,2},{6,4},{1,7},{3,1},{5,3},{7,5},{8,14},{10,8},{12,... | collective-permute-start | bytes 1671176 | tf_op jit(solution)/shard_map/ppermute | solution.py:327
  56.0 17.6 %collective-permute-start.1 = (f32[432,128]{1,0:T(8,128)S(1)}, f32[432,128]{1,0:T(8,128)S(1)}, u32[]{:S(2)}, u32[]{:S(2)}) collective-permute-start(f32[432,128]{1,0:T(8,128)S(1)} %bitcast.26), channel_id=1, source_target_pairs={{0,4},{2,6},{4,0},{6,2},{1,5},{3,7},{5,1},{7,3},{8,12},{10,14},{12... | collective-permute-start | bytes 663560 | tf_op jit(solution)/shard_map/ppermute | solution.py:327
  66.6 13.0 %collective-permute-start.3 = (f32[656,128]{1,0:T(8,128)S(1)}, f32[656,128]{1,0:T(8,128)S(1)}, u32[]{:S(2)}, u32[]{:S(2)}) collective-permute-start(f32[656,128]{1,0:T(8,128)S(1)} %slice.18), channel_id=1, source_target_pairs={{0,2},{2,4},{4,6},{6,0},{1,3},{3,5},{5,7},{7,1},{8,10},{10,12},{12... | collective-permute-start | bytes 1007624 | tf_op jit(solution)/shard_map/ppermute | solution.py:327
  69.9 11.7 %collective-permute-start.4 = (f32[1088,128]{1,0:T(8,128)S(1)}, f32[1088,128]{1,0:T(8,128)S(1)}, u32[]{:S(2)}, u32[]{:S(2)}) collective-permute-start(f32[1088,128]{1,0:T(8,128)S(1)} %select_maximum_fusion.refs_0_), channel_id=1, source_target_pairs={{0,1},{1,0},{2,3},{3,2},{4,5},{5,4},{6,7},{7,6},{8,9},{9,8},{10,11... | collective-permute-start | bytes 1671176 | tf_op jit(solution)/shard_map/ppermute | solution.py:330
  73.7 25.3 %copy-start.8 = (f32[8,8,128]{2,1,0:T(8,128)S(1)}, f32[8,8,128]{2,1,0:T(8,128)}, u32[]{:S(2)}) copy-start(f32[8,8,128]{2,1,0:T(8,128)} %constant.15.clone.const_ref) | copy-start | bytes 98308
  73.7 7.9 %collective-permute-start.7 = (f32[1088,128]{1,0:T(8,128)S(1)}, f32[1088,128]{1,0:T(8,128)S(1)}, u32[]{:S(2)}, u32[]{:S(2)}) collective-permute-start(f32[1088,128]{1,0:T(8,128)S(1)} %collective-permute-done.2.refs_3_), channel_id=1, source_target_pairs={{0,1},{1,0},{2,3},{3,2},{4,5},{5,4},{6,7},{7,6},{8,9},{9,8},{10,11... | collective-permute-start | bytes 1671176 | tf_op jit(solution)/shard_map/ppermute | solution.py:330
  75.7 6.0 %collective-permute-start.5 = (f32[1088,128]{1,0:T(8,128)S(1)}, f32[1088,128]{1,0:T(8,128)S(1)}, u32[]{:S(2)}, u32[]{:S(2)}) collective-permute-start(f32[1088,128]{1,0:T(8,128)S(1)} %collective-permute-done.refs_1_), channel_id=1, source_target_pairs={{0,1},{1,0},{2,3},{3,2},{4,5},{5,4},{6,7},{7,6},{8,9},{9,8},{10,11... | collective-permute-start | bytes 1671176 | tf_op jit(solution)/shard_map/ppermute | solution.py:330
  79.6 4.0 %collective-permute-start.6 = (f32[1088,128]{1,0:T(8,128)S(1)}, f32[1088,128]{1,0:T(8,128)}, u32[]{:S(2)}, u32[]{:S(2)}) collective-permute-start(f32[1088,128]{1,0:T(8,128)S(1)} %constant_dynamic-update-slice_fusion.refs_2_), channel_id=1, source_target_pairs={{0,1},{1,0},{2,3},{3,2},{4,5},{5,4},{6,7},{7,6},{8,9},{9,8},{10,11... | collective-permute-start | bytes 1671176 | tf_op jit(solution)/shard_map/ppermute | solution.py:330
  81.6 21.7 %copy-start.1 = (f32[1088,128]{1,0:T(8,128)}, f32[1088,128]{1,0:T(8,128)S(1)}, u32[]{:S(2)}) copy-start(f32[1088,128]{1,0:T(8,128)S(1)} %collective-permute-done.4.refs_4_) | copy-start | bytes 1671172
  81.6 0.9 copy-start.4
  82.5 0.8 copy-start.3
  103.3 66.7 %all-to-all-start.3 = ((f32[32,7,4,128]{3,2,1,0:T(4,128)}), f32[32,7,4,128]{3,2,1,0:T(4,128)S(1)}, u32[]{:S(2)}, u32[]{:S(2)}) async-start(f32[32,7,4,128]{3,2,1,0:T(4,128)} %bitcast.10), calls=%async_computation.3 | async-start | bytes 917504 | tf_op jit(solution)/shard_map/all_to_all | solution.py:342
  169.9 0.8 copy-start.7
  170.8 0.6 copy-start.6

commit v6 on v5

--- a/solution.py
+++ b/solution.py
@@ -7,6 +7,7 @@
 from jax.experimental import pallas as pl
 from jax.experimental.pallas import tpu as pltpu
 from jax.sharding import PartitionSpec as P
+
 
 NEWTON = 3
 CAP = 2
@@ -300,6 +301,7 @@
         else:
             out_ref[b] = back_ref[jnp.maximum(at_ref[b], 0)]
 
+
 def unpack(at, back, before):
     held = [] if before is None else [before]
     return pl.pallas_call(
@@ -321,7 +323,7 @@
     fields = old_fields.reshape(elems, 4, 4, LANES).transpose(0, 2, 1, 3).reshape(-1, LANES)
     own = jnp.concatenate([fields, coefs], axis=0)
     segs = lax.axis_size("seg")
-    middle = own.shape[0] * 2 // 40 * 8
+    middle = own.shape[0] * 9 // 160 * 8
 
     def along(array, step):
         return lax.ppermute(array, "seg", [(i, (i + step) % segs) for i in range(segs)])
@@ -333,9 +335,10 @@
     after = along(own, segs - 1)
     near = along(own[:middle], 2)
     far = along(before[middle:], 1)
-    opposite = jnp.concatenate([near, far], axis=0)
-    half = [own, after, opposite, before]
-    return half + [swapped(piece) for piece in half]
+    opposite = [jnp.concatenate([near, far], axis=0)]
+    swaps = [swapped(own), swapped(after)]
+    swaps += [swapped(opposite[0]), swapped(before)]
+    return [own, after, *opposite, before, *swaps]
 
 
 def all_to_all(array):

time: 172 us -> 172 us (level)
  no operation moved by 1% of the time
where the time goes in v6:
time: 172 us; the launch traced here: 171 us
  waiting for transfers between devices  82.8 us (48%)
  starting transfers between devices  75.6 us (44%)
  Pallas kernels  7.26 us (4%)
  local copies, waits for them, and re-layouts  3.29 us (2%)
    all_to_all x2, waiting for transfers between devices, all_to_all(): lax.all_to_all(array, 'block', split_axis=0, concat_axis=0, tiled=True)  72.8 us
    all_to_all x2, starting transfers between devices, all_to_all(): lax.all_to_all(array, 'block', split_axis=0, concat_axis=0, tiled=True)  52.9 us
    ppermute x4, starting transfers between devices, along(): lax.ppermute(array, 'seg', [(i, (i + step) % segs) for i in range(segs)])  14.4 us
    ppermute x4, waiting for transfers between devices, along(): lax.ppermute(array, 'seg', [(i, (i + step) % segs) for i in range(segs)])  9.68 us
    ppermute x4, starting transfers between devices, swapped(): return lax.ppermute(array, 'sub', [(0, 1), (1, 0)])  8.29 us
    pallas_call x1, Pallas kernels, evaluate(): pl.pallas_call(functools.partial(evaluate_kernel, elems, slots, len(piece...  4.61 us
  transfers between devices with their start and end apart: 10, of which 6 were waited for; matrix products, arithmetic and copies ran while one was open for 1% of the time, Pallas kernels for 0%

profile of v6, /device:TPU:40, one launch (start us, length us, event | category | flops | bytes accessed | tf_op | source)
XLA Modules:
  0.0 170.9 jit_solution(5918445597718863645)
XLA Ops:
  0.0 0.0 copy-start
  0.0 0.0 copy-start.10
  0.0 0.0 copy-start.5
  0.0 0.7 copy-done.10
  0.7 2.1 %pack.3 = (f32[32,22,1,128]{3,2,1,0:T(1,128)}, s32[32]{0:T(128)S(1)}) custom-call(s32[32]{0:T(128)S(1)} %copy-done.10, f32[32,3,128]{2,1,0:T(4,128)} %bitcast.23), custom_call_target="tpu_custom_call" | custom-call | tf_op jit(solution)/shard_map/pack/pallas_call | solution.py:107
  2.7 0.0 copy-start.9
  2.8 0.0 copy-start.11
  2.8 45.8 %all-to-all-start.2 = ((f32[32,22,1,128]{3,2,1,0:T(1,128)}), f32[32,22,1,128]{3,2,1,0:T(1,128)S(1)}, u32[]{:S(2)}, u32[]{:S(2)}) async-start(f32[32,22,1,128]{3,2,1,0:T(1,128)} %get-tuple-element.49), calls=%async_computation.2 | async-start | bytes 720896 | tf_op jit(solution)/shard_map/all_to_all | solution.py:345
  48.6 0.0 copy-done
  48.6 0.0 copy-done.9
  48.6 0.0 copy-done.11
  48.6 0.2 fusion
  48.8 0.0 copy-done.5
  48.9 3.6 %collective-permute-start.2 = (f32[1088,128]{1,0:T(8,128)S(1)}, f32[1088,128]{1,0:T(8,128)S(1)}, u32[]{:S(2)}, u32[]{:S(2)}) collective-permute-start(f32[1088,128]{1,0:T(8,128)S(1)} %select_maximum_fusion.refs_0_), channel_id=1, source_target_pairs={{0,2},{2,4},{4,6},{6,0},{1,3},{3,5},{5,7},{7,1},{8,10},{10,12},{12... | collective-permute-start | bytes 1671176 | tf_op jit(solution)/shard_map/ppermute | solution.py:329
  52.5 3.5 %collective-permute-start = (f32[1088,128]{1,0:T(8,128)S(1)}, f32[1088,128]{1,0:T(8,128)S(1)}, u32[]{:S(2)}, u32[]{:S(2)}) collective-permute-start(f32[1088,128]{1,0:T(8,128)S(1)} %select_maximum_fusion.refs_0_), channel_id=1, source_target_pairs={{0,6},{2,0},{4,2},{6,4},{1,7},{3,1},{5,3},{7,5},{8,14},{10,8},{12,... | collective-permute-start | bytes 1671176 | tf_op jit(solution)/shard_map/ppermute | solution.py:329
  56.0 4.0 %collective-permute-start.1 = (f32[488,128]{1,0:T(8,128)S(1)}, f32[488,128]{1,0:T(8,128)S(1)}, u32[]{:S(2)}, u32[]{:S(2)}) collective-permute-start(f32[488,128]{1,0:T(8,128)S(1)} %slice.13), channel_id=1, source_target_pairs={{0,4},{2,6},{4,0},{6,2},{1,5},{3,7},{5,1},{7,3},{8,12},{10,14},{12... | collective-permute-start | bytes 749576 | tf_op jit(solution)/shard_map/ppermute | solution.py:329
  60.1 6.5 %collective-permute-done.2.refs_3_ = f32[1088,128]{1,0:T(8,128)S(1)} collective-permute-done((f32[1088,128]{1,0:T(8,128)S(1)}, f32[1088,128]{1,0:T(8,128)S(1)}, u32[]{:S(2)}, u32[]{:S(2)}) %collective-permute-start.2) | collective-permute-done | bytes 557088 | tf_op jit(solution)/shard_map/ppermute | solution.py:329
  66.6 3.3 %collective-permute-start.3 = (f32[600,128]{1,0:T(8,128)S(1)}, f32[600,128]{1,0:T(8,128)S(1)}, u32[]{:S(2)}, u32[]{:S(2)}) collective-permute-start(f32[600,128]{1,0:T(8,128)S(1)} %slice.14), channel_id=1, source_target_pairs={{0,2},{2,4},{4,6},{6,0},{1,3},{3,5},{5,7},{7,1},{8,10},{10,12},{12... | collective-permute-start | bytes 921608 | tf_op jit(solution)/shard_map/ppermute | solution.py:329
  69.9 2.0 %collective-permute-start.4 = (f32[1088,128]{1,0:T(8,128)S(1)}, f32[1088,128]{1,0:T(8,128)S(1)}, u32[]{:S(2)}, u32[]{:S(2)}) collective-permute-start(f32[1088,128]{1,0:T(8,128)S(1)} %select_maximum_fusion.refs_0_), channel_id=1, source_target_pairs={{0,1},{1,0},{2,3},{3,2},{4,5},{5,4},{6,7},{7,6},{8,9},{9,8},{10,11... | collective-permute-start | bytes 1671176 | tf_op jit(solution)/shard_map/ppermute | solution.py:332
  71.9 2.4 %collective-permute-done.1 = f32[488,128]{1,0:T(8,128)S(1)} collective-permute-done((f32[488,128]{1,0:T(8,128)S(1)}, f32[488,128]{1,0:T(8,128)S(1)}, u32[]{:S(2)}, u32[]{:S(2)}) %collective-permute-start.1) | collective-permute-done | bytes 249888 | tf_op jit(solution)/shard_map/ppermute | solution.py:329
  74.3 0.0 copy-start.8
  74.3 2.0 %collective-permute-start.7 = (f32[1088,128]{1,0:T(8,128)S(1)}, f32[1088,128]{1,0:T(8,128)S(1)}, u32[]{:S(2)}, u32[]{:S(2)}) collective-permute-start(f32[1088,128]{1,0:T(8,128)S(1)} %collective-permute-done.2.refs_3_), channel_id=1, source_target_pairs={{0,1},{1,0},{2,3},{3,2},{4,5},{5,4},{6,7},{7,6},{8,9},{9,8},{10,11... | collective-permute-start | bytes 1671176 | tf_op jit(solution)/shard_map/ppermute | solution.py:332
  76.3 0.0 collective-permute-done.refs_1_
  76.3 2.4 %collective-permute-start.5 = (f32[1088,128]{1,0:T(8,128)S(1)}, f32[1088,128]{1,0:T(8,128)S(1)}, u32[]{:S(2)}, u32[]{:S(2)}) collective-permute-start(f32[1088,128]{1,0:T(8,128)S(1)} %collective-permute-done.refs_1_), channel_id=1, source_target_pairs={{0,1},{1,0},{2,3},{3,2},{4,5},{5,4},{6,7},{7,6},{8,9},{9,8},{10,11... | collective-permute-start | bytes 1671176 | tf_op jit(solution)/shard_map/ppermute | solution.py:332
  78.7 0.8 collective-permute-done.3
  79.5 2.0 %collective-permute-start.6 = (f32[1088,128]{1,0:T(8,128)S(1)}, f32[1088,128]{1,0:T(8,128)}, u32[]{:S(2)}, u32[]{:S(2)}) collective-permute-start(f32[1088,128]{1,0:T(8,128)S(1)} %constant_dynamic-update-slice_fusion.refs_2_), channel_id=1, source_target_pairs={{0,1},{1,0},{2,3},{3,2},{4,5},{5,4},{6,7},{7,6},{8,9},{9,8},{10,11... | collective-permute-start | bytes 1671176 | tf_op jit(solution)/shard_map/ppermute | solution.py:332
  81.5 0.0 collective-permute-done.4.refs_4_
  81.5 0.0 copy-start.1
  81.5 0.0 collective-permute-done.5.refs_5_
  81.5 0.0 copy-start.4
  81.5 0.0 collective-permute-done.7.refs_7_
  81.5 0.8 copy-done.4
  82.4 0.0 copy-start.3
  82.4 0.8 copy-done.3
  83.2 0.4 collective-permute-done.6.refs_6_
  83.5 15.4 %all-to-all-done.2.recv_ref = f32[32,22,1,128]{3,2,1,0:T(1,128)S(1)} async-done(((f32[32,22,1,128]{3,2,1,0:T(1,128)}), f32[32,22,1,128]{3,2,1,0:T(1,128)S(1)}, u32[]{:S(2)}, u32[]{:S(2)}) %all-to-all-start.2) | async-done | bytes 360480 | tf_op jit(solution)/shard_map/all_to_all | solution.py:345
  99.0 0.0 copy-done.8
  99.0 4.6 %evaluate.3 = f32[224,4,128]{2,1,0:T(4,128)} custom-call(f32[32,22,1,128]{3,2,1,0:T(1,128)S(1)} %all-to-all-done.2.recv_ref, f32[8,8,128]{2,1,0:T(8,128)S(1)} %copy-done.8, f32[1088,128]{1,0:T(8,128)S(1)} %select_maximum_fusion.refs_0_, f32[1088,128]{1,0:T(8,128)S(1)} %collective-permute-done.refs_1_, ...), custom_call_target="tpu_custom_call" | custom-call | tf_op jit(solution)/shard_map/evaluate/pallas_call | solution.py:274
  103.6 0.0 copy-done.1
  103.6 7.1 %all-to-all-start.3 = ((f32[32,7,4,128]{3,2,1,0:T(4,128)}), f32[32,7,4,128]{3,2,1,0:T(4,128)S(1)}, u32[]{:S(2)}, u32[]{:S(2)}) async-start(f32[32,7,4,128]{3,2,1,0:T(4,128)} %bitcast.10), calls=%async_computation.3 | async-start | bytes 917504 | tf_op jit(solution)/shard_map/all_to_all | solution.py:345
  110.8 0.7 slice_reduce_fusion
  112.1 57.3 %all-to-all-done.3 = f32[32,7,4,128]{3,2,1,0:T(4,128)S(1)} async-done(((f32[32,7,4,128]{3,2,1,0:T(4,128)}), f32[32,7,4,128]{3,2,1,0:T(4,128)S(1)}, u32[]{:S(2)}, u32[]{:S(2)}) %all-to-all-start.3) | async-done | bytes 458784 | tf_op jit(solution)/shard_map/all_to_all | solution.py:345
  169.4 0.0 copy-start.7
  169.4 0.6 unpack.3
  170.0 0.2 copy-done.7
  170.3 0.0 copy-start.6
  170.3 0.6 copy-done.6
  (6 shorter events, 0.1 us)
Async XLA Ops:
  0.0 48.6 %copy-start = (f32[24,64]{1,0:T(8,128)S(1)}, f32[24,64]{1,0:T(8,128)}, u32[]{:S(2)}) copy-start(f32[24,64]{1,0:T(8,128)} %param.11) | copy-start | bytes 18436
  0.0 0.7 copy-start.10
  0.0 48.8 %copy-start.5 = (f32[64,4,512]{2,1,0:T(4,128)S(1)}, f32[64,4,512]{2,1,0:T(4,128)}, u32[]{:S(2)}) copy-start(f32[64,4,512]{2,1,0:T(4,128)} %param.10) | copy-start | bytes 1572868
  2.7 45.8 %copy-start.9 = (f32[24,24]{1,0:T(8,128)S(1)}, f32[24,24]{1,0:T(8,128)}, u32[]{:S(2)}) copy-start(f32[24,24]{1,0:T(8,128)} %constant.13.clone) | copy-start | bytes 6916
  2.8 45.8 %copy-start.11 = (f32[24]{0:T(128)S(1)}, f32[24]{0:T(128)}, u32[]{:S(2)}) copy-start(f32[24]{0:T(128)} %constant.21) | copy-start | bytes 292
  2.8 96.2 %all-to-all-start.2 = ((f32[32,22,1,128]{3,2,1,0:T(1,128)}), f32[32,22,1,128]{3,2,1,0:T(1,128)S(1)}, u32[]{:S(2)}, u32[]{:S(2)}) async-start(f32[32,22,1,128]{3,2,1,0:T(1,128)} %get-tuple-element.49), calls=%async_computation.2 | async-start | bytes 720896 | tf_op jit(solution)/shard_map/all_to_all | solution.py:345
  48.9 17.7 %collective-permute-start.2 = (f32[1088,128]{1,0:T(8,128)S(1)}, f32[1088,128]{1,0:T(8,128)S(1)}, u32[]{:S(2)}, u32[]{:S(2)}) collective-permute-start(f32[1088,128]{1,0:T(8,128)S(1)} %select_maximum_fusion.refs_0_), channel_id=1, source_target_pairs={{0,2},{2,4},{4,6},{6,0},{1,3},{3,5},{5,7},{7,1},{8,10},{10,12},{12... | collective-permute-start | bytes 1671176 | tf_op jit(solution)/shard_map/ppermute | solution.py:329
  52.5 23.8 %collective-permute-start = (f32[1088,128]{1,0:T(8,128)S(1)}, f32[1088,128]{1,0:T(8,128)S(1)}, u32[]{:S(2)}, u32[]{:S(2)}) collective-permute-start(f32[1088,128]{1,0:T(8,128)S(1)} %select_maximum_fusion.refs_0_), channel_id=1, source_target_pairs={{0,6},{2,0},{4,2},{6,4},{1,7},{3,1},{5,3},{7,5},{8,14},{10,8},{12,... | collective-permute-start | bytes 1671176 | tf_op jit(solution)/shard_map/ppermute | solution.py:329
  56.0 18.2 %collective-permute-start.1 = (f32[488,128]{1,0:T(8,128)S(1)}, f32[488,128]{1,0:T(8,128)S(1)}, u32[]{:S(2)}, u32[]{:S(2)}) collective-permute-start(f32[488,128]{1,0:T(8,128)S(1)} %slice.13), channel_id=1, source_target_pairs={{0,4},{2,6},{4,0},{6,2},{1,5},{3,7},{5,1},{7,3},{8,12},{10,14},{12... | collective-permute-start | bytes 749576 | tf_op jit(solution)/shard_map/ppermute | solution.py:329
  66.6 12.9 %collective-permute-start.3 = (f32[600,128]{1,0:T(8,128)S(1)}, f32[600,128]{1,0:T(8,128)S(1)}, u32[]{:S(2)}, u32[]{:S(2)}) collective-permute-start(f32[600,128]{1,0:T(8,128)S(1)} %slice.14), channel_id=1, source_target_pairs={{0,2},{2,4},{4,6},{6,0},{1,3},{3,5},{5,7},{7,1},{8,10},{10,12},{12... | collective-permute-start | bytes 921608 | tf_op jit(solution)/shard_map/ppermute | solution.py:329
  69.9 11.6 %collective-permute-start.4 = (f32[1088,128]{1,0:T(8,128)S(1)}, f32[1088,128]{1,0:T(8,128)S(1)}, u32[]{:S(2)}, u32[]{:S(2)}) collective-permute-start(f32[1088,128]{1,0:T(8,128)S(1)} %select_maximum_fusion.refs_0_), channel_id=1, source_target_pairs={{0,1},{1,0},{2,3},{3,2},{4,5},{5,4},{6,7},{7,6},{8,9},{9,8},{10,11... | collective-permute-start | bytes 1671176 | tf_op jit(solution)/shard_map/ppermute | solution.py:332
  74.3 24.7 %copy-start.8 = (f32[8,8,128]{2,1,0:T(8,128)S(1)}, f32[8,8,128]{2,1,0:T(8,128)}, u32[]{:S(2)}) copy-start(f32[8,8,128]{2,1,0:T(8,128)} %constant.15.clone.const_ref) | copy-start | bytes 98308
  74.3 7.2 %collective-permute-start.7 = (f32[1088,128]{1,0:T(8,128)S(1)}, f32[1088,128]{1,0:T(8,128)S(1)}, u32[]{:S(2)}, u32[]{:S(2)}) collective-permute-start(f32[1088,128]{1,0:T(8,128)S(1)} %collective-permute-done.2.refs_3_), channel_id=1, source_target_pairs={{0,1},{1,0},{2,3},{3,2},{4,5},{5,4},{6,7},{7,6},{8,9},{9,8},{10,11... | collective-permute-start | bytes 1671176 | tf_op jit(solution)/shard_map/ppermute | solution.py:332
  76.3 5.2 %collective-permute-start.5 = (f32[1088,128]{1,0:T(8,128)S(1)}, f32[1088,128]{1,0:T(8,128)S(1)}, u32[]{:S(2)}, u32[]{:S(2)}) collective-permute-start(f32[1088,128]{1,0:T(8,128)S(1)} %collective-permute-done.refs_1_), channel_id=1, source_target_pairs={{0,1},{1,0},{2,3},{3,2},{4,5},{5,4},{6,7},{7,6},{8,9},{9,8},{10,11... | collective-permute-start | bytes 1671176 | tf_op jit(solution)/shard_map/ppermute | solution.py:332
  79.5 4.0 %collective-permute-start.6 = (f32[1088,128]{1,0:T(8,128)S(1)}, f32[1088,128]{1,0:T(8,128)}, u32[]{:S(2)}, u32[]{:S(2)}) collective-permute-start(f32[1088,128]{1,0:T(8,128)S(1)} %constant_dynamic-update-slice_fusion.refs_2_), channel_id=1, source_target_pairs={{0,1},{1,0},{2,3},{3,2},{4,5},{5,4},{6,7},{7,6},{8,9},{9,8},{10,11... | collective-permute-start | bytes 1671176 | tf_op jit(solution)/shard_map/ppermute | solution.py:332
  81.5 22.1 %copy-start.1 = (f32[1088,128]{1,0:T(8,128)}, f32[1088,128]{1,0:T(8,128)S(1)}, u32[]{:S(2)}) copy-start(f32[1088,128]{1,0:T(8,128)S(1)} %collective-permute-done.4.refs_4_) | copy-start | bytes 1671172
  81.5 0.9 copy-start.4
  82.4 0.8 copy-start.3
  103.6 65.8 %all-to-all-start.3 = ((f32[32,7,4,128]{3,2,1,0:T(4,128)}), f32[32,7,4,128]{3,2,1,0:T(4,128)S(1)}, u32[]{:S(2)}, u32[]{:S(2)}) async-start(f32[32,7,4,128]{3,2,1,0:T(4,128)} %bitcast.10), calls=%async_computation.3 | async-start | bytes 917504 | tf_op jit(solution)/shard_map/all_to_all | solution.py:345
  169.4 0.8 copy-start.7
  170.3 0.6 copy-start.6

commit v7 on v6

--- a/solution.py
+++ b/solution.py
@@ -203,7 +203,7 @@
         target = (shapes if of_coefs else fields).at[pl.ds(there, count)]
         source = pieces[index].at[pl.ds(row, count)]
         copies.append(pltpu.make_async_copy(source, target, sems.at[n + 1]))
-    for copy in copies:
+    for copy in reversed(copies):
         copy.start()
     ids.wait()
 
@@ -233,13 +233,13 @@
             for a in range(3):
                 points[a, pl.ds(u, 1), :] = recv_ref[s, k * 3 + a]
             coefs[pl.ds(u, 1), :] = shapes[pl.ds(code, 1), :]
-        return tuple(where) + (points[0], points[1], points[2], coefs[...])
+        all_coefs = coefs[...]
+        coef = [jnp.broadcast_to(all_coefs[:, m : m + 1], (8, LANES)) for m in range(24)]
+        return tuple(where) + tuple(newton(coef, [points[a] for a in range(3)]))
 
     def group(g, held):
-        where, target, all_coefs = held[:16], held[16:19], held[19]
+        where, pos = held[:16], held[16:]
         following = gather(g + 1)
-        coef = [jnp.broadcast_to(all_coefs[:, m : m + 1], (8, LANES)) for m in range(24)]
-        pos = newton(coef, target)
         for u in range(8):
             slot, start = where[2 * u : 2 * u + 2]
             along_x, along_y, along_z = [

time: 172 us -> 171 us (level)
  no operation moved by 1% of the time
where the time goes in v7:
time: 171 us; the launch traced here: 170 us
  waiting for transfers between devices  82.9 us (48%)
  starting transfers between devices  75.2 us (44%)
  Pallas kernels  6.67 us (4%)
  local copies, waits for them, and re-layouts  3.29 us (2%)
    all_to_all x2, waiting for transfers between devices, all_to_all(): lax.all_to_all(array, 'block', split_axis=0, concat_axis=0, tiled=True)  72.9 us
    all_to_all x2, starting transfers between devices, all_to_all(): lax.all_to_all(array, 'block', split_axis=0, concat_axis=0, tiled=True)  52.5 us
    ppermute x4, starting transfers between devices, along(): lax.ppermute(array, 'seg', [(i, (i + step) % segs) for i in range(segs)])  14.4 us
    ppermute x4, waiting for transfers between devices, along(): lax.ppermute(array, 'seg', [(i, (i + step) % segs) for i in range(segs)])  9.68 us
    ppermute x4, starting transfers between devices, swapped(): return lax.ppermute(array, 'sub', [(0, 1), (1, 0)])  8.29 us
    pallas_call x1, Pallas kernels, evaluate(): pl.pallas_call(functools.partial(evaluate_kernel, elems, slots, len(piece...  4.02 us
  transfers between devices with their start and end apart: 10, of which 6 were waited for; matrix products, arithmetic and copies ran while one was open for 1% of the time, Pallas kernels for 0%

profile of v7, /device:TPU:40, one launch (start us, length us, event | category | flops | bytes accessed | tf_op | source)
XLA Modules:
  0.0 170.0 jit_solution(12553069057675549204)
XLA Ops:
  0.0 0.0 copy-start
  0.0 0.0 copy-start.10
  0.0 0.0 copy-start.5
  0.0 0.7 copy-done.10
  0.7 2.1 %pack.3 = (f32[32,22,1,128]{3,2,1,0:T(1,128)}, s32[32]{0:T(128)S(1)}) custom-call(s32[32]{0:T(128)S(1)} %copy-done.10, f32[32,3,128]{2,1,0:T(4,128)} %bitcast.23), custom_call_target="tpu_custom_call" | custom-call | tf_op jit(solution)/shard_map/pack/pallas_call | solution.py:107
  2.7 0.0 copy-start.9
  2.8 0.0 copy-start.11
  2.8 45.8 %all-to-all-start.2 = ((f32[32,22,1,128]{3,2,1,0:T(1,128)}), f32[32,22,1,128]{3,2,1,0:T(1,128)S(1)}, u32[]{:S(2)}, u32[]{:S(2)}) async-start(f32[32,22,1,128]{3,2,1,0:T(1,128)} %get-tuple-element.49), calls=%async_computation.2 | async-start | bytes 720896 | tf_op jit(solution)/shard_map/all_to_all | solution.py:345
  48.6 0.0 copy-done
  48.6 0.0 copy-done.9
  48.6 0.0 copy-done.11
  48.6 0.2 fusion
  48.8 0.0 copy-done.5
  48.9 3.6 %collective-permute-start.2 = (f32[1088,128]{1,0:T(8,128)S(1)}, f32[1088,128]{1,0:T(8,128)S(1)}, u32[]{:S(2)}, u32[]{:S(2)}) collective-permute-start(f32[1088,128]{1,0:T(8,128)S(1)} %select_maximum_fusion.refs_0_), channel_id=1, source_target_pairs={{0,2},{2,4},{4,6},{6,0},{1,3},{3,5},{5,7},{7,1},{8,10},{10,12},{12... | collective-permute-start | bytes 1671176 | tf_op jit(solution)/shard_map/ppermute | solution.py:329
  52.5 3.5 %collective-permute-start = (f32[1088,128]{1,0:T(8,128)S(1)}, f32[1088,128]{1,0:T(8,128)S(1)}, u32[]{:S(2)}, u32[]{:S(2)}) collective-permute-start(f32[1088,128]{1,0:T(8,128)S(1)} %select_maximum_fusion.refs_0_), channel_id=1, source_target_pairs={{0,6},{2,0},{4,2},{6,4},{1,7},{3,1},{5,3},{7,5},{8,14},{10,8},{12,... | collective-permute-start | bytes 1671176 | tf_op jit(solution)/shard_map/ppermute | solution.py:329
  56.0 4.0 %collective-permute-start.1 = (f32[488,128]{1,0:T(8,128)S(1)}, f32[488,128]{1,0:T(8,128)S(1)}, u32[]{:S(2)}, u32[]{:S(2)}) collective-permute-start(f32[488,128]{1,0:T(8,128)S(1)} %slice.13), channel_id=1, source_target_pairs={{0,4},{2,6},{4,0},{6,2},{1,5},{3,7},{5,1},{7,3},{8,12},{10,14},{12... | collective-permute-start | bytes 749576 | tf_op jit(solution)/shard_map/ppermute | solution.py:329
  60.1 6.5 %collective-permute-done.2.refs_3_ = f32[1088,128]{1,0:T(8,128)S(1)} collective-permute-done((f32[1088,128]{1,0:T(8,128)S(1)}, f32[1088,128]{1,0:T(8,128)S(1)}, u32[]{:S(2)}, u32[]{:S(2)}) %collective-permute-start.2) | collective-permute-done | bytes 557088 | tf_op jit(solution)/shard_map/ppermute | solution.py:329
  66.6 3.3 %collective-permute-start.3 = (f32[600,128]{1,0:T(8,128)S(1)}, f32[600,128]{1,0:T(8,128)S(1)}, u32[]{:S(2)}, u32[]{:S(2)}) collective-permute-start(f32[600,128]{1,0:T(8,128)S(1)} %slice.14), channel_id=1, source_target_pairs={{0,2},{2,4},{4,6},{6,0},{1,3},{3,5},{5,7},{7,1},{8,10},{10,12},{12... | collective-permute-start | bytes 921608 | tf_op jit(solution)/shard_map/ppermute | solution.py:329
  69.9 2.0 %collective-permute-start.4 = (f32[1088,128]{1,0:T(8,128)S(1)}, f32[1088,128]{1,0:T(8,128)S(1)}, u32[]{:S(2)}, u32[]{:S(2)}) collective-permute-start(f32[1088,128]{1,0:T(8,128)S(1)} %select_maximum_fusion.refs_0_), channel_id=1, source_target_pairs={{0,1},{1,0},{2,3},{3,2},{4,5},{5,4},{6,7},{7,6},{8,9},{9,8},{10,11... | collective-permute-start | bytes 1671176 | tf_op jit(solution)/shard_map/ppermute | solution.py:332
  71.9 2.4 %collective-permute-done.1 = f32[488,128]{1,0:T(8,128)S(1)} collective-permute-done((f32[488,128]{1,0:T(8,128)S(1)}, f32[488,128]{1,0:T(8,128)S(1)}, u32[]{:S(2)}, u32[]{:S(2)}) %collective-permute-start.1) | collective-permute-done | bytes 249888 | tf_op jit(solution)/shard_map/ppermute | solution.py:329
  74.3 0.0 copy-start.8
  74.3 2.0 %collective-permute-start.7 = (f32[1088,128]{1,0:T(8,128)S(1)}, f32[1088,128]{1,0:T(8,128)S(1)}, u32[]{:S(2)}, u32[]{:S(2)}) collective-permute-start(f32[1088,128]{1,0:T(8,128)S(1)} %collective-permute-done.2.refs_3_), channel_id=1, source_target_pairs={{0,1},{1,0},{2,3},{3,2},{4,5},{5,4},{6,7},{7,6},{8,9},{9,8},{10,11... | collective-permute-start | bytes 1671176 | tf_op jit(solution)/shard_map/ppermute | solution.py:332
  76.3 0.0 collective-permute-done.refs_1_
  76.3 2.4 %collective-permute-start.5 = (f32[1088,128]{1,0:T(8,128)S(1)}, f32[1088,128]{1,0:T(8,128)S(1)}, u32[]{:S(2)}, u32[]{:S(2)}) collective-permute-start(f32[1088,128]{1,0:T(8,128)S(1)} %collective-permute-done.refs_1_), channel_id=1, source_target_pairs={{0,1},{1,0},{2,3},{3,2},{4,5},{5,4},{6,7},{7,6},{8,9},{9,8},{10,11... | collective-permute-start | bytes 1671176 | tf_op jit(solution)/shard_map/ppermute | solution.py:332
  78.7 0.8 collective-permute-done.3
  79.5 2.0 %collective-permute-start.6 = (f32[1088,128]{1,0:T(8,128)S(1)}, f32[1088,128]{1,0:T(8,128)}, u32[]{:S(2)}, u32[]{:S(2)}) collective-permute-start(f32[1088,128]{1,0:T(8,128)S(1)} %constant_dynamic-update-slice_fusion.refs_2_), channel_id=1, source_target_pairs={{0,1},{1,0},{2,3},{3,2},{4,5},{5,4},{6,7},{7,6},{8,9},{9,8},{10,11... | collective-permute-start | bytes 1671176 | tf_op jit(solution)/shard_map/ppermute | solution.py:332
  81.5 0.0 collective-permute-done.4.refs_4_
  81.5 0.0 copy-start.1
  81.5 0.0 collective-permute-done.5.refs_5_
  81.5 0.0 copy-start.4
  81.5 0.0 collective-permute-done.7.refs_7_
  81.5 0.8 copy-done.4
  82.4 0.0 copy-start.3
  82.4 0.8 copy-done.3
  83.2 0.4 collective-permute-done.6.refs_6_
  83.5 15.4 %all-to-all-done.2.recv_ref = f32[32,22,1,128]{3,2,1,0:T(1,128)S(1)} async-done(((f32[32,22,1,128]{3,2,1,0:T(1,128)}), f32[32,22,1,128]{3,2,1,0:T(1,128)S(1)}, u32[]{:S(2)}, u32[]{:S(2)}) %all-to-all-start.2) | async-done | bytes 360480 | tf_op jit(solution)/shard_map/all_to_all | solution.py:345
  99.0 0.0 copy-done.8
  99.0 4.0 %evaluate.3 = f32[224,4,128]{2,1,0:T(4,128)} custom-call(f32[32,22,1,128]{3,2,1,0:T(1,128)S(1)} %all-to-all-done.2.recv_ref, f32[8,8,128]{2,1,0:T(8,128)S(1)} %copy-done.8, f32[1088,128]{1,0:T(8,128)S(1)} %select_maximum_fusion.refs_0_, f32[1088,128]{1,0:T(8,128)S(1)} %collective-permute-done.refs_1_, ...), custom_call_target="tpu_custom_call" | custom-call | tf_op jit(solution)/shard_map/evaluate/pallas_call | solution.py:274
  103.0 0.0 copy-done.1
  103.0 6.7 %all-to-all-start.3 = ((f32[32,7,4,128]{3,2,1,0:T(4,128)}), f32[32,7,4,128]{3,2,1,0:T(4,128)S(1)}, u32[]{:S(2)}, u32[]{:S(2)}) async-start(f32[32,7,4,128]{3,2,1,0:T(4,128)} %bitcast.10), calls=%async_computation.3 | async-start | bytes 917504 | tf_op jit(solution)/shard_map/all_to_all | solution.py:345
  109.8 0.7 slice_reduce_fusion
  111.1 57.4 %all-to-all-done.3 = f32[32,7,4,128]{3,2,1,0:T(4,128)S(1)} async-done(((f32[32,7,4,128]{3,2,1,0:T(4,128)}), f32[32,7,4,128]{3,2,1,0:T(4,128)S(1)}, u32[]{:S(2)}, u32[]{:S(2)}) %all-to-all-start.3) | async-done | bytes 458784 | tf_op jit(solution)/shard_map/all_to_all | solution.py:345
  168.6 0.0 copy-start.7
  168.6 0.6 unpack.3
  169.2 0.2 copy-done.7
  169.4 0.0 copy-start.6
  169.4 0.6 copy-done.6
  (6 shorter events, 0.1 us)
Async XLA Ops:
  0.0 48.6 %copy-start = (f32[24,64]{1,0:T(8,128)S(1)}, f32[24,64]{1,0:T(8,128)}, u32[]{:S(2)}) copy-start(f32[24,64]{1,0:T(8,128)} %param.11) | copy-start | bytes 18436
  0.0 0.7 copy-start.10
  0.0 48.8 %copy-start.5 = (f32[64,4,512]{2,1,0:T(4,128)S(1)}, f32[64,4,512]{2,1,0:T(4,128)}, u32[]{:S(2)}) copy-start(f32[64,4,512]{2,1,0:T(4,128)} %param.10) | copy-start | bytes 1572868
  2.7 45.8 %copy-start.9 = (f32[24,24]{1,0:T(8,128)S(1)}, f32[24,24]{1,0:T(8,128)}, u32[]{:S(2)}) copy-start(f32[24,24]{1,0:T(8,128)} %constant.13.clone) | copy-start | bytes 6916
  2.8 45.8 %copy-start.11 = (f32[24]{0:T(128)S(1)}, f32[24]{0:T(128)}, u32[]{:S(2)}) copy-start(f32[24]{0:T(128)} %constant.21) | copy-start | bytes 292
  2.8 96.2 %all-to-all-start.2 = ((f32[32,22,1,128]{3,2,1,0:T(1,128)}), f32[32,22,1,128]{3,2,1,0:T(1,128)S(1)}, u32[]{:S(2)}, u32[]{:S(2)}) async-start(f32[32,22,1,128]{3,2,1,0:T(1,128)} %get-tuple-element.49), calls=%async_computation.2 | async-start | bytes 720896 | tf_op jit(solution)/shard_map/all_to_all | solution.py:345
  48.9 17.7 %collective-permute-start.2 = (f32[1088,128]{1,0:T(8,128)S(1)}, f32[1088,128]{1,0:T(8,128)S(1)}, u32[]{:S(2)}, u32[]{:S(2)}) collective-permute-start(f32[1088,128]{1,0:T(8,128)S(1)} %select_maximum_fusion.refs_0_), channel_id=1, source_target_pairs={{0,2},{2,4},{4,6},{6,0},{1,3},{3,5},{5,7},{7,1},{8,10},{10,12},{12... | collective-permute-start | bytes 1671176 | tf_op jit(solution)/shard_map/ppermute | solution.py:329
  52.5 23.8 %collective-permute-start = (f32[1088,128]{1,0:T(8,128)S(1)}, f32[1088,128]{1,0:T(8,128)S(1)}, u32[]{:S(2)}, u32[]{:S(2)}) collective-permute-start(f32[1088,128]{1,0:T(8,128)S(1)} %select_maximum_fusion.refs_0_), channel_id=1, source_target_pairs={{0,6},{2,0},{4,2},{6,4},{1,7},{3,1},{5,3},{7,5},{8,14},{10,8},{12,... | collective-permute-start | bytes 1671176 | tf_op jit(solution)/shard_map/ppermute | solution.py:329
  56.0 18.2 %collective-permute-start.1 = (f32[488,128]{1,0:T(8,128)S(1)}, f32[488,128]{1,0:T(8,128)S(1)}, u32[]{:S(2)}, u32[]{:S(2)}) collective-permute-start(f32[488,128]{1,0:T(8,128)S(1)} %slice.13), channel_id=1, source_target_pairs={{0,4},{2,6},{4,0},{6,2},{1,5},{3,7},{5,1},{7,3},{8,12},{10,14},{12... | collective-permute-start | bytes 749576 | tf_op jit(solution)/shard_map/ppermute | solution.py:329
  66.6 12.9 %collective-permute-start.3 = (f32[600,128]{1,0:T(8,128)S(1)}, f32[600,128]{1,0:T(8,128)S(1)}, u32[]{:S(2)}, u32[]{:S(2)}) collective-permute-start(f32[600,128]{1,0:T(8,128)S(1)} %slice.14), channel_id=1, source_target_pairs={{0,2},{2,4},{4,6},{6,0},{1,3},{3,5},{5,7},{7,1},{8,10},{10,12},{12... | collective-permute-start | bytes 921608 | tf_op jit(solution)/shard_map/ppermute | solution.py:329
  69.9 11.6 %collective-permute-start.4 = (f32[1088,128]{1,0:T(8,128)S(1)}, f32[1088,128]{1,0:T(8,128)S(1)}, u32[]{:S(2)}, u32[]{:S(2)}) collective-permute-start(f32[1088,128]{1,0:T(8,128)S(1)} %select_maximum_fusion.refs_0_), channel_id=1, source_target_pairs={{0,1},{1,0},{2,3},{3,2},{4,5},{5,4},{6,7},{7,6},{8,9},{9,8},{10,11... | collective-permute-start | bytes 1671176 | tf_op jit(solution)/shard_map/ppermute | solution.py:332
  74.3 24.7 %copy-start.8 = (f32[8,8,128]{2,1,0:T(8,128)S(1)}, f32[8,8,128]{2,1,0:T(8,128)}, u32[]{:S(2)}) copy-start(f32[8,8,128]{2,1,0:T(8,128)} %constant.15.clone.const_ref) | copy-start | bytes 98308
  74.3 7.2 %collective-permute-start.7 = (f32[1088,128]{1,0:T(8,128)S(1)}, f32[1088,128]{1,0:T(8,128)S(1)}, u32[]{:S(2)}, u32[]{:S(2)}) collective-permute-start(f32[1088,128]{1,0:T(8,128)S(1)} %collective-permute-done.2.refs_3_), channel_id=1, source_target_pairs={{0,1},{1,0},{2,3},{3,2},{4,5},{5,4},{6,7},{7,6},{8,9},{9,8},{10,11... | collective-permute-start | bytes 1671176 | tf_op jit(solution)/shard_map/ppermute | solution.py:332
  76.3 5.2 %collective-permute-start.5 = (f32[1088,128]{1,0:T(8,128)S(1)}, f32[1088,128]{1,0:T(8,128)S(1)}, u32[]{:S(2)}, u32[]{:S(2)}) collective-permute-start(f32[1088,128]{1,0:T(8,128)S(1)} %collective-permute-done.refs_1_), channel_id=1, source_target_pairs={{0,1},{1,0},{2,3},{3,2},{4,5},{5,4},{6,7},{7,6},{8,9},{9,8},{10,11... | collective-permute-start | bytes 1671176 | tf_op jit(solution)/shard_map/ppermute | solution.py:332
  79.5 4.0 %collective-permute-start.6 = (f32[1088,128]{1,0:T(8,128)S(1)}, f32[1088,128]{1,0:T(8,128)}, u32[]{:S(2)}, u32[]{:S(2)}) collective-permute-start(f32[1088,128]{1,0:T(8,128)S(1)} %constant_dynamic-update-slice_fusion.refs_2_), channel_id=1, source_target_pairs={{0,1},{1,0},{2,3},{3,2},{4,5},{5,4},{6,7},{7,6},{8,9},{9,8},{10,11... | collective-permute-start | bytes 1671176 | tf_op jit(solution)/shard_map/ppermute | solution.py:332
  81.5 21.5 %copy-start.1 = (f32[1088,128]{1,0:T(8,128)}, f32[1088,128]{1,0:T(8,128)S(1)}, u32[]{:S(2)}) copy-start(f32[1088,128]{1,0:T(8,128)S(1)} %collective-permute-done.4.refs_4_) | copy-start | bytes 1671172
  81.5 0.9 copy-start.4
  82.4 0.8 copy-start.3
  103.0 65.5 %all-to-all-start.3 = ((f32[32,7,4,128]{3,2,1,0:T(4,128)}), f32[32,7,4,128]{3,2,1,0:T(4,128)S(1)}, u32[]{:S(2)}, u32[]{:S(2)}) async-start(f32[32,7,4,128]{3,2,1,0:T(4,128)} %bitcast.10), calls=%async_computation.3 | async-start | bytes 917504 | tf_op jit(solution)/shard_map/all_to_all | solution.py:345
  168.6 0.8 copy-start.7
  169.4 0.6 copy-start.6
